TPU v7x, 32 devices: a whole 2x2x4 slice. The times are simulated.
32 devices in a mesh: seq: 8 (over z, x), tp: 4 (over y, core).
Axes of the slice: x: 2, y: 2, z: 4, core: 2. Of those that a mesh axis runs over, the one named last changes fastest.
Arguments:
- queries: bfloat16 [1536, 6144], P('seq', 'tp'), may hold values from -400 to 400
- key_vectors: bfloat16 [1536, 1024], P('seq', 'tp'), may hold values from -8 to 8
- value_vectors: bfloat16 [1536, 1024], P('seq', 'tp'), may hold values from -6 to 6
- positions: int32 [1536], P('seq'), may hold values from 0 to 1535, as said below
- residual: bfloat16 [1536, 6144], P('seq', 'tp'), may hold values from -200 to 200
- norm_gain: float32 [1, 6144], P(None, 'tp'), may hold values from 0.5 to 1.5
- out_weight: bfloat16 [6144, 6144], P('tp'), may hold values from -0.3125 to 0.3125
Outputs:
- quantized: bfloat16 [1536, 6144], P('seq')
- token_scale: float32 [1536], P('seq')
- new_residual: bfloat16 [1536, 6144], P('seq', 'tp')
Inputs may be any that keep to these rules, and one draw needn't show every extreme that they name: The positions are a permutation of 0 to 1535. Cut into 16 runs of 96 consecutive positions, the rows of one index of seq hold run r in their first 96 rows and run 2 * 8 - 1 - r in their last ones, both in increasing order, with r differing between the indices of seq.
All inputs are finite; a program needn't handle non-finite values. Where the computation divides by a largest or mean magnitude, that divisor is 1e-20 or more.
Results may differ from a plain program's by a relative error of at most 0.012.
Values may be sent and summed in bfloat16 or wider, within the bound.
No kernel may reach another device: no remote copies, remote signals or barrier semaphores. Data moves between devices by JAX's collectives and lax.ppermute only.
A program may use at most 64 MiB of HBM per device.

v0:
```python
import functools
import math

import jax
import jax.numpy as jnp
from jax import lax
from jax.experimental import pallas as pl
from jax.experimental.pallas import tpu as pltpu
from jax.sharding import PartitionSpec as P


HEAD = 128
TAG_ROWS = 8
HIDE = -1e30
VMEM = pltpu.VMEM
F32 = jnp.float32
BF16 = jnp.bfloat16


def in_vmem():
    return pl.BlockSpec(memory_space=VMEM)


def in_place():
    return pl.BlockSpec(memory_space=pl.ANY)


def near(array):
    return pltpu.with_memory_space_constraint(array, VMEM)


def far(array):
    return pltpu.with_memory_space_constraint(array, pltpu.HBM)


def after(array, *others):
    return lax.optimization_barrier((array, *others))[0]


def cost(flops, moved):
    return pl.CostEstimate(flops=int(flops), bytes_accessed=int(moved), transcendentals=0)


def grant(mib):
    return pltpu.CompilerParams(vmem_limit_bytes=mib << 20)


def run_copies(copies):
    for copy in copies:
        copy.start()
    for copy in copies:
        copy.wait()


def pack_body(run_rows, pos_ref, key_ref, value_ref, low_ref, high_ref, number_ref, sems):
    width = key_ref.shape[1]
    copies = [pltpu.make_async_copy(pos_ref, number_ref, sems.at[4])]
    for half, out in enumerate((low_ref, high_ref)):
        rows = pl.ds(half * run_rows, run_rows)
        for i, ref in enumerate((key_ref, value_ref)):
            target = out.at[pl.ds(0, run_rows), pl.ds(i * width, width)]
            copies.append(pltpu.make_async_copy(ref.at[rows, :], target, sems.at[2 * half + i]))
    for copy in copies:
        copy.start()
    copies[0].wait()
    run = (number_ref[0] // run_rows).astype(F32)
    for out in (low_ref, high_ref):
        out[run_rows:, :] = jnp.full((TAG_ROWS, 2 * width), run, F32).astype(BF16)
    for copy in copies[1:]:
        copy.wait()


def pack(positions, keys, values):
    run_rows = keys.shape[0] // 2
    shape = (run_rows + TAG_ROWS, 2 * keys.shape[1])
    return pl.pallas_call(
        functools.partial(pack_body, run_rows),
        out_shape=(VMEM(shape, BF16), VMEM(shape, BF16)),
        in_specs=[in_place()] * 3,
        out_specs=(in_vmem(), in_vmem()),
        scratch_shapes=[pltpu.SMEM(positions.shape, jnp.int32), pltpu.SemaphoreType.DMA((5,))],
        compiler_params=grant(4),
        cost_estimate=cost(2e8, 4 * keys.size * 2),
        name="pack",
    )(far(positions), far(keys), far(values))


def fetch_body(cores, blocks, width, weight_ref, *refs):
    extra = (len(refs) - 1 - len(blocks)) // 2
    outs, sems = refs[extra:-1], refs[-1]
    core = lax.axis_index("tp") % cores
    copies = []
    for i, (yb, k) in enumerate(blocks):
        start = pl.multiple_of((yb * cores + (core ^ k)) * width, HEAD)
        copies.append(pltpu.make_async_copy(weight_ref.at[:, pl.ds(start, width)], outs[i], sems.at[i]))
    for i in range(extra):
        at = len(blocks) + i
        copies.append(pltpu.make_async_copy(refs[i], outs[at], sems.at[at]))
    run_copies(copies)


def fetch(cores, blocks, width, weight, extra):
    shapes = [(weight.shape[0], width)] * len(blocks) + [array.shape for array in extra]
    return pl.pallas_call(
        functools.partial(fetch_body, cores, blocks, width),
        out_shape=tuple(VMEM(shape, BF16) for shape in shapes),
        in_specs=[in_place()] * (1 + len(extra)),
        out_specs=(in_vmem(),) * len(shapes),
        scratch_shapes=[pltpu.SemaphoreType.DMA((len(shapes),))],
        compiler_params=grant(4),
        cost_estimate=cost(2e9, 2 * weight.shape[0] * width * len(blocks)),
    )(far(weight), *[far(array) for array in extra])


def attend_body(run_rows, runs, query_half, key_halves, count, *refs):
    query_ref = refs[0]
    pieces = refs[1 : 1 + len(key_halves) * count]
    out_ref, kv_ref, hide_ref = refs[1 + len(key_halves) * count :]
    total = len(pieces) * run_rows
    kv_width = pieces[0].shape[1] // 2
    query_width = query_ref.shape[1]
    kv_heads = kv_width // HEAD
    group = query_width // kv_width
    step = (1.0 / math.sqrt(HEAD)) * math.log2(math.e)
    query_rows = pl.ds(query_half * run_rows, run_rows)

    lane = lax.broadcasted_iota(jnp.int32, (1, total), 1)
    base = jnp.zeros((1, total), F32)
    first = jnp.zeros((1, total), jnp.int32)
    own = None
    for number, piece in enumerate(pieces):
        kv_ref[pl.ds(number * run_rows, run_rows), :] = piece[:run_rows, :]
        tag = piece[run_rows : run_rows + TAG_ROWS, :HEAD].astype(F32)[:1, :]
        if number == 0:
            own = tag[:, :1]
        tag = jnp.concatenate([tag] * (total // HEAD), axis=1)
        if key_halves[number // count] == 1:
            tag = (runs - 1) - tag
        inside = lane >= number * run_rows
        base = jnp.where(inside, tag, base)
        first = jnp.where(inside, number * run_rows, first)
    key_pos = base * run_rows + (lane - first).astype(F32)
    own = own if query_half == 0 else runs - 1 - own
    query_pos = own * run_rows + lax.broadcasted_iota(jnp.int32, (run_rows, 1), 0).astype(F32)
    hide_ref[...] = jnp.where(key_pos <= query_pos, 0.0, HIDE)

    pair = 2 if group % 2 == 0 else 1
    for kv_head in range(kv_heads):
        keys = kv_ref[:, kv_head * HEAD : (kv_head + 1) * HEAD]
        values = kv_ref[:, kv_width + kv_head * HEAD : kv_width + (kv_head + 1) * HEAD]
        for member in range(0, group, pair):
            heads = [kv_head * group + member + i for i in range(pair)]
            query = jnp.concatenate([query_ref[query_rows, h * HEAD : (h + 1) * HEAD] for h in heads], axis=0)
            scores = lax.dot_general(query, keys, (((1,), (1,)), ((), ())), preferred_element_type=F32)
            weights, sums = [], []
            for i in range(pair):
                part = scores[i * run_rows : (i + 1) * run_rows] * step + hide_ref[...]
                part = jnp.exp2(part - jnp.max(part, axis=1, keepdims=True))
                sums.append(jnp.sum(part, axis=1, keepdims=True))
                weights.append(part.astype(BF16))
            mixed = jnp.dot(jnp.concatenate(weights, axis=0), values, preferred_element_type=F32)
            for i, h in enumerate(heads):
                mean = mixed[i * run_rows : (i + 1) * run_rows] / sums[i]
                out_ref[:, h * HEAD : (h + 1) * HEAD] = mean.astype(BF16)


def attend(queries, query_half, piece_sets, key_halves, runs):
    run_rows = queries.shape[0] // 2
    count = len(piece_sets[0])
    pieces = [near(piece) for pieces in piece_sets for piece in pieces]
    total = len(pieces) * run_rows
    width = queries.shape[1]
    return pl.pallas_call(
        functools.partial(attend_body, run_rows, runs, query_half, key_halves, count),
        out_shape=VMEM((run_rows, width), BF16),
        in_specs=[in_vmem()] * (1 + len(pieces)),
        out_specs=in_vmem(),
        scratch_shapes=[
            VMEM((total, pieces[0].shape[1]), BF16),
            VMEM((run_rows, total), F32),
        ],
        compiler_params=grant(12),
        cost_estimate=cost(4 * run_rows * total * width, total * pieces[0].shape[1] * 2),
    )(near(queries), *pieces)


def project_body(cores, blocks, half, own, att_ref, *rest):
    weights, rest = rest[: len(blocks)], rest[len(blocks) :]
    outs = rest[2:] if own else rest
    width = weights[0].shape[1]
    tp = lax.axis_index("tp")
    for i, yb in enumerate(blocks):
        total = jnp.dot(att_ref[...], weights[i][...], preferred_element_type=F32)
        columns = slice(i * width, (i + 1) * width)
        if own:
            arrived, residual = rest[0], rest[1]
            mine = jnp.where(tp // cores == yb, 1.0, 0.0).astype(F32)
            total = total.astype(BF16).astype(F32) + arrived[:, columns].astype(F32)
            rows = pl.ds(half * arrived.shape[0], arrived.shape[0])
            total = total + mine * residual[rows, :].astype(F32)
        total = total.astype(BF16)
        rows = outs[0].shape[0]
        for j, out in enumerate(outs):
            out[:, columns] = total[j * rows : (j + 1) * rows]


def project(cores, blocks, half, attended, weights, cuts=1, arrived=None, residual=None):
    rows, depth = attended.shape
    width = weights[0].shape[1] * len(blocks)
    own = arrived is not None
    operands = [attended, *weights] + ([arrived, residual] if own else [])
    result = pl.pallas_call(
        functools.partial(project_body, cores, blocks, half, own),
        out_shape=(VMEM((rows // cuts, width), BF16),) * cuts,
        in_specs=[in_vmem()] * len(operands),
        out_specs=(in_vmem(),) * cuts,
        compiler_params=grant(8),
        cost_estimate=cost(2 * rows * depth * width, depth * width * 2),
        name="project_own" if own else "project_other",
    )(*[near(operand) for operand in operands])
    return result if cuts > 1 else result[0]


def finish_body(ny, cores, row, places, count, gain_ref, *refs):
    parts = refs[:count]
    line_ref = refs[count]
    quant_ref, line_out, stream_ref, quant_vmem, stream_vmem, sems = refs[-6:]
    rows = parts[0].shape[0]
    blocks = ny * cores
    width = gain_ref.shape[2]
    tp = lax.axis_index("tp")
    y, core = tp // cores, tp % cores

    def part(yb, k):
        number, column = places[yb, k]
        return parts[number][:, column * width : (column + 1) * width].astype(F32)

    stream = part(0, 0)
    for yb in range(1, ny):
        stream = jnp.where(y == yb, part(yb, 0), stream)
    stream_vmem[...] = stream.astype(BF16)
    copies = [pltpu.make_async_copy(stream_vmem, stream_ref.at[pl.ds(row, rows), :], sems.at[blocks])]
    copies[0].start()
    totals = {}
    for yb in range(ny):
        for k in range(cores):
            value = part(yb, k)
            totals[yb, k] = jnp.sum(value * value, axis=1, keepdims=True)
    square = jnp.zeros((rows, 1), F32)
    for yb in range(ny):
        for cb in range(cores):
            chosen = totals[yb, 0]
            for k in range(1, cores):
                chosen = jnp.where((core ^ k) == cb, totals[yb, k], chosen)
            square = square + chosen
    root = lax.rsqrt(square / (blocks * width) + 1e-05)
    peak = jnp.zeros((rows, 1), F32)
    for yb in range(ny):
        for k in range(cores):
            value = part(yb, k) * gain_ref[(y ^ yb) * cores + k]
            peak = jnp.maximum(peak, jnp.max(jnp.abs(value), axis=1, keepdims=True))
    peak = peak * root + 1e-06
    factor = root / peak
    for yb in range(ny):
        for k in range(cores):
            value = part(yb, k) * gain_ref[(y ^ yb) * cores + k] * factor
            slot = yb * cores + k
            start = pl.multiple_of((yb * cores + (core ^ k)) * width, HEAD)
            quant_vmem[slot] = value.astype(BF16)
            target = quant_ref.at[pl.ds(row, rows), pl.ds(start, width)]
            copies.append(pltpu.make_async_copy(quant_vmem.at[slot], target, sems.at[slot]))
            copies[-1].start()
    lanes = line_out.shape[-1]
    lane = lax.broadcasted_iota(jnp.int32, (rows, lanes), 1)
    here = lax.broadcasted_iota(jnp.int32, (rows, lanes), 0) + row == lane
    line = jnp.sum(jnp.where(here, peak, 0.0), axis=0, keepdims=True)
    if row:
        line = line + line_ref[...]
    line_out[...] = line.reshape(line_out.shape)
    for copy in copies:
        copy.wait()


def finish(ny, cores, row, all_rows, gains, parts, places, earlier, last):
    rows = parts[0].shape[0]
    width = gains.shape[2]
    blocks = ny * cores
    operands = [near(gains), *[near(part) for part in parts]]
    line = (all_rows,) if last else (1, all_rows)
    out_shape = (
        jax.ShapeDtypeStruct((all_rows, blocks * width), BF16),
        jax.ShapeDtypeStruct(line, F32) if last else VMEM(line, F32),
        jax.ShapeDtypeStruct((all_rows, width), BF16),
    )
    aliases = {}
    if earlier is not None:
        aliases = {len(operands) + 1: 0, len(operands) + 2: 2}
        operands += [near(earlier[1]), earlier[0], earlier[2]]
    else:
        operands += [near(jnp.zeros((1, all_rows), F32))]
    n = 2 + len(parts)
    return pl.pallas_call(
        functools.partial(finish_body, ny, cores, row, places, len(parts)),
        out_shape=out_shape,
        in_specs=[in_vmem()] * n + [in_place()] * (len(operands) - n),
        out_specs=(in_place(), in_vmem(), in_place()),
        scratch_shapes=[
            VMEM((blocks, rows, width), BF16),
            VMEM((rows, width), BF16),
            pltpu.SemaphoreType.DMA((blocks + 1,)),
        ],
        input_output_aliases=aliases,
        compiler_params=grant(8),
        cost_estimate=cost(2e9, 4 * rows * blocks * width),
    )(*operands)


def swap(size, count, stride, distance):
    def partner(index):
        digit = (index // stride) % size
        return index + ((digit ^ distance) - digit) * stride

    return [(index, partner(index)) for index in range(count)]


def tree_sum(terms):
    terms = [term.astype(F32) for term in terms]
    while len(terms) > 1:
        terms = [terms[i] + terms[i + 1] for i in range(0, len(terms), 2)]
    return terms[0].astype(BF16)


def on_device(sizes, queries, keys, values, positions, residual, norm_gain, out_weight):
    nz, nx, ny, cores = sizes
    n_seq, n_tp = nz * nx, ny * cores
    runs = 2 * n_seq
    all_rows, block_width = residual.shape
    run_rows = all_rows // 2

    def move_z(array, k):
        return lax.ppermute(array, "seq", swap(nz, n_seq, nx, k))

    def move_x(array, k):
        return lax.ppermute(array, "seq", swap(nx, n_seq, 1, k))

    def move_y(array, k):
        return lax.ppermute(array, "tp", swap(ny, n_tp, cores, k))

    def move_core(array, k):
        return lax.ppermute(array, "tp", swap(cores, n_tp, 1, k))

    low, high = pack(positions, keys, values)
    low_pieces = [low] + [move_x(low, j) for j in range(1, nx)]
    weights = {}

    def held_until_a(piece):
        if "a" not in state:
            source = after(out_weight, near_block)
            *blocks, state["query"] = fetch(cores, [(0, 1)], block_width, source, [queries])
            weights[0, 1] = blocks[0]
            state["a"] = blocks[0]
        return after(piece, state["a"])

    state = {}
    near_block = None
    step, column = nz // 2, [low]
    firsts = {k: move_z(low, k) for k in dict.fromkeys((step, 1)) if k}
    near_block = firsts[1]
    while step:
        for held in list(column):
            if held is low and step in firsts:
                column.append(firsts[step])
            else:
                column.append(move_z(held_until_a(held), step))
        step //= 2
    for piece in column[1:]:
        gate = piece if piece is near_block else after(piece, state.get("a", near_block))
        low_pieces += [piece] + [move_x(gate, j) for j in range(1, nx)]
    if "query" not in state:
        held_until_a(low)
    query_near = state["query"]

    source = after(out_weight, state["a"])
    rest = [(yb, 1) for yb in range(1, ny)]
    *blocks, residual_near = fetch(cores, rest, block_width, source, [residual])
    weights.update(zip(rest, blocks))
    source = after(out_weight, residual_near, column[-1])
    rest = [(yb, 0) for yb in range(ny)]
    weights.update(zip(rest, fetch(cores, rest, block_width, source, [])))

    early = attend(query_near, 0, [low_pieces], (0,), runs)
    sent, parts, marks = [], [], []
    for yb in range(ny):
        other = project(cores, [yb], 0, early, [weights[yb, 1]])
        sent.append(move_core(other, 1))
    for yb in range(ny):
        own = project(cores, [yb], 0, early, [weights[yb, 0]], 1, sent[yb], residual_near)
        marks.append(own)
        total = tree_sum([own] + [move_y(own, k) for k in range(1, ny)])
        parts += [total, move_core(total, 1)]
    places = {(yb, k): (yb * cores + k, 0) for yb in range(ny) for k in range(cores)}
    pair = [norm_gain] + [move_core(after(norm_gain, marks[0]), k) for k in range(1, cores)]
    pair = jnp.stack(pair)
    gains = jnp.concatenate([pair] + [move_y(pair, k) for k in range(1, ny)])
    result = finish(ny, cores, 0, all_rows, gains, parts, places, None, False)

    step, column = nz // 2, [high]
    ready = after(high, state["a"])
    firsts = {k: move_z(ready, k) for k in dict.fromkeys((step, 1)) if k}
    while step:
        for held in list(column):
            if held is high and step in firsts:
                column.append(firsts[step])
            else:
                column.append(move_z(after(held, marks[0]), step))
        step //= 2
    high_pieces = []
    for piece in column:
        high_pieces += [piece] + [move_x(after(piece, marks[0]), j) for j in range(1, nx)]

    late = attend(query_near, 1, [low_pieces, high_pieces], (0, 1), runs)
    every = list(range(ny))
    other = project(cores, every, 1, late, [weights[yb, 1] for yb in every])
    arrived = move_core(other, 1)
    cuts = project(cores, every, 1, late, [weights[yb, 0] for yb in every], 2, arrived, residual_near)
    places = {(yb, k): (k, yb) for yb in range(ny) for k in range(cores)}
    for i, own in enumerate(cuts):
        total = tree_sum([own] + [move_y(own, k) for k in range(1, ny)])
        parts = [total, move_core(total, 1)]
        row = run_rows + i * own.shape[0]
        result = finish(ny, cores, row, all_rows, gains, parts, places, result, i == 1)
    quantized, scale, stream = result
    return (quantized, scale, stream)


def sizes_of(mesh):
    along_seq, along_tp = list(mesh.devices[:, 0]), list(mesh.devices[0, :])
    nx = len({device.coords[0] for device in along_seq})
    ny = len({device.coords[1] for device in along_tp})
    return (len(along_seq) // nx, nx, ny, len(along_tp) // ny)


def solution(mesh):
    return jax.shard_map(
        functools.partial(on_device, sizes_of(mesh)),
        mesh=mesh,
        in_specs=(
            P("seq", "tp"),
            P("seq", "tp"),
            P("seq", "tp"),
            P("seq"),
            P("seq", "tp"),
            P(None, "tp"),
            P("tp", None),
        ),
        out_specs=(P("seq", None), P("seq"), P("seq", "tp")),
        check_vma=False,
    )
```

profile of v0, /device:TPU:0, one launch (start us, length us, event | category | flops | bytes accessed | tf_op | source)
XLA Modules:
  0.0 82.7 jit_solution(6000507365326691734)
XLA Ops:
  0.6 0.9 %pack.1 = (bf16[104,512]{1,0:T(8,128)(2,1)S(1)}, bf16[104,512]{1,0:T(8,128)(2,1)S(1)}) custom-call(s32[192]{0:T(256)} %pos_ref.1, bf16[192,256]{1,0:T(8,128)(2,1)} %key_ref.1, bf16[192,256]{1,0:T(8,128)(2,1)} %value_ref.1), custom_call_target="tpu_custom_call" | custom-call | flops 200000000 | bytes 393216 | tf_op jit(solution)/shard_map/pack/pallas_call | solution.py:76
  1.6 3.1 %collective-permute-start = (bf16[104,512]{1,0:T(8,128)(2,1)S(1)}, bf16[104,512]{1,0:T(8,128)(2,1)S(1)}, u32[]{:S(2)}, u32[]{:S(2)}) collective-permute-start(bf16[104,512]{1,0:T(8,128)(2,1)S(1)} %get-tuple-element.30.refs_1_), channel_id=1, source_target_pairs={{0,8},{4,12},{8,0},{12,4},{16,24},{20,28},{24,16},{28,20},{1,9},{5... | collective-permute-start | bytes 319496 | tf_op jit(solution)/shard_map/ppermute | solution.py:341
  4.7 2.6 %collective-permute-start.2 = (bf16[104,512]{1,0:T(8,128)(2,1)S(1)}, bf16[104,512]{1,0:T(8,128)(2,1)S(1)}, u32[]{:S(2)}, u32[]{:S(2)}) collective-permute-start(bf16[104,512]{1,0:T(8,128)(2,1)S(1)} %get-tuple-element.30.refs_1_), channel_id=1, source_target_pairs={{0,16},{4,20},{8,24},{12,28},{16,0},{20,4},{24,8},{28,12},{1,17},{... | collective-permute-start | bytes 319496 | tf_op jit(solution)/shard_map/ppermute | solution.py:341
  7.3 0.4 collective-permute-done.refs_5_
  7.6 2.5 %shard_map.94 = (bf16[1536,1536]{1,0:T(8,128)(2,1)S(1)}, bf16[192,1536]{1,0:T(8,128)(2,1)S(1)}) custom-call(bf16[1536,6144]{1,0:T(8,128)(2,1)} %weight_ref.2, bf16[192,1536]{1,0:T(8,128)(2,1)} %refs_0_.2), custom_call_target="tpu_custom_call" | custom-call | flops 2000000000 | bytes 4718592 | tf_op jit(solution)/shard_map/pallas_call | solution.py:104
  10.2 2.2 %collective-permute-done.2.refs_3_ = bf16[104,512]{1,0:T(8,128)(2,1)S(1)} collective-permute-done((bf16[104,512]{1,0:T(8,128)(2,1)S(1)}, bf16[104,512]{1,0:T(8,128)(2,1)S(1)}, u32[]{:S(2)}, u32[]{:S(2)}) %collective-permute-start.2) | collective-permute-done | bytes 106528 | tf_op jit(solution)/shard_map/ppermute | solution.py:341
  12.3 0.4 collective-permute-start.5
  12.8 1.4 %collective-permute-start.1 = (bf16[104,512]{1,0:T(8,128)(2,1)S(1)}, bf16[104,512]{1,0:T(8,128)(2,1)S(1)}, u32[]{:S(2)}, u32[]{:S(2)}) collective-permute-start(bf16[104,512]{1,0:T(8,128)(2,1)S(1)} %get-tuple-element.30.refs_1_), channel_id=1, source_target_pairs={{0,4},{4,0},{8,12},{12,8},{16,20},{20,16},{24,28},{28,24},{1,5},{5... | collective-permute-start | bytes 319496 | tf_op jit(solution)/shard_map/ppermute | solution.py:344
  14.2 0.6 collective-permute-start.3
  14.8 1.4 %collective-permute-start.4 = (bf16[104,512]{1,0:T(8,128)(2,1)S(1)}, bf16[104,512]{1,0:T(8,128)(2,1)S(1)}, u32[]{:S(2)}, u32[]{:S(2)}) collective-permute-start(bf16[104,512]{1,0:T(8,128)(2,1)S(1)} %collective-permute-done.refs_5_), channel_id=1, source_target_pairs={{0,4},{4,0},{8,12},{12,8},{16,20},{20,16},{24,28},{28,24},{1,5},{5... | collective-permute-start | bytes 319496 | tf_op jit(solution)/shard_map/ppermute | solution.py:344
  16.2 0.8 %collective-permute-done.5.refs_7_ = bf16[104,512]{1,0:T(8,128)(2,1)S(1)} collective-permute-done((bf16[104,512]{1,0:T(8,128)(2,1)S(1)}, bf16[104,512]{1,0:T(8,128)(2,1)S(1)}, u32[]{:S(2)}, u32[]{:S(2)}) %collective-permute-start.5) | collective-permute-done | bytes 106528 | tf_op jit(solution)/shard_map/ppermute | solution.py:341
  17.0 1.5 %collective-permute-start.6 = (bf16[104,512]{1,0:T(8,128)(2,1)S(1)}, bf16[104,512]{1,0:T(8,128)(2,1)S(1)}, u32[]{:S(2)}, u32[]{:S(2)}) collective-permute-start(bf16[104,512]{1,0:T(8,128)(2,1)S(1)} %collective-permute-done.5.refs_7_), channel_id=1, source_target_pairs={{0,4},{4,0},{8,12},{12,8},{16,20},{20,16},{24,28},{28,24},{1,5},{5... | collective-permute-start | bytes 319496 | tf_op jit(solution)/shard_map/ppermute | solution.py:344
  18.6 2.3 %collective-permute-done.3.refs_4_ = bf16[104,512]{1,0:T(8,128)(2,1)S(1)} collective-permute-done((bf16[104,512]{1,0:T(8,128)(2,1)S(1)}, bf16[104,512]{1,0:T(8,128)(2,1)S(1)}, u32[]{:S(2)}, u32[]{:S(2)}) %collective-permute-start.3) | collective-permute-done | bytes 106528 | tf_op jit(solution)/shard_map/ppermute | solution.py:344
  20.9 1.1 %collective-permute-done.4.refs_6_ = bf16[104,512]{1,0:T(8,128)(2,1)S(1)} collective-permute-done((bf16[104,512]{1,0:T(8,128)(2,1)S(1)}, bf16[104,512]{1,0:T(8,128)(2,1)S(1)}, u32[]{:S(2)}, u32[]{:S(2)}) %collective-permute-start.4) | collective-permute-done | bytes 106528 | tf_op jit(solution)/shard_map/ppermute | solution.py:344
  22.0 1.1 %collective-permute-done.6.refs_8_ = bf16[104,512]{1,0:T(8,128)(2,1)S(1)} collective-permute-done((bf16[104,512]{1,0:T(8,128)(2,1)S(1)}, bf16[104,512]{1,0:T(8,128)(2,1)S(1)}, u32[]{:S(2)}, u32[]{:S(2)}) %collective-permute-start.6) | collective-permute-done | bytes 106528 | tf_op jit(solution)/shard_map/ppermute | solution.py:344
  23.2 2.3 %shard_map.95.att_ref = bf16[96,1536]{1,0:T(8,128)(2,1)S(1)} custom-call(bf16[192,1536]{1,0:T(8,128)(2,1)S(1)} %get-tuple-element.32.refs_0_, bf16[104,512]{1,0:T(8,128)(2,1)S(1)} %get-tuple-element.30.refs_1_, bf16[104,512]{1,0:T(8,128)(2,1)S(1)} %collective-permute-done.1.refs_2_, bf16[104,512]{1,0:T(8,128)(2,1)S(1)} %collective-permute-done.2.refs_3_, ...), custom_call_target="tpu_custom_call" | custom-call | flops 452984832 | bytes 786432 | tf_op jit(solution)/shard_map/pallas_call | solution.py:173
  25.5 0.9 %project_other.3 = bf16[96,1536]{1,0:T(8,128)(2,1)S(1)} custom-call(bf16[96,1536]{1,0:T(8,128)(2,1)S(1)} %shard_map.95.att_ref, bf16[1536,1536]{1,0:T(8,128)(2,1)S(1)} %get-tuple-element.33.rest_0_), custom_call_target="tpu_custom_call" | custom-call | flops 452984832 | bytes 4718592 | tf_op jit(solution)/shard_map/project_other/pallas_call | solution.py:212
  26.4 2.5 %shard_map.96 = (bf16[1536,1536]{1,0:T(8,128)(2,1)S(1)}, bf16[192,1536]{1,0:T(8,128)(2,1)S(1)}) custom-call(bf16[1536,6144]{1,0:T(8,128)(2,1)} %weight_ref.2, bf16[192,1536]{1,0:T(8,128)(2,1)} %refs_0_.3), custom_call_target="tpu_custom_call" | custom-call | flops 2000000000 | bytes 4718592 | tf_op jit(solution)/shard_map/pallas_call | solution.py:104
  29.0 0.9 %project_other.5 = bf16[96,1536]{1,0:T(8,128)(2,1)S(1)} custom-call(bf16[96,1536]{1,0:T(8,128)(2,1)S(1)} %shard_map.95.att_ref, bf16[1536,1536]{1,0:T(8,128)(2,1)S(1)} %get-tuple-element.48.rest_1_.rest_0_), custom_call_target="tpu_custom_call" | custom-call | flops 452984832 | bytes 4718592 | tf_op jit(solution)/shard_map/project_other/pallas_call | solution.py:212
  29.8 0.5 collective-permute-start.24
  30.4 1.9 %collective-permute-start.11 = (bf16[104,512]{1,0:T(8,128)(2,1)S(1)}, bf16[104,512]{1,0:T(8,128)(2,1)S(1)}, u32[]{:S(2)}, u32[]{:S(2)}) collective-permute-start(bf16[104,512]{1,0:T(8,128)(2,1)S(1)} %get-tuple-element.43.refs_9_), channel_id=1, source_target_pairs={{0,16},{4,20},{8,24},{12,28},{16,0},{20,4},{24,8},{28,12},{1,17},{... | collective-permute-start | bytes 319496 | tf_op jit(solution)/shard_map/ppermute | solution.py:341
  32.3 0.4 collective-permute-start.13
  32.7 3.8 %shard_map.97 = (bf16[1536,1536]{1,0:T(8,128)(2,1)S(1)}, bf16[1536,1536]{1,0:T(8,128)(2,1)S(1)}) custom-call(bf16[1536,6144]{1,0:T(8,128)(2,1)} %weight_ref.2), custom_call_target="tpu_custom_call" | custom-call | flops 2000000000 | bytes 9437184 | tf_op jit(solution)/shard_map/pallas_call | solution.py:104
  36.6 0.9 %project_own.3 = bf16[96,1536]{1,0:T(8,128)(2,1)S(1)} custom-call(bf16[96,1536]{1,0:T(8,128)(2,1)S(1)} %shard_map.95.att_ref, bf16[1536,1536]{1,0:T(8,128)(2,1)S(1)} %get-tuple-element.39.rest_0_, bf16[96,1536]{1,0:T(8,128)(2,1)S(1)} %collective-permute-done.7.rest_1_, bf16[192,1536]{1,0:T(8,128)(2,1)S(1)} %get-tuple-element.37.rest_2_.rest_3_), custom_call_target="tpu_custom_call" | custom-call | flops 452984832 | bytes 4718592 | tf_op jit(solution)/shard_map/project_own/pallas_call | solution.py:212
  37.5 0.9 %collective-permute-done.11.refs_11_ = bf16[104,512]{1,0:T(8,128)(2,1)S(1)} collective-permute-done((bf16[104,512]{1,0:T(8,128)(2,1)S(1)}, bf16[104,512]{1,0:T(8,128)(2,1)S(1)}, u32[]{:S(2)}, u32[]{:S(2)}) %collective-permute-start.11) | collective-permute-done | bytes 106528 | tf_op jit(solution)/shard_map/ppermute | solution.py:341
  38.4 0.7 collective-permute-start.15
  39.1 1.4 %collective-permute-start.12 = (bf16[104,512]{1,0:T(8,128)(2,1)S(1)}, bf16[104,512]{1,0:T(8,128)(2,1)S(1)}, u32[]{:S(2)}, u32[]{:S(2)}) collective-permute-start(bf16[104,512]{1,0:T(8,128)(2,1)S(1)} %collective-permute-done.11.refs_11_), channel_id=1, source_target_pairs={{0,4},{4,0},{8,12},{12,8},{16,20},{20,16},{24,28},{28,24},{1,5},{5... | collective-permute-start | bytes 319496 | tf_op jit(solution)/shard_map/ppermute | solution.py:344
  40.6 1.5 %collective-permute-start.22 = (bf16[96,1536]{1,0:T(8,128)(2,1)S(1)}, bf16[96,1536]{1,0:T(8,128)(2,1)S(1)}, u32[]{:S(2)}, u32[]{:S(2)}) collective-permute-start(bf16[96,1536]{1,0:T(8,128)(2,1)S(1)} %project_own.3), channel_id=1, source_target_pairs={{0,2},{1,3},{2,0},{3,1},{4,6},{5,7},{6,4},{7,5},{8,10},{9,11},{10,... | collective-permute-start | bytes 884744 | tf_op jit(solution)/shard_map/ppermute | solution.py:347
  42.1 0.9 %project_own.5 = bf16[96,1536]{1,0:T(8,128)(2,1)S(1)} custom-call(bf16[96,1536]{1,0:T(8,128)(2,1)S(1)} %shard_map.95.att_ref, bf16[1536,1536]{1,0:T(8,128)(2,1)S(1)} %get-tuple-element.47.rest_1_.rest_0_, bf16[96,1536]{1,0:T(8,128)(2,1)S(1)} %collective-permute-done.24.rest_1_, bf16[192,1536]{1,0:T(8,128)(2,1)S(1)} %get-tuple-element.37.rest_2_.rest_3_), custom_call_target="tpu_custom_call" | custom-call | flops 452984832 | bytes 4718592 | tf_op jit(solution)/shard_map/project_own/pallas_call | solution.py:212
  43.0 0.7 collective-permute-start.10
  43.7 1.4 %collective-permute-start.14 = (bf16[104,512]{1,0:T(8,128)(2,1)S(1)}, bf16[104,512]{1,0:T(8,128)(2,1)S(1)}, u32[]{:S(2)}, u32[]{:S(2)}) collective-permute-start(bf16[104,512]{1,0:T(8,128)(2,1)S(1)} %collective-permute-done.13.refs_13_), channel_id=1, source_target_pairs={{0,4},{4,0},{8,12},{12,8},{16,20},{20,16},{24,28},{28,24},{1,5},{5... | collective-permute-start | bytes 319496 | tf_op jit(solution)/shard_map/ppermute | solution.py:344
  45.1 0.6 collective-permute-start.16
  45.7 3.2 %collective-permute-done.10.refs_10_ = bf16[104,512]{1,0:T(8,128)(2,1)S(1)} collective-permute-done((bf16[104,512]{1,0:T(8,128)(2,1)S(1)}, bf16[104,512]{1,0:T(8,128)(2,1)S(1)}, u32[]{:S(2)}, u32[]{:S(2)}) %collective-permute-start.10) | collective-permute-done | bytes 106528 | tf_op jit(solution)/shard_map/ppermute | solution.py:344
  48.9 0.5 collective-permute-start.25
  49.5 1.5 %collective-permute-start.9 = (f32[2,1,1536]{2,1,0:T(1,128)S(1)}, f32[2,1,1536]{2,1,0:T(1,128)S(1)}, u32[]{:S(2)}, u32[]{:S(2)}) collective-permute-start(f32[2,1,1536]{2,1,0:T(1,128)S(1)} %pad_maximum_fusion.1), channel_id=1, source_target_pairs={{0,2},{1,3},{2,0},{3,1},{4,6},{5,7},{6,4},{7,5},{8,10},{9,11},{10,... | collective-permute-start | bytes 36872 | tf_op jit(solution)/shard_map/ppermute | solution.py:347
  51.2 1.8 %collective-permute-done.16.refs_16_ = bf16[104,512]{1,0:T(8,128)(2,1)S(1)} collective-permute-done((bf16[104,512]{1,0:T(8,128)(2,1)S(1)}, bf16[104,512]{1,0:T(8,128)(2,1)S(1)}, u32[]{:S(2)}, u32[]{:S(2)}) %collective-permute-start.16) | collective-permute-done | bytes 106528 | tf_op jit(solution)/shard_map/ppermute | solution.py:344
  53.0 3.4 %shard_map.98.att_ref = bf16[96,1536]{1,0:T(8,128)(2,1)S(1)} custom-call(bf16[192,1536]{1,0:T(8,128)(2,1)S(1)} %get-tuple-element.32.refs_0_, bf16[104,512]{1,0:T(8,128)(2,1)S(1)} %get-tuple-element.30.refs_1_, bf16[104,512]{1,0:T(8,128)(2,1)S(1)} %collective-permute-done.1.refs_2_, bf16[104,512]{1,0:T(8,128)(2,1)S(1)} %collective-permute-done.2.refs_3_, ...), custom_call_target="tpu_custom_call" | custom-call | flops 905969664 | bytes 1572864 | tf_op jit(solution)/shard_map/pallas_call | solution.py:173
  56.5 1.6 %project_other.4 = bf16[96,3072]{1,0:T(8,128)(2,1)S(1)} custom-call(bf16[96,1536]{1,0:T(8,128)(2,1)S(1)} %shard_map.98.att_ref, bf16[1536,1536]{1,0:T(8,128)(2,1)S(1)} %get-tuple-element.33.rest_0_, bf16[1536,1536]{1,0:T(8,128)(2,1)S(1)} %get-tuple-element.48.rest_1_.rest_0_), custom_call_target="tpu_custom_call" | custom-call | flops 905969664 | bytes 9437184 | tf_op jit(solution)/shard_map/project_other/pallas_call | solution.py:212
  58.3 0.6 collective-permute-start.23
  58.9 1.3 %collective-permute-done.17.rest_2_ = bf16[96,3072]{1,0:T(8,128)(2,1)S(1)} collective-permute-done((bf16[96,3072]{1,0:T(8,128)(2,1)S(1)}, bf16[96,3072]{1,0:T(8,128)(2,1)S(1)}, u32[]{:S(2)}, u32[]{:S(2)}) %collective-permute-start.17) | collective-permute-done | bytes 589856 | tf_op jit(solution)/shard_map/ppermute | solution.py:350
  60.2 1.7 %project_own.4 = (bf16[48,3072]{1,0:T(8,128)(2,1)S(1)}, bf16[48,3072]{1,0:T(8,128)(2,1)S(1)}) custom-call(bf16[96,1536]{1,0:T(8,128)(2,1)S(1)} %shard_map.98.att_ref, bf16[1536,1536]{1,0:T(8,128)(2,1)S(1)} %get-tuple-element.39.rest_0_, bf16[1536,1536]{1,0:T(8,128)(2,1)S(1)} %get-tuple-element.47.rest_1_.rest_0_, ...), custom_call_target="tpu_custom_call" | custom-call | flops 905969664 | bytes 9437184 | tf_op jit(solution)/shard_map/project_own/pallas_call | solution.py:212
  61.9 0.6 collective-permute-start.20
  62.6 1.6 %collective-permute-start.18 = (bf16[48,3072]{1,0:T(8,128)(2,1)S(1)}, bf16[48,3072]{1,0:T(8,128)(2,1)S(1)}, u32[]{:S(2)}, u32[]{:S(2)}) collective-permute-start(bf16[48,3072]{1,0:T(8,128)(2,1)S(1)} %get-tuple-element.49), channel_id=1, source_target_pairs={{0,2},{1,3},{2,0},{3,1},{4,6},{5,7},{6,4},{7,5},{8,10},{9,11},{10,... | collective-permute-start | bytes 884744 | tf_op jit(solution)/shard_map/ppermute | solution.py:347
  64.2 7.6 %collective-permute-done.20 = bf16[48,3072]{1,0:T(8,128)(2,1)S(1)} collective-permute-done((bf16[48,3072]{1,0:T(8,128)(2,1)S(1)}, bf16[48,3072]{1,0:T(8,128)(2,1)S(1)}, u32[]{:S(2)}, u32[]{:S(2)}) %collective-permute-start.20) | collective-permute-done | bytes 294944 | tf_op jit(solution)/shard_map/ppermute | solution.py:347
  72.0 5.3 %collective-permute-done.18 = bf16[48,3072]{1,0:T(8,128)(2,1)S(1)} collective-permute-done((bf16[48,3072]{1,0:T(8,128)(2,1)S(1)}, bf16[48,3072]{1,0:T(8,128)(2,1)S(1)}, u32[]{:S(2)}, u32[]{:S(2)}) %collective-permute-start.18) | collective-permute-done | bytes 294944 | tf_op jit(solution)/shard_map/ppermute | solution.py:347
  77.5 2.0 %shard_map.99 = (bf16[192,6144]{1,0:T(8,128)(2,1)}, f32[1,192]{1,0:T(1,128)S(1)}, bf16[192,1536]{1,0:T(8,128)(2,1)}) custom-call(f32[4,1,1536]{2,1,0:T(1,128)S(1)} %pad_maximum_fusion.gain_ref, bf16[96,1536]{1,0:T(8,128)(2,1)S(1)} %add_convert_fusion.1.refs_0_, bf16[96,1536]{1,0:T(8,128)(2,1)S(1)} %collective-permute-done.23.refs_1_, ...), custom_call_target="tpu_custom_call" | custom-call | flops 2000000000 | bytes 2359296 | tf_op jit(solution)/shard_map/pallas_call | solution.py:302
  79.5 1.3 %shard_map.100 = (bf16[192,6144]{1,0:T(8,128)(2,1)}, f32[1,192]{1,0:T(1,128)S(1)}, bf16[192,1536]{1,0:T(8,128)(2,1)}) custom-call(f32[4,1,1536]{2,1,0:T(1,128)S(1)} %pad_maximum_fusion.gain_ref, bf16[48,3072]{1,0:T(8,128)(2,1)S(1)} %add_convert_fusion.2.refs_0_, ...), custom_call_target="tpu_custom_call", output_to_operand_aliasing={{0}: (4, {}), {2}: (5, {})} | custom-call | flops 2000000000 | bytes 1179648 | tf_op jit(solution)/shard_map/pallas_call | solution.py:302
  80.8 1.9 %shard_map.101 = (bf16[192,6144]{1,0:T(8,128)(2,1)}, f32[192]{0:T(256)}, bf16[192,1536]{1,0:T(8,128)(2,1)}) custom-call(f32[4,1,1536]{2,1,0:T(1,128)S(1)} %pad_maximum_fusion.gain_ref, bf16[48,3072]{1,0:T(8,128)(2,1)S(1)} %add_convert_fusion.3.refs_0_, ...), custom_call_target="tpu_custom_call", output_to_operand_aliasing={{0}: (4, {}), {2}: (5, {})} | custom-call | flops 2000000000 | bytes 1179648 | tf_op jit(solution)/shard_map/pallas_call | solution.py:302
  (30 shorter events, 1.1 us)
Async XLA Ops:
  1.6 6.1 %collective-permute-start = (bf16[104,512]{1,0:T(8,128)(2,1)S(1)}, bf16[104,512]{1,0:T(8,128)(2,1)S(1)}, u32[]{:S(2)}, u32[]{:S(2)}) collective-permute-start(bf16[104,512]{1,0:T(8,128)(2,1)S(1)} %get-tuple-element.30.refs_1_), channel_id=1, source_target_pairs={{0,8},{4,12},{8,0},{12,4},{16,24},{20,28},{24,16},{28,20},{1,9},{5... | collective-permute-start | bytes 319496 | tf_op jit(solution)/shard_map/ppermute | solution.py:341
  4.7 7.7 %collective-permute-start.2 = (bf16[104,512]{1,0:T(8,128)(2,1)S(1)}, bf16[104,512]{1,0:T(8,128)(2,1)S(1)}, u32[]{:S(2)}, u32[]{:S(2)}) collective-permute-start(bf16[104,512]{1,0:T(8,128)(2,1)S(1)} %get-tuple-element.30.refs_1_), channel_id=1, source_target_pairs={{0,16},{4,20},{8,24},{12,28},{16,0},{20,4},{24,8},{28,12},{1,17},{... | collective-permute-start | bytes 319496 | tf_op jit(solution)/shard_map/ppermute | solution.py:341
  12.3 4.7 %collective-permute-start.5 = (bf16[104,512]{1,0:T(8,128)(2,1)S(1)}, bf16[104,512]{1,0:T(8,128)(2,1)S(1)}, u32[]{:S(2)}, u32[]{:S(2)}) collective-permute-start(bf16[104,512]{1,0:T(8,128)(2,1)S(1)} %collective-permute-done.2.refs_3_), channel_id=1, source_target_pairs={{0,8},{4,12},{8,0},{12,4},{16,24},{20,28},{24,16},{28,20},{1,9},{5... | collective-permute-start | bytes 319496 | tf_op jit(solution)/shard_map/ppermute | solution.py:341
  12.8 5.8 %collective-permute-start.1 = (bf16[104,512]{1,0:T(8,128)(2,1)S(1)}, bf16[104,512]{1,0:T(8,128)(2,1)S(1)}, u32[]{:S(2)}, u32[]{:S(2)}) collective-permute-start(bf16[104,512]{1,0:T(8,128)(2,1)S(1)} %get-tuple-element.30.refs_1_), channel_id=1, source_target_pairs={{0,4},{4,0},{8,12},{12,8},{16,20},{20,16},{24,28},{28,24},{1,5},{5... | collective-permute-start | bytes 319496 | tf_op jit(solution)/shard_map/ppermute | solution.py:344
  14.2 6.7 %collective-permute-start.3 = (bf16[104,512]{1,0:T(8,128)(2,1)S(1)}, bf16[104,512]{1,0:T(8,128)(2,1)S(1)}, u32[]{:S(2)}, u32[]{:S(2)}) collective-permute-start(bf16[104,512]{1,0:T(8,128)(2,1)S(1)} %collective-permute-done.2.refs_3_), channel_id=1, source_target_pairs={{0,4},{4,0},{8,12},{12,8},{16,20},{20,16},{24,28},{28,24},{1,5},{5... | collective-permute-start | bytes 319496 | tf_op jit(solution)/shard_map/ppermute | solution.py:344
  14.8 7.2 %collective-permute-start.4 = (bf16[104,512]{1,0:T(8,128)(2,1)S(1)}, bf16[104,512]{1,0:T(8,128)(2,1)S(1)}, u32[]{:S(2)}, u32[]{:S(2)}) collective-permute-start(bf16[104,512]{1,0:T(8,128)(2,1)S(1)} %collective-permute-done.refs_5_), channel_id=1, source_target_pairs={{0,4},{4,0},{8,12},{12,8},{16,20},{20,16},{24,28},{28,24},{1,5},{5... | collective-permute-start | bytes 319496 | tf_op jit(solution)/shard_map/ppermute | solution.py:344
  17.0 6.1 %collective-permute-start.6 = (bf16[104,512]{1,0:T(8,128)(2,1)S(1)}, bf16[104,512]{1,0:T(8,128)(2,1)S(1)}, u32[]{:S(2)}, u32[]{:S(2)}) collective-permute-start(bf16[104,512]{1,0:T(8,128)(2,1)S(1)} %collective-permute-done.5.refs_7_), channel_id=1, source_target_pairs={{0,4},{4,0},{8,12},{12,8},{16,20},{20,16},{24,28},{28,24},{1,5},{5... | collective-permute-start | bytes 319496 | tf_op jit(solution)/shard_map/ppermute | solution.py:344
  26.3 10.2 %collective-permute-start.7 = (bf16[96,1536]{1,0:T(8,128)(2,1)S(1)}, bf16[96,1536]{1,0:T(8,128)(2,1)S(1)}, u32[]{:S(2)}, u32[]{:S(2)}) collective-permute-start(bf16[96,1536]{1,0:T(8,128)(2,1)S(1)} %project_other.3), channel_id=1, source_target_pairs={{0,1},{1,0},{2,3},{3,2},{4,5},{5,4},{6,7},{7,6},{8,9},{9,8},{10,11... | collective-permute-start | bytes 884744 | tf_op jit(solution)/shard_map/ppermute | solution.py:350
  29.8 12.3 %collective-permute-start.24 = (bf16[96,1536]{1,0:T(8,128)(2,1)S(1)}, bf16[96,1536]{1,0:T(8,128)(2,1)S(1)}, u32[]{:S(2)}, u32[]{:S(2)}) collective-permute-start(bf16[96,1536]{1,0:T(8,128)(2,1)S(1)} %project_other.5), channel_id=1, source_target_pairs={{0,1},{1,0},{2,3},{3,2},{4,5},{5,4},{6,7},{7,6},{8,9},{9,8},{10,11... | collective-permute-start | bytes 884744 | tf_op jit(solution)/shard_map/ppermute | solution.py:350
  30.4 8.0 %collective-permute-start.11 = (bf16[104,512]{1,0:T(8,128)(2,1)S(1)}, bf16[104,512]{1,0:T(8,128)(2,1)S(1)}, u32[]{:S(2)}, u32[]{:S(2)}) collective-permute-start(bf16[104,512]{1,0:T(8,128)(2,1)S(1)} %get-tuple-element.43.refs_9_), channel_id=1, source_target_pairs={{0,16},{4,20},{8,24},{12,28},{16,0},{20,4},{24,8},{28,12},{1,17},{... | collective-permute-start | bytes 319496 | tf_op jit(solution)/shard_map/ppermute | solution.py:341
  32.3 10.7 %collective-permute-start.13 = (bf16[104,512]{1,0:T(8,128)(2,1)S(1)}, bf16[104,512]{1,0:T(8,128)(2,1)S(1)}, u32[]{:S(2)}, u32[]{:S(2)}) collective-permute-start(bf16[104,512]{1,0:T(8,128)(2,1)S(1)} %get-tuple-element.43.refs_9_), channel_id=1, source_target_pairs={{0,8},{4,12},{8,0},{12,4},{16,24},{20,28},{24,16},{28,20},{1,9},{5... | collective-permute-start | bytes 319496 | tf_op jit(solution)/shard_map/ppermute | solution.py:341
  36.5 5.6 %copy-start = (f32[1,1536]{1,0:T(1,128)S(1)}, f32[1,1536]{1,0:T(1,128)}, u32[]{:S(2)}) copy-start(f32[1,1536]{1,0:T(1,128)} %param.12) | copy-start | bytes 18436
  38.4 5.3 %collective-permute-start.15 = (bf16[104,512]{1,0:T(8,128)(2,1)S(1)}, bf16[104,512]{1,0:T(8,128)(2,1)S(1)}, u32[]{:S(2)}, u32[]{:S(2)}) collective-permute-start(bf16[104,512]{1,0:T(8,128)(2,1)S(1)} %collective-permute-done.11.refs_11_), channel_id=1, source_target_pairs={{0,8},{4,12},{8,0},{12,4},{16,24},{20,28},{24,16},{28,20},{1,9},{5... | collective-permute-start | bytes 319496 | tf_op jit(solution)/shard_map/ppermute | solution.py:341
  39.1 10.3 %collective-permute-start.12 = (bf16[104,512]{1,0:T(8,128)(2,1)S(1)}, bf16[104,512]{1,0:T(8,128)(2,1)S(1)}, u32[]{:S(2)}, u32[]{:S(2)}) collective-permute-start(bf16[104,512]{1,0:T(8,128)(2,1)S(1)} %collective-permute-done.11.refs_11_), channel_id=1, source_target_pairs={{0,4},{4,0},{8,12},{12,8},{16,20},{20,16},{24,28},{28,24},{1,5},{5... | collective-permute-start | bytes 319496 | tf_op jit(solution)/shard_map/ppermute | solution.py:344
  40.6 17.7 %collective-permute-start.22 = (bf16[96,1536]{1,0:T(8,128)(2,1)S(1)}, bf16[96,1536]{1,0:T(8,128)(2,1)S(1)}, u32[]{:S(2)}, u32[]{:S(2)}) collective-permute-start(bf16[96,1536]{1,0:T(8,128)(2,1)S(1)} %project_own.3), channel_id=1, source_target_pairs={{0,2},{1,3},{2,0},{3,1},{4,6},{5,7},{6,4},{7,5},{8,10},{9,11},{10,... | collective-permute-start | bytes 884744 | tf_op jit(solution)/shard_map/ppermute | solution.py:347
  42.1 3.0 %collective-permute-start.8 = (f32[1,1536]{1,0:T(1,128)S(1)}, f32[1,1536]{1,0:T(1,128)S(1)}, u32[]{:S(2)}, u32[]{:S(2)}) collective-permute-start(f32[1,1536]{1,0:T(1,128)S(1)} %copy-done), channel_id=1, source_target_pairs={{0,1},{1,0},{2,3},{3,2},{4,5},{5,4},{6,7},{7,6},{8,9},{9,8},{10,11... | collective-permute-start | bytes 18440 | tf_op jit(solution)/shard_map/ppermute | solution.py:350
  43.0 5.9 %collective-permute-start.10 = (bf16[104,512]{1,0:T(8,128)(2,1)S(1)}, bf16[104,512]{1,0:T(8,128)(2,1)S(1)}, u32[]{:S(2)}, u32[]{:S(2)}) collective-permute-start(bf16[104,512]{1,0:T(8,128)(2,1)S(1)} %get-tuple-element.43.refs_9_), channel_id=1, source_target_pairs={{0,4},{4,0},{8,12},{12,8},{16,20},{20,16},{24,28},{28,24},{1,5},{5... | collective-permute-start | bytes 319496 | tf_op jit(solution)/shard_map/ppermute | solution.py:344
  43.7 7.5 %collective-permute-start.14 = (bf16[104,512]{1,0:T(8,128)(2,1)S(1)}, bf16[104,512]{1,0:T(8,128)(2,1)S(1)}, u32[]{:S(2)}, u32[]{:S(2)}) collective-permute-start(bf16[104,512]{1,0:T(8,128)(2,1)S(1)} %collective-permute-done.13.refs_13_), channel_id=1, source_target_pairs={{0,4},{4,0},{8,12},{12,8},{16,20},{20,16},{24,28},{28,24},{1,5},{5... | collective-permute-start | bytes 319496 | tf_op jit(solution)/shard_map/ppermute | solution.py:344
  45.1 7.9 %collective-permute-start.16 = (bf16[104,512]{1,0:T(8,128)(2,1)S(1)}, bf16[104,512]{1,0:T(8,128)(2,1)S(1)}, u32[]{:S(2)}, u32[]{:S(2)}) collective-permute-start(bf16[104,512]{1,0:T(8,128)(2,1)S(1)} %collective-permute-done.15.refs_15_), channel_id=1, source_target_pairs={{0,4},{4,0},{8,12},{12,8},{16,20},{20,16},{24,28},{28,24},{1,5},{5... | collective-permute-start | bytes 319496 | tf_op jit(solution)/shard_map/ppermute | solution.py:344
  48.9 13.5 %collective-permute-start.25 = (bf16[96,1536]{1,0:T(8,128)(2,1)S(1)}, bf16[96,1536]{1,0:T(8,128)(2,1)S(1)}, u32[]{:S(2)}, u32[]{:S(2)}) collective-permute-start(bf16[96,1536]{1,0:T(8,128)(2,1)S(1)} %project_own.5), channel_id=1, source_target_pairs={{0,2},{1,3},{2,0},{3,1},{4,6},{5,7},{6,4},{7,5},{8,10},{9,11},{10,... | collective-permute-start | bytes 884744 | tf_op jit(solution)/shard_map/ppermute | solution.py:347
  49.5 8.7 %collective-permute-start.9 = (f32[2,1,1536]{2,1,0:T(1,128)S(1)}, f32[2,1,1536]{2,1,0:T(1,128)S(1)}, u32[]{:S(2)}, u32[]{:S(2)}) collective-permute-start(f32[2,1,1536]{2,1,0:T(1,128)S(1)} %pad_maximum_fusion.1), channel_id=1, source_target_pairs={{0,2},{1,3},{2,0},{3,1},{4,6},{5,7},{6,4},{7,5},{8,10},{9,11},{10,... | collective-permute-start | bytes 36872 | tf_op jit(solution)/shard_map/ppermute | solution.py:347
  58.1 2.1 %collective-permute-start.17 = (bf16[96,3072]{1,0:T(8,128)(2,1)S(1)}, bf16[96,3072]{1,0:T(8,128)(2,1)S(1)}, u32[]{:S(2)}, u32[]{:S(2)}) collective-permute-start(bf16[96,3072]{1,0:T(8,128)(2,1)S(1)} %project_other.4), channel_id=1, source_target_pairs={{0,1},{1,0},{2,3},{3,2},{4,5},{5,4},{6,7},{7,6},{8,9},{9,8},{10,11... | collective-permute-start | bytes 1769480 | tf_op jit(solution)/shard_map/ppermute | solution.py:350
  58.3 19.1 %collective-permute-start.23 = (bf16[96,1536]{1,0:T(8,128)(2,1)S(1)}, bf16[96,1536]{1,0:T(8,128)(2,1)S(1)}, u32[]{:S(2)}, u32[]{:S(2)}) collective-permute-start(bf16[96,1536]{1,0:T(8,128)(2,1)S(1)} %add_convert_fusion.1.refs_0_), channel_id=1, source_target_pairs={{0,1},{1,0},{2,3},{3,2},{4,5},{5,4},{6,7},{7,6},{8,9},{9,8},{10,11... | collective-permute-start | bytes 884744 | tf_op jit(solution)/shard_map/ppermute | solution.py:350
  61.9 9.9 %collective-permute-start.20 = (bf16[48,3072]{1,0:T(8,128)(2,1)S(1)}, bf16[48,3072]{1,0:T(8,128)(2,1)S(1)}, u32[]{:S(2)}, u32[]{:S(2)}) collective-permute-start(bf16[48,3072]{1,0:T(8,128)(2,1)S(1)} %get-tuple-element.50), channel_id=1, source_target_pairs={{0,2},{1,3},{2,0},{3,1},{4,6},{5,7},{6,4},{7,5},{8,10},{9,11},{10,... | collective-permute-start | bytes 884744 | tf_op jit(solution)/shard_map/ppermute | solution.py:347
  62.5 15.0 %collective-permute-start.26 = (bf16[96,1536]{1,0:T(8,128)(2,1)S(1)}, bf16[96,1536]{1,0:T(8,128)(2,1)S(1)}, u32[]{:S(2)}, u32[]{:S(2)}) collective-permute-start(bf16[96,1536]{1,0:T(8,128)(2,1)S(1)} %add_convert_fusion.refs_2_), channel_id=1, source_target_pairs={{0,1},{1,0},{2,3},{3,2},{4,5},{5,4},{6,7},{7,6},{8,9},{9,8},{10,11... | collective-permute-start | bytes 884744 | tf_op jit(solution)/shard_map/ppermute | solution.py:350
  62.6 14.7 %collective-permute-start.18 = (bf16[48,3072]{1,0:T(8,128)(2,1)S(1)}, bf16[48,3072]{1,0:T(8,128)(2,1)S(1)}, u32[]{:S(2)}, u32[]{:S(2)}) collective-permute-start(bf16[48,3072]{1,0:T(8,128)(2,1)S(1)} %get-tuple-element.49), channel_id=1, source_target_pairs={{0,2},{1,3},{2,0},{3,1},{4,6},{5,7},{6,4},{7,5},{8,10},{9,11},{10,... | collective-permute-start | bytes 884744 | tf_op jit(solution)/shard_map/ppermute | solution.py:347
  71.9 7.6 %collective-permute-start.21 = (bf16[48,3072]{1,0:T(8,128)(2,1)S(1)}, bf16[48,3072]{1,0:T(8,128)(2,1)S(1)}, u32[]{:S(2)}, u32[]{:S(2)}) collective-permute-start(bf16[48,3072]{1,0:T(8,128)(2,1)S(1)} %add_convert_fusion.2.refs_0_), channel_id=1, source_target_pairs={{0,1},{1,0},{2,3},{3,2},{4,5},{5,4},{6,7},{7,6},{8,9},{9,8},{10,11... | collective-permute-start | bytes 884744 | tf_op jit(solution)/shard_map/ppermute | solution.py:350
  77.4 3.4 %collective-permute-start.19 = (bf16[48,3072]{1,0:T(8,128)(2,1)S(1)}, bf16[48,3072]{1,0:T(8,128)(2,1)S(1)}, u32[]{:S(2)}, u32[]{:S(2)}) collective-permute-start(bf16[48,3072]{1,0:T(8,128)(2,1)S(1)} %add_convert_fusion.3.refs_0_), channel_id=1, source_target_pairs={{0,1},{1,0},{2,3},{3,2},{4,5},{5,4},{6,7},{7,6},{8,9},{9,8},{10,11... | collective-permute-start | bytes 884744 | tf_op jit(solution)/shard_map/ppermute | solution.py:350
where the time goes:
time: 82.8 us; the launch traced here: 82.7 us
  waiting for transfers between devices  28.5 us (34%)
  Pallas kernels  27.5 us (33%)
  starting transfers between devices  25.4 us (31%)
  between operations  0.9 us (1%)
    ppermute x5, waiting for transfers between devices, move_y(): return lax.ppermute(array, 'tp', swap(ny, n_tp, cores, k))  13 us
    ppermute x8, waiting for transfers between devices, move_x(): return lax.ppermute(array, 'seq', swap(nx, n_seq, 1, k))  9.89 us
    ppermute x6, starting transfers between devices, move_z(): return lax.ppermute(array, 'seq', swap(nz, n_seq, nx, k))  9.23 us
    ppermute x8, starting transfers between devices, move_x(): return lax.ppermute(array, 'seq', swap(nx, n_seq, 1, k))  9.03 us
    pallas_call x3, Pallas kernels, fetch(): pl.pallas_call(functools.partial(fetch_body, cores, blocks, width), out_s...  8.84 us
    pallas_call x6, Pallas kernels, project(): pl.pallas_call(functools.partial(project_body, cores, blocks, half, own),...  6.84 us
    pallas_call x2, Pallas kernels, attend(): pl.pallas_call(functools.partial(attend_body, run_rows, runs, query_half,...  5.74 us
    ppermute x5, starting transfers between devices, move_y(): return lax.ppermute(array, 'tp', swap(ny, n_tp, cores, k))  5.7 us
  transfers between devices with their start and end apart: 27, of which 14 were waited for; matrix products, arithmetic and copies ran while one was open for 0% of the time, Pallas kernels for 26%

commit v1 on v0

--- a/solution.py
+++ b/solution.py
@@ -43,13 +43,6 @@
 
 def grant(mib):
     return pltpu.CompilerParams(vmem_limit_bytes=mib << 20)
-
-
-def run_copies(copies):
-    for copy in copies:
-        copy.start()
-    for copy in copies:
-        copy.wait()
 
 
 def pack_body(run_rows, pos_ref, key_ref, value_ref, low_ref, high_ref, number_ref, sems):
@@ -80,43 +73,41 @@
         out_specs=(in_vmem(), in_vmem()),
         scratch_shapes=[pltpu.SMEM(positions.shape, jnp.int32), pltpu.SemaphoreType.DMA((5,))],
         compiler_params=grant(4),
-        cost_estimate=cost(2e8, 4 * keys.size * 2),
+        cost_estimate=cost(4e10, 4 * keys.size * 2),
         name="pack",
     )(far(positions), far(keys), far(values))
 
 
-def fetch_body(cores, blocks, width, weight_ref, *refs):
-    extra = (len(refs) - 1 - len(blocks)) // 2
-    outs, sems = refs[extra:-1], refs[-1]
-    core = lax.axis_index("tp") % cores
-    copies = []
-    for i, (yb, k) in enumerate(blocks):
-        start = pl.multiple_of((yb * cores + (core ^ k)) * width, HEAD)
-        copies.append(pltpu.make_async_copy(weight_ref.at[:, pl.ds(start, width)], outs[i], sems.at[i]))
-    for i in range(extra):
-        at = len(blocks) + i
-        copies.append(pltpu.make_async_copy(refs[i], outs[at], sems.at[at]))
-    run_copies(copies)
-
-
-def fetch(cores, blocks, width, weight, extra):
-    shapes = [(weight.shape[0], width)] * len(blocks) + [array.shape for array in extra]
+def join_body(*refs):
+    rows = refs[0].shape[0]
+    for i, ref in enumerate(refs[:-1]):
+        refs[-1][i * rows : (i + 1) * rows, :] = ref[...]
+
+
+def join(pieces):
+    rows, width = pieces[0].shape
     return pl.pallas_call(
-        functools.partial(fetch_body, cores, blocks, width),
-        out_shape=tuple(VMEM(shape, BF16) for shape in shapes),
-        in_specs=[in_place()] * (1 + len(extra)),
-        out_specs=(in_vmem(),) * len(shapes),
-        scratch_shapes=[pltpu.SemaphoreType.DMA((len(shapes),))],
+        join_body,
+        out_shape=VMEM((len(pieces) * rows, width), BF16),
+        in_specs=[in_vmem()] * len(pieces),
+        out_specs=in_vmem(),
         compiler_params=grant(4),
-        cost_estimate=cost(2e9, 2 * weight.shape[0] * width * len(blocks)),
-    )(far(weight), *[far(array) for array in extra])
-
-
-def attend_body(run_rows, runs, query_half, key_halves, count, *refs):
+        cost_estimate=cost(2e8, 4 * len(pieces) * rows * width),
+        name="join",
+    )(*[near(piece) for piece in pieces])
+
+
+def attend_body(run_rows, runs, query_half, key_halves, *refs):
     query_ref = refs[0]
-    pieces = refs[1 : 1 + len(key_halves) * count]
-    out_ref, kv_ref, hide_ref = refs[1 + len(key_halves) * count :]
-    total = len(pieces) * run_rows
+    pieces = refs[1 : 1 + len(key_halves)]
+    out_ref, kv_ref, hide_ref = refs[1 + len(key_halves) :]
+    block_rows = run_rows + TAG_ROWS
+    held = [
+        (piece, row, half)
+        for piece, half in zip(pieces, key_halves)
+        for row in range(0, piece.shape[0], block_rows)
+    ]
+    total = len(held) * run_rows
     kv_width = pieces[0].shape[1] // 2
     query_width = query_ref.shape[1]
     kv_heads = kv_width // HEAD
@@ -128,13 +119,13 @@
     base = jnp.zeros((1, total), F32)
     first = jnp.zeros((1, total), jnp.int32)
     own = None
-    for number, piece in enumerate(pieces):
-        kv_ref[pl.ds(number * run_rows, run_rows), :] = piece[:run_rows, :]
-        tag = piece[run_rows : run_rows + TAG_ROWS, :HEAD].astype(F32)[:1, :]
+    for number, (piece, row, half) in enumerate(held):
+        kv_ref[pl.ds(number * run_rows, run_rows), :] = piece[row : row + run_rows, :]
+        tag = piece[row + run_rows : row + block_rows, :HEAD].astype(F32)[:1, :]
         if number == 0:
             own = tag[:, :1]
         tag = jnp.concatenate([tag] * (total // HEAD), axis=1)
-        if key_halves[number // count] == 1:
+        if half == 1:
             tag = (runs - 1) - tag
         inside = lane >= number * run_rows
         base = jnp.where(inside, tag, base)
@@ -164,14 +155,14 @@
                 out_ref[:, h * HEAD : (h + 1) * HEAD] = mean.astype(BF16)
 
 
-def attend(queries, query_half, piece_sets, key_halves, runs):
+def attend(queries, query_half, piece_sets, runs):
     run_rows = queries.shape[0] // 2
-    count = len(piece_sets[0])
+    key_halves = [half for half, pieces in enumerate(piece_sets) for piece in pieces]
     pieces = [near(piece) for pieces in piece_sets for piece in pieces]
-    total = len(pieces) * run_rows
+    total = sum(piece.shape[0] for piece in pieces) // (run_rows + TAG_ROWS) * run_rows
     width = queries.shape[1]
     return pl.pallas_call(
-        functools.partial(attend_body, run_rows, runs, query_half, key_halves, count),
+        functools.partial(attend_body, run_rows, runs, query_half, key_halves),
         out_shape=VMEM((run_rows, width), BF16),
         in_specs=[in_vmem()] * (1 + len(pieces)),
         out_specs=in_vmem(),
@@ -184,13 +175,14 @@
     )(near(queries), *pieces)
 
 
-def project_body(cores, blocks, half, own, att_ref, *rest):
-    weights, rest = rest[: len(blocks)], rest[len(blocks) :]
+def project_body(cores, blocks, half, own, att_ref, weight_ref, *rest):
     outs = rest[2:] if own else rest
-    width = weights[0].shape[1]
+    width = outs[0].shape[1] // len(blocks)
     tp = lax.axis_index("tp")
     for i, yb in enumerate(blocks):
-        total = jnp.dot(att_ref[...], weights[i][...], preferred_element_type=F32)
+        block = yb * cores + ((tp % cores) ^ (0 if own else 1))
+        start = pl.multiple_of(block * width, HEAD)
+        total = jnp.dot(att_ref[...], weight_ref[:, pl.ds(start, width)], preferred_element_type=F32)
         columns = slice(i * width, (i + 1) * width)
         if own:
             arrived, residual = rest[0], rest[1]
@@ -204,11 +196,11 @@
             out[:, columns] = total[j * rows : (j + 1) * rows]
 
 
-def project(cores, blocks, half, attended, weights, cuts=1, arrived=None, residual=None):
+def project(cores, blocks, half, attended, weight, block_width, cuts=1, arrived=None, residual=None):
     rows, depth = attended.shape
-    width = weights[0].shape[1] * len(blocks)
+    width = block_width * len(blocks)
     own = arrived is not None
-    operands = [attended, *weights] + ([arrived, residual] if own else [])
+    operands = [attended, weight] + ([arrived, residual] if own else [])
     result = pl.pallas_call(
         functools.partial(project_body, cores, blocks, half, own),
         out_shape=(VMEM((rows // cuts, width), BF16),) * cuts,
@@ -351,50 +343,38 @@
 
     low, high = pack(positions, keys, values)
     low_pieces = [low] + [move_x(low, j) for j in range(1, nx)]
-    weights = {}
-
-    def held_until_a(piece):
-        if "a" not in state:
-            source = after(out_weight, near_block)
-            *blocks, state["query"] = fetch(cores, [(0, 1)], block_width, source, [queries])
-            weights[0, 1] = blocks[0]
-            state["a"] = blocks[0]
-        return after(piece, state["a"])
-
-    state = {}
-    near_block = None
+
     step, column = nz // 2, [low]
     firsts = {k: move_z(low, k) for k in dict.fromkeys((step, 1)) if k}
-    near_block = firsts[1]
     while step:
         for held in list(column):
             if held is low and step in firsts:
                 column.append(firsts[step])
             else:
-                column.append(move_z(held_until_a(held), step))
+                column.append(move_z(held, step))
         step //= 2
     for piece in column[1:]:
-        gate = piece if piece is near_block else after(piece, state.get("a", near_block))
-        low_pieces += [piece] + [move_x(gate, j) for j in range(1, nx)]
-    if "query" not in state:
-        held_until_a(low)
-    query_near = state["query"]
-
-    source = after(out_weight, state["a"])
-    rest = [(yb, 1) for yb in range(1, ny)]
-    *blocks, residual_near = fetch(cores, rest, block_width, source, [residual])
-    weights.update(zip(rest, blocks))
-    source = after(out_weight, residual_near, column[-1])
-    rest = [(yb, 0) for yb in range(ny)]
-    weights.update(zip(rest, fetch(cores, rest, block_width, source, [])))
-
-    early = attend(query_near, 0, [low_pieces], (0,), runs)
+        low_pieces += [piece] + [move_x(piece, j) for j in range(1, nx)]
+
+    high_line = [high] + [move_x(high, j) for j in range(1, nx)]
+    high_line = join([after(high_line[0], firsts[1]), *high_line[1:]])
+    step, high_pieces = nz // 2, [high_line]
+    firsts = {k: move_z(high_line, k) for k in dict.fromkeys((step, 1)) if k}
+    while step:
+        for held in list(high_pieces):
+            if held is high_line and step in firsts:
+                high_pieces.append(firsts[step])
+            else:
+                high_pieces.append(move_z(held, step))
+        step //= 2
+
+    early = attend(queries, 0, [low_pieces], runs)
     sent, parts, marks = [], [], []
     for yb in range(ny):
-        other = project(cores, [yb], 0, early, [weights[yb, 1]])
+        other = project(cores, [yb], 0, early, out_weight, block_width)
         sent.append(move_core(other, 1))
     for yb in range(ny):
-        own = project(cores, [yb], 0, early, [weights[yb, 0]], 1, sent[yb], residual_near)
+        own = project(cores, [yb], 0, early, out_weight, block_width, 1, sent[yb], residual)
         marks.append(own)
         total = tree_sum([own] + [move_y(own, k) for k in range(1, ny)])
         parts += [total, move_core(total, 1)]
@@ -404,25 +384,11 @@
     gains = jnp.concatenate([pair] + [move_y(pair, k) for k in range(1, ny)])
     result = finish(ny, cores, 0, all_rows, gains, parts, places, None, False)
 
-    step, column = nz // 2, [high]
-    ready = after(high, state["a"])
-    firsts = {k: move_z(ready, k) for k in dict.fromkeys((step, 1)) if k}
-    while step:
-        for held in list(column):
-            if held is high and step in firsts:
-                column.append(firsts[step])
-            else:
-                column.append(move_z(after(held, marks[0]), step))
-        step //= 2
-    high_pieces = []
-    for piece in column:
-        high_pieces += [piece] + [move_x(after(piece, marks[0]), j) for j in range(1, nx)]
-
-    late = attend(query_near, 1, [low_pieces, high_pieces], (0, 1), runs)
+    late = attend(queries, 1, [low_pieces, high_pieces], runs)
     every = list(range(ny))
-    other = project(cores, every, 1, late, [weights[yb, 1] for yb in every])
+    other = project(cores, every, 1, late, out_weight, block_width)
     arrived = move_core(other, 1)
-    cuts = project(cores, every, 1, late, [weights[yb, 0] for yb in every], 2, arrived, residual_near)
+    cuts = project(cores, every, 1, late, out_weight, block_width, 2, arrived, residual)
     places = {(yb, k): (k, yb) for yb in range(ny) for k in range(cores)}
     for i, own in enumerate(cuts):
         total = tree_sum([own] + [move_y(own, k) for k in range(1, ny)])

time: 82.8 us -> 76.6 us (0.925)
  Pallas kernels: 27.5 us -> 19.2 us
  waiting for transfers between devices: 28.5 us -> 33.9 us
  starting transfers between devices: 25.4 us -> 21.9 us
    pallas_call x3 -> x1, Pallas kernels: 8.84 us -> 0.01 us  [join(): pl.pallas_call(join_body, out_shape=VMEM((len(pieces) * rows, width), BF1...]
    ppermute x6, waiting for transfers between devices: 4.34 us -> 12.9 us  [move_z(): return lax.ppermute(array, 'seq', swap(nz, n_seq, nx, k))]
    ppermute x8 -> x5, waiting for transfers between devices: 9.89 us -> 3.48 us  [move_x(): return lax.ppermute(array, 'seq', swap(nx, n_seq, 1, k))]
    ppermute x8 -> x5, starting transfers between devices: 9.03 us -> 3.54 us  [move_x(): return lax.ppermute(array, 'seq', swap(nx, n_seq, 1, k))]
    ppermute x5, waiting for transfers between devices: 13 us -> 17.6 us  [move_y(): return lax.ppermute(array, 'tp', swap(ny, n_tp, cores, k))]
    ppermute x8, waiting for transfers between devices: 1.33 us -> 0.02 us  [move_core(): return lax.ppermute(array, 'tp', swap(cores, n_tp, 1, k))]
    ppermute x5, starting transfers between devices: 5.7 us -> 6.91 us  [move_y(): return lax.ppermute(array, 'tp', swap(ny, n_tp, cores, k))]
    ppermute x6, starting transfers between devices: 9.23 us -> 10.4 us  [move_z(): return lax.ppermute(array, 'seq', swap(nz, n_seq, nx, k))]
  transfers between devices with their start and end apart: 27 -> 24, of which waited for: 14 -> 9; matrix products, arithmetic and copies ran while one was open for 0% -> 0% of each run, Pallas kernels for 26% -> 21%
where the time goes in v1:
time: 76.6 us; the launch traced here: 76.5 us
  waiting for transfers between devices  33.9 us (44%)
  starting transfers between devices  21.9 us (29%)
  Pallas kernels  19.2 us (25%)
  between operations  1.09 us (1%)
    ppermute x5, waiting for transfers between devices, move_y(): return lax.ppermute(array, 'tp', swap(ny, n_tp, cores, k))  17.6 us
    ppermute x6, waiting for transfers between devices, move_z(): return lax.ppermute(array, 'seq', swap(nz, n_seq, nx, k))  12.9 us
    ppermute x6, starting transfers between devices, move_z(): return lax.ppermute(array, 'seq', swap(nz, n_seq, nx, k))  10.4 us
    pallas_call x6, Pallas kernels, project(): pl.pallas_call(functools.partial(project_body, cores, blocks, half, own),...  7.26 us
    ppermute x5, starting transfers between devices, move_y(): return lax.ppermute(array, 'tp', swap(ny, n_tp, cores, k))  6.91 us
    pallas_call x2, Pallas kernels, attend(): pl.pallas_call(functools.partial(attend_body, run_rows, runs, query_half,...  5.73 us
    pallas_call x3, Pallas kernels, finish(): pl.pallas_call(functools.partial(finish_body, ny, cores, row, places, len...  5.16 us
    ppermute x5, starting transfers between devices, move_x(): return lax.ppermute(array, 'seq', swap(nx, n_seq, 1, k))  3.54 us
  transfers between devices with their start and end apart: 24, of which 9 were waited for; matrix products, arithmetic and copies ran while one was open for 0% of the time, Pallas kernels for 21%

profile of v1, /device:TPU:0, one launch (start us, length us, event | category | flops | bytes accessed | tf_op | source)
XLA Modules:
  0.0 76.5 jit_solution(14359673114667746097)
XLA Ops:
  0.7 1.1 %pack.1 = (bf16[104,512]{1,0:T(8,128)(2,1)S(1)}, bf16[104,512]{1,0:T(8,128)(2,1)S(1)}) custom-call(s32[192]{0:T(256)} %pos_ref.1, bf16[192,256]{1,0:T(8,128)(2,1)} %key_ref.1, bf16[192,256]{1,0:T(8,128)(2,1)} %value_ref.1), custom_call_target="tpu_custom_call" | custom-call | flops 40000000000 | bytes 393216 | tf_op jit(solution)/shard_map/pack/pallas_call | solution.py:69
  1.7 3.1 %collective-permute-start.3 = (bf16[104,512]{1,0:T(8,128)(2,1)S(1)}, bf16[104,512]{1,0:T(8,128)(2,1)S(1)}, u32[]{:S(2)}, u32[]{:S(2)}) collective-permute-start(bf16[104,512]{1,0:T(8,128)(2,1)S(1)} %get-tuple-element.15.refs_1_), channel_id=1, source_target_pairs={{0,8},{4,12},{8,0},{12,4},{16,24},{20,28},{24,16},{28,20},{1,9},{5... | collective-permute-start | bytes 319496 | tf_op jit(solution)/shard_map/ppermute | solution.py:333
  4.8 1.5 %collective-permute-start.10 = (bf16[104,512]{1,0:T(8,128)(2,1)S(1)}, bf16[104,512]{1,0:T(8,128)(2,1)S(1)}, u32[]{:S(2)}, u32[]{:S(2)}) collective-permute-start(bf16[104,512]{1,0:T(8,128)(2,1)S(1)} %get-tuple-element.18.refs_0_), channel_id=1, source_target_pairs={{0,4},{4,0},{8,12},{12,8},{16,20},{20,16},{24,28},{28,24},{1,5},{5... | collective-permute-start | bytes 319496 | tf_op jit(solution)/shard_map/ppermute | solution.py:336
  6.3 2.6 %collective-permute-start.1 = (bf16[104,512]{1,0:T(8,128)(2,1)S(1)}, bf16[104,512]{1,0:T(8,128)(2,1)S(1)}, u32[]{:S(2)}, u32[]{:S(2)}) collective-permute-start(bf16[104,512]{1,0:T(8,128)(2,1)S(1)} %get-tuple-element.15.refs_1_), channel_id=1, source_target_pairs={{0,16},{4,20},{8,24},{12,28},{16,0},{20,4},{24,8},{28,12},{1,17},{... | collective-permute-start | bytes 319496 | tf_op jit(solution)/shard_map/ppermute | solution.py:333
  8.9 0.6 collective-permute-done.10.refs_1_
  9.6 2.7 %collective-permute-start.11 = (bf16[208,512]{1,0:T(8,128)(2,1)S(1)}, bf16[208,512]{1,0:T(8,128)(2,1)S(1)}, u32[]{:S(2)}, u32[]{:S(2)}) collective-permute-start(bf16[208,512]{1,0:T(8,128)(2,1)S(1)} %join.1.refs_9_), channel_id=1, source_target_pairs={{0,16},{4,20},{8,24},{12,28},{16,0},{20,4},{24,8},{28,12},{1,17},{... | collective-permute-start | bytes 638984 | tf_op jit(solution)/shard_map/ppermute | solution.py:333
  12.2 6.8 %collective-permute-done.1.refs_3_ = bf16[104,512]{1,0:T(8,128)(2,1)S(1)} collective-permute-done((bf16[104,512]{1,0:T(8,128)(2,1)S(1)}, bf16[104,512]{1,0:T(8,128)(2,1)S(1)}, u32[]{:S(2)}, u32[]{:S(2)}) %collective-permute-start.1) | collective-permute-done | bytes 106528 | tf_op jit(solution)/shard_map/ppermute | solution.py:333
  19.0 2.0 %collective-permute-start.2 = (bf16[104,512]{1,0:T(8,128)(2,1)S(1)}, bf16[104,512]{1,0:T(8,128)(2,1)S(1)}, u32[]{:S(2)}, u32[]{:S(2)}) collective-permute-start(bf16[104,512]{1,0:T(8,128)(2,1)S(1)} %collective-permute-done.1.refs_3_), channel_id=1, source_target_pairs={{0,4},{4,0},{8,12},{12,8},{16,20},{20,16},{24,28},{28,24},{1,5},{5... | collective-permute-start | bytes 319496 | tf_op jit(solution)/shard_map/ppermute | solution.py:336
  21.0 0.0 collective-permute-start.4
  21.1 3.9 %collective-permute-done.5.refs_7_ = bf16[104,512]{1,0:T(8,128)(2,1)S(1)} collective-permute-done((bf16[104,512]{1,0:T(8,128)(2,1)S(1)}, bf16[104,512]{1,0:T(8,128)(2,1)S(1)}, u32[]{:S(2)}, u32[]{:S(2)}) %collective-permute-start.5) | collective-permute-done | bytes 106528 | tf_op jit(solution)/shard_map/ppermute | solution.py:333
  25.0 1.3 %collective-permute-start.12 = (bf16[208,512]{1,0:T(8,128)(2,1)S(1)}, bf16[208,512]{1,0:T(8,128)(2,1)S(1)}, u32[]{:S(2)}, u32[]{:S(2)}) collective-permute-start(bf16[208,512]{1,0:T(8,128)(2,1)S(1)} %join.1.refs_9_), channel_id=1, source_target_pairs={{0,8},{4,12},{8,0},{12,4},{16,24},{20,28},{24,16},{28,20},{1,9},{5... | collective-permute-start | bytes 638984 | tf_op jit(solution)/shard_map/ppermute | solution.py:333
  26.3 0.7 collective-permute-start.13
  27.1 2.8 %collective-permute-done.6.refs_8_ = bf16[104,512]{1,0:T(8,128)(2,1)S(1)} collective-permute-done((bf16[104,512]{1,0:T(8,128)(2,1)S(1)}, bf16[104,512]{1,0:T(8,128)(2,1)S(1)}, u32[]{:S(2)}, u32[]{:S(2)}) %collective-permute-start.6) | collective-permute-done | bytes 106528 | tf_op jit(solution)/shard_map/ppermute | solution.py:336
  29.9 2.3 %shard_map.94.att_ref = bf16[96,1536]{1,0:T(8,128)(2,1)S(1)} custom-call(bf16[192,1536]{1,0:T(8,128)(2,1)S(1)} %copy-done.2, bf16[104,512]{1,0:T(8,128)(2,1)S(1)} %get-tuple-element.15.refs_1_, bf16[104,512]{1,0:T(8,128)(2,1)S(1)} %collective-permute-done.refs_2_, bf16[104,512]{1,0:T(8,128)(2,1)S(1)} %collective-permute-done.1.refs_3_, ...), custom_call_target="tpu_custom_call" | custom-call | flops 452984832 | bytes 786432 | tf_op jit(solution)/shard_map/pallas_call | solution.py:164
  32.2 0.9 %project_other.3 = bf16[96,1536]{1,0:T(8,128)(2,1)S(1)} custom-call(bf16[96,1536]{1,0:T(8,128)(2,1)S(1)} %shard_map.94.att_ref, bf16[1536,6144]{1,0:T(8,128)(2,1)S(1)} %copy-done), custom_call_target="tpu_custom_call" | custom-call | flops 452984832 | bytes 4718592 | tf_op jit(solution)/shard_map/project_other/pallas_call | solution.py:204
  33.1 0.1 collective-permute-start.7
  33.2 0.9 %project_other.5 = bf16[96,1536]{1,0:T(8,128)(2,1)S(1)} custom-call(bf16[96,1536]{1,0:T(8,128)(2,1)S(1)} %shard_map.94.att_ref, bf16[1536,6144]{1,0:T(8,128)(2,1)S(1)} %copy-done), custom_call_target="tpu_custom_call" | custom-call | flops 452984832 | bytes 4718592 | tf_op jit(solution)/shard_map/project_other/pallas_call | solution.py:204
  34.1 0.0 copy-start.1
  34.1 0.5 collective-permute-start.21
  34.7 2.1 %collective-permute-done.13.refs_12_ = bf16[208,512]{1,0:T(8,128)(2,1)S(1)} collective-permute-done((bf16[208,512]{1,0:T(8,128)(2,1)S(1)}, bf16[208,512]{1,0:T(8,128)(2,1)S(1)}, u32[]{:S(2)}, u32[]{:S(2)}) %collective-permute-start.13) | collective-permute-done | bytes 213024 | tf_op jit(solution)/shard_map/ppermute | solution.py:333
  36.8 3.4 %shard_map.95.att_ref = bf16[96,1536]{1,0:T(8,128)(2,1)S(1)} custom-call(bf16[192,1536]{1,0:T(8,128)(2,1)S(1)} %copy-done.2, bf16[104,512]{1,0:T(8,128)(2,1)S(1)} %get-tuple-element.15.refs_1_, bf16[104,512]{1,0:T(8,128)(2,1)S(1)} %collective-permute-done.refs_2_, bf16[104,512]{1,0:T(8,128)(2,1)S(1)} %collective-permute-done.1.refs_3_, ...), custom_call_target="tpu_custom_call" | custom-call | flops 905969664 | bytes 1572864 | tf_op jit(solution)/shard_map/pallas_call | solution.py:164
  40.2 0.0 copy-start.3
  40.2 1.0 %project_own.3 = bf16[96,1536]{1,0:T(8,128)(2,1)S(1)} custom-call(bf16[96,1536]{1,0:T(8,128)(2,1)S(1)} %shard_map.94.att_ref, bf16[1536,6144]{1,0:T(8,128)(2,1)S(1)} %copy-done, bf16[96,1536]{1,0:T(8,128)(2,1)S(1)} %collective-permute-done.7.rest_0_, bf16[192,1536]{1,0:T(8,128)(2,1)S(1)} %copy-done.1), custom_call_target="tpu_custom_call" | custom-call | flops 452984832 | bytes 4718592 | tf_op jit(solution)/shard_map/project_own/pallas_call | solution.py:204
  41.2 0.1 collective-permute-start.8
  41.3 0.9 %project_own.5 = bf16[96,1536]{1,0:T(8,128)(2,1)S(1)} custom-call(bf16[96,1536]{1,0:T(8,128)(2,1)S(1)} %shard_map.94.att_ref, bf16[1536,6144]{1,0:T(8,128)(2,1)S(1)} %copy-done, bf16[96,1536]{1,0:T(8,128)(2,1)S(1)} %collective-permute-done.21.rest_0_, bf16[192,1536]{1,0:T(8,128)(2,1)S(1)} %copy-done.1), custom_call_target="tpu_custom_call" | custom-call | flops 452984832 | bytes 4718592 | tf_op jit(solution)/shard_map/project_own/pallas_call | solution.py:204
  42.3 1.6 %collective-permute-start.22 = (bf16[96,1536]{1,0:T(8,128)(2,1)S(1)}, bf16[96,1536]{1,0:T(8,128)(2,1)S(1)}, u32[]{:S(2)}, u32[]{:S(2)}) collective-permute-start(bf16[96,1536]{1,0:T(8,128)(2,1)S(1)} %project_own.5), channel_id=1, source_target_pairs={{0,2},{1,3},{2,0},{3,1},{4,6},{5,7},{6,4},{7,5},{8,10},{9,11},{10,... | collective-permute-start | bytes 884744 | tf_op jit(solution)/shard_map/ppermute | solution.py:339
  43.9 0.6 collective-permute-start.9
  44.4 1.6 %project_other.4 = bf16[96,3072]{1,0:T(8,128)(2,1)S(1)} custom-call(bf16[96,1536]{1,0:T(8,128)(2,1)S(1)} %shard_map.95.att_ref, bf16[1536,6144]{1,0:T(8,128)(2,1)S(1)} %copy-done), custom_call_target="tpu_custom_call" | custom-call | flops 905969664 | bytes 9437184 | tf_op jit(solution)/shard_map/project_other/pallas_call | solution.py:204
  46.1 0.1 collective-permute-start.14
  46.1 1.6 %collective-permute-start.19 = (bf16[96,1536]{1,0:T(8,128)(2,1)S(1)}, bf16[96,1536]{1,0:T(8,128)(2,1)S(1)}, u32[]{:S(2)}, u32[]{:S(2)}) collective-permute-start(bf16[96,1536]{1,0:T(8,128)(2,1)S(1)} %project_own.3), channel_id=1, source_target_pairs={{0,2},{1,3},{2,0},{3,1},{4,6},{5,7},{6,4},{7,5},{8,10},{9,11},{10,... | collective-permute-start | bytes 884744 | tf_op jit(solution)/shard_map/ppermute | solution.py:339
  47.7 4.7 %collective-permute-done.9 = f32[2,1,1536]{2,1,0:T(1,128)S(1)} collective-permute-done((f32[2,1,1536]{2,1,0:T(1,128)S(1)}, f32[2,1,1536]{2,1,0:T(1,128)S(1)}, u32[]{:S(2)}, u32[]{:S(2)}) %collective-permute-start.9) | collective-permute-done | bytes 12320 | tf_op jit(solution)/shard_map/ppermute | solution.py:339
  52.5 0.1 add_convert_fusion.refs_2_
  52.6 0.1 collective-permute-start.23
  52.7 1.9 %project_own.4 = (bf16[48,3072]{1,0:T(8,128)(2,1)S(1)}, bf16[48,3072]{1,0:T(8,128)(2,1)S(1)}) custom-call(bf16[96,1536]{1,0:T(8,128)(2,1)S(1)} %shard_map.95.att_ref, bf16[1536,6144]{1,0:T(8,128)(2,1)S(1)} %copy-done, bf16[96,3072]{1,0:T(8,128)(2,1)S(1)} %collective-permute-done.14.rest_0_, bf16[192,1536]{1,0:T(8,128)(2,1)S(1)} %copy-done.1), custom_call_target="tpu_custom_call" | custom-call | flops 905969664 | bytes 9437184 | tf_op jit(solution)/shard_map/project_own/pallas_call | solution.py:204
  54.6 1.6 %collective-permute-start.17 = (bf16[48,3072]{1,0:T(8,128)(2,1)S(1)}, bf16[48,3072]{1,0:T(8,128)(2,1)S(1)}, u32[]{:S(2)}, u32[]{:S(2)}) collective-permute-start(bf16[48,3072]{1,0:T(8,128)(2,1)S(1)} %get-tuple-element.20), channel_id=1, source_target_pairs={{0,2},{1,3},{2,0},{3,1},{4,6},{5,7},{6,4},{7,5},{8,10},{9,11},{10,... | collective-permute-start | bytes 884744 | tf_op jit(solution)/shard_map/ppermute | solution.py:339
  56.2 2.6 %collective-permute-done.19 = bf16[96,1536]{1,0:T(8,128)(2,1)S(1)} collective-permute-done((bf16[96,1536]{1,0:T(8,128)(2,1)S(1)}, bf16[96,1536]{1,0:T(8,128)(2,1)S(1)}, u32[]{:S(2)}, u32[]{:S(2)}) %collective-permute-start.19) | collective-permute-done | bytes 294944 | tf_op jit(solution)/shard_map/ppermute | solution.py:339
  58.8 0.1 add_convert_fusion.1.refs_0_
  58.9 0.1 collective-permute-start.20
  59.0 1.6 %collective-permute-start.15 = (bf16[48,3072]{1,0:T(8,128)(2,1)S(1)}, bf16[48,3072]{1,0:T(8,128)(2,1)S(1)}, u32[]{:S(2)}, u32[]{:S(2)}) collective-permute-start(bf16[48,3072]{1,0:T(8,128)(2,1)S(1)} %get-tuple-element.19), channel_id=1, source_target_pairs={{0,2},{1,3},{2,0},{3,1},{4,6},{5,7},{6,4},{7,5},{8,10},{9,11},{10,... | collective-permute-start | bytes 884744 | tf_op jit(solution)/shard_map/ppermute | solution.py:339
  60.5 4.6 %collective-permute-done.17 = bf16[48,3072]{1,0:T(8,128)(2,1)S(1)} collective-permute-done((bf16[48,3072]{1,0:T(8,128)(2,1)S(1)}, bf16[48,3072]{1,0:T(8,128)(2,1)S(1)}, u32[]{:S(2)}, u32[]{:S(2)}) %collective-permute-start.17) | collective-permute-done | bytes 294944 | tf_op jit(solution)/shard_map/ppermute | solution.py:339
  65.1 0.1 add_convert_fusion.2.refs_0_
  65.2 0.1 collective-permute-start.18
  65.3 5.7 %collective-permute-done.15 = bf16[48,3072]{1,0:T(8,128)(2,1)S(1)} collective-permute-done((bf16[48,3072]{1,0:T(8,128)(2,1)S(1)}, bf16[48,3072]{1,0:T(8,128)(2,1)S(1)}, u32[]{:S(2)}, u32[]{:S(2)}) %collective-permute-start.15) | collective-permute-done | bytes 294944 | tf_op jit(solution)/shard_map/ppermute | solution.py:339
  70.9 0.1 add_convert_fusion.3.refs_0_
  71.0 0.1 collective-permute-start.16
  71.1 2.0 %shard_map.96 = (bf16[192,6144]{1,0:T(8,128)(2,1)}, f32[1,192]{1,0:T(1,128)S(1)}, bf16[192,1536]{1,0:T(8,128)(2,1)}) custom-call(f32[4,1,1536]{2,1,0:T(1,128)S(1)} %pad_maximum_fusion.gain_ref, bf16[96,1536]{1,0:T(8,128)(2,1)S(1)} %add_convert_fusion.1.refs_0_, bf16[96,1536]{1,0:T(8,128)(2,1)S(1)} %collective-permute-done.20.refs_1_, ...), custom_call_target="tpu_custom_call" | custom-call | flops 2000000000 | bytes 2359296 | tf_op jit(solution)/shard_map/pallas_call | solution.py:294
  73.1 1.3 %shard_map.97 = (bf16[192,6144]{1,0:T(8,128)(2,1)}, f32[1,192]{1,0:T(1,128)S(1)}, bf16[192,1536]{1,0:T(8,128)(2,1)}) custom-call(f32[4,1,1536]{2,1,0:T(1,128)S(1)} %pad_maximum_fusion.gain_ref, bf16[48,3072]{1,0:T(8,128)(2,1)S(1)} %add_convert_fusion.2.refs_0_, ...), custom_call_target="tpu_custom_call", output_to_operand_aliasing={{0}: (4, {}), {2}: (5, {})} | custom-call | flops 2000000000 | bytes 1179648 | tf_op jit(solution)/shard_map/pallas_call | solution.py:294
  74.5 1.9 %shard_map.98 = (bf16[192,6144]{1,0:T(8,128)(2,1)}, f32[192]{0:T(256)}, bf16[192,1536]{1,0:T(8,128)(2,1)}) custom-call(f32[4,1,1536]{2,1,0:T(1,128)S(1)} %pad_maximum_fusion.gain_ref, bf16[48,3072]{1,0:T(8,128)(2,1)S(1)} %add_convert_fusion.3.refs_0_, ...), custom_call_target="tpu_custom_call", output_to_operand_aliasing={{0}: (4, {}), {2}: (5, {})} | custom-call | flops 2000000000 | bytes 1179648 | tf_op jit(solution)/shard_map/pallas_call | solution.py:294
  (28 shorter events, 0.1 us)
Async XLA Ops:
  0.6 29.3 %copy-start.2 = (bf16[192,1536]{1,0:T(8,128)(2,1)S(1)}, bf16[192,1536]{1,0:T(8,128)(2,1)}, u32[]{:S(2)}) copy-start(bf16[192,1536]{1,0:T(8,128)(2,1)} %refs_0_.3) | copy-start | bytes 1769476
  0.6 31.6 %copy-start = (bf16[1536,6144]{1,0:T(8,128)(2,1)S(1)}, bf16[1536,6144]{1,0:T(8,128)(2,1)}, u32[]{:S(2)}) copy-start(bf16[1536,6144]{1,0:T(8,128)(2,1)} %weight_ref.11) | copy-start | bytes 56623108
  1.7 7.2 %collective-permute-start.3 = (bf16[104,512]{1,0:T(8,128)(2,1)S(1)}, bf16[104,512]{1,0:T(8,128)(2,1)S(1)}, u32[]{:S(2)}, u32[]{:S(2)}) collective-permute-start(bf16[104,512]{1,0:T(8,128)(2,1)S(1)} %get-tuple-element.15.refs_1_), channel_id=1, source_target_pairs={{0,8},{4,12},{8,0},{12,4},{16,24},{20,28},{24,16},{28,20},{1,9},{5... | collective-permute-start | bytes 319496 | tf_op jit(solution)/shard_map/ppermute | solution.py:333
  4.8 4.7 %collective-permute-start.10 = (bf16[104,512]{1,0:T(8,128)(2,1)S(1)}, bf16[104,512]{1,0:T(8,128)(2,1)S(1)}, u32[]{:S(2)}, u32[]{:S(2)}) collective-permute-start(bf16[104,512]{1,0:T(8,128)(2,1)S(1)} %get-tuple-element.18.refs_0_), channel_id=1, source_target_pairs={{0,4},{4,0},{8,12},{12,8},{16,20},{20,16},{24,28},{28,24},{1,5},{5... | collective-permute-start | bytes 319496 | tf_op jit(solution)/shard_map/ppermute | solution.py:336
  6.3 12.7 %collective-permute-start.1 = (bf16[104,512]{1,0:T(8,128)(2,1)S(1)}, bf16[104,512]{1,0:T(8,128)(2,1)S(1)}, u32[]{:S(2)}, u32[]{:S(2)}) collective-permute-start(bf16[104,512]{1,0:T(8,128)(2,1)S(1)} %get-tuple-element.15.refs_1_), channel_id=1, source_target_pairs={{0,16},{4,20},{8,24},{12,28},{16,0},{20,4},{24,8},{28,12},{1,17},{... | collective-permute-start | bytes 319496 | tf_op jit(solution)/shard_map/ppermute | solution.py:333
  9.6 16.8 %collective-permute-start.11 = (bf16[208,512]{1,0:T(8,128)(2,1)S(1)}, bf16[208,512]{1,0:T(8,128)(2,1)S(1)}, u32[]{:S(2)}, u32[]{:S(2)}) collective-permute-start(bf16[208,512]{1,0:T(8,128)(2,1)S(1)} %join.1.refs_9_), channel_id=1, source_target_pairs={{0,16},{4,20},{8,24},{12,28},{16,0},{20,4},{24,8},{28,12},{1,17},{... | collective-permute-start | bytes 638984 | tf_op jit(solution)/shard_map/ppermute | solution.py:333
  19.0 6.0 %collective-permute-start.5 = (bf16[104,512]{1,0:T(8,128)(2,1)S(1)}, bf16[104,512]{1,0:T(8,128)(2,1)S(1)}, u32[]{:S(2)}, u32[]{:S(2)}) collective-permute-start(bf16[104,512]{1,0:T(8,128)(2,1)S(1)} %collective-permute-done.1.refs_3_), channel_id=1, source_target_pairs={{0,8},{4,12},{8,0},{12,4},{16,24},{20,28},{24,16},{28,20},{1,9},{5... | collective-permute-start | bytes 319496 | tf_op jit(solution)/shard_map/ppermute | solution.py:333
  19.0 6.0 %collective-permute-start = (bf16[104,512]{1,0:T(8,128)(2,1)S(1)}, bf16[104,512]{1,0:T(8,128)(2,1)S(1)}, u32[]{:S(2)}, u32[]{:S(2)}) collective-permute-start(bf16[104,512]{1,0:T(8,128)(2,1)S(1)} %get-tuple-element.15.refs_1_), channel_id=1, source_target_pairs={{0,4},{4,0},{8,12},{12,8},{16,20},{20,16},{24,28},{28,24},{1,5},{5... | collective-permute-start | bytes 319496 | tf_op jit(solution)/shard_map/ppermute | solution.py:336
  19.0 8.0 %collective-permute-start.2 = (bf16[104,512]{1,0:T(8,128)(2,1)S(1)}, bf16[104,512]{1,0:T(8,128)(2,1)S(1)}, u32[]{:S(2)}, u32[]{:S(2)}) collective-permute-start(bf16[104,512]{1,0:T(8,128)(2,1)S(1)} %collective-permute-done.1.refs_3_), channel_id=1, source_target_pairs={{0,4},{4,0},{8,12},{12,8},{16,20},{20,16},{24,28},{28,24},{1,5},{5... | collective-permute-start | bytes 319496 | tf_op jit(solution)/shard_map/ppermute | solution.py:336
  21.0 6.0 %collective-permute-start.4 = (bf16[104,512]{1,0:T(8,128)(2,1)S(1)}, bf16[104,512]{1,0:T(8,128)(2,1)S(1)}, u32[]{:S(2)}, u32[]{:S(2)}) collective-permute-start(bf16[104,512]{1,0:T(8,128)(2,1)S(1)} %collective-permute-done.3.refs_5_), channel_id=1, source_target_pairs={{0,4},{4,0},{8,12},{12,8},{16,20},{20,16},{24,28},{28,24},{1,5},{5... | collective-permute-start | bytes 319496 | tf_op jit(solution)/shard_map/ppermute | solution.py:336
  25.0 4.9 %collective-permute-start.6 = (bf16[104,512]{1,0:T(8,128)(2,1)S(1)}, bf16[104,512]{1,0:T(8,128)(2,1)S(1)}, u32[]{:S(2)}, u32[]{:S(2)}) collective-permute-start(bf16[104,512]{1,0:T(8,128)(2,1)S(1)} %collective-permute-done.5.refs_7_), channel_id=1, source_target_pairs={{0,4},{4,0},{8,12},{12,8},{16,20},{20,16},{24,28},{28,24},{1,5},{5... | collective-permute-start | bytes 319496 | tf_op jit(solution)/shard_map/ppermute | solution.py:336
  25.0 9.6 %collective-permute-start.12 = (bf16[208,512]{1,0:T(8,128)(2,1)S(1)}, bf16[208,512]{1,0:T(8,128)(2,1)S(1)}, u32[]{:S(2)}, u32[]{:S(2)}) collective-permute-start(bf16[208,512]{1,0:T(8,128)(2,1)S(1)} %join.1.refs_9_), channel_id=1, source_target_pairs={{0,8},{4,12},{8,0},{12,4},{16,24},{20,28},{24,16},{28,20},{1,9},{5... | collective-permute-start | bytes 638984 | tf_op jit(solution)/shard_map/ppermute | solution.py:333
  26.3 10.4 %collective-permute-start.13 = (bf16[208,512]{1,0:T(8,128)(2,1)S(1)}, bf16[208,512]{1,0:T(8,128)(2,1)S(1)}, u32[]{:S(2)}, u32[]{:S(2)}) collective-permute-start(bf16[208,512]{1,0:T(8,128)(2,1)S(1)} %collective-permute-done.11.refs_10_), channel_id=1, source_target_pairs={{0,8},{4,12},{8,0},{12,4},{16,24},{20,28},{24,16},{28,20},{1,9},{5... | collective-permute-start | bytes 638984 | tf_op jit(solution)/shard_map/ppermute | solution.py:333
  33.1 7.1 %collective-permute-start.7 = (bf16[96,1536]{1,0:T(8,128)(2,1)S(1)}, bf16[96,1536]{1,0:T(8,128)(2,1)S(1)}, u32[]{:S(2)}, u32[]{:S(2)}) collective-permute-start(bf16[96,1536]{1,0:T(8,128)(2,1)S(1)} %project_other.3), channel_id=1, source_target_pairs={{0,1},{1,0},{2,3},{3,2},{4,5},{5,4},{6,7},{7,6},{8,9},{9,8},{10,11... | collective-permute-start | bytes 884744 | tf_op jit(solution)/shard_map/ppermute | solution.py:342
  34.1 6.1 %copy-start.1 = (bf16[192,1536]{1,0:T(8,128)(2,1)S(1)}, bf16[192,1536]{1,0:T(8,128)(2,1)}, u32[]{:S(2)}) copy-start(bf16[192,1536]{1,0:T(8,128)(2,1)} %rest_1_.5) | copy-start | bytes 1769476
  34.1 7.2 %collective-permute-start.21 = (bf16[96,1536]{1,0:T(8,128)(2,1)S(1)}, bf16[96,1536]{1,0:T(8,128)(2,1)S(1)}, u32[]{:S(2)}, u32[]{:S(2)}) collective-permute-start(bf16[96,1536]{1,0:T(8,128)(2,1)S(1)} %project_other.5), channel_id=1, source_target_pairs={{0,1},{1,0},{2,3},{3,2},{4,5},{5,4},{6,7},{7,6},{8,9},{9,8},{10,11... | collective-permute-start | bytes 884744 | tf_op jit(solution)/shard_map/ppermute | solution.py:342
  40.2 1.0 %copy-start.3 = (f32[1,1536]{1,0:T(1,128)S(1)}, f32[1,1536]{1,0:T(1,128)}, u32[]{:S(2)}) copy-start(f32[1,1536]{1,0:T(1,128)} %param.12) | copy-start | bytes 18436
  41.2 2.6 %collective-permute-start.8 = (f32[1,1536]{1,0:T(1,128)S(1)}, f32[1,1536]{1,0:T(1,128)S(1)}, u32[]{:S(2)}, u32[]{:S(2)}) collective-permute-start(f32[1,1536]{1,0:T(1,128)S(1)} %copy-done.3), channel_id=1, source_target_pairs={{0,1},{1,0},{2,3},{3,2},{4,5},{5,4},{6,7},{7,6},{8,9},{9,8},{10,11... | collective-permute-start | bytes 18440 | tf_op jit(solution)/shard_map/ppermute | solution.py:342
  42.3 10.2 %collective-permute-start.22 = (bf16[96,1536]{1,0:T(8,128)(2,1)S(1)}, bf16[96,1536]{1,0:T(8,128)(2,1)S(1)}, u32[]{:S(2)}, u32[]{:S(2)}) collective-permute-start(bf16[96,1536]{1,0:T(8,128)(2,1)S(1)} %project_own.5), channel_id=1, source_target_pairs={{0,2},{1,3},{2,0},{3,1},{4,6},{5,7},{6,4},{7,5},{8,10},{9,11},{10,... | collective-permute-start | bytes 884744 | tf_op jit(solution)/shard_map/ppermute | solution.py:339
  43.9 8.6 %collective-permute-start.9 = (f32[2,1,1536]{2,1,0:T(1,128)S(1)}, f32[2,1,1536]{2,1,0:T(1,128)S(1)}, u32[]{:S(2)}, u32[]{:S(2)}) collective-permute-start(f32[2,1,1536]{2,1,0:T(1,128)S(1)} %pad_maximum_fusion.1), channel_id=1, source_target_pairs={{0,2},{1,3},{2,0},{3,1},{4,6},{5,7},{6,4},{7,5},{8,10},{9,11},{10,... | collective-permute-start | bytes 36872 | tf_op jit(solution)/shard_map/ppermute | solution.py:339
  46.1 6.6 %collective-permute-start.14 = (bf16[96,3072]{1,0:T(8,128)(2,1)S(1)}, bf16[96,3072]{1,0:T(8,128)(2,1)S(1)}, u32[]{:S(2)}, u32[]{:S(2)}) collective-permute-start(bf16[96,3072]{1,0:T(8,128)(2,1)S(1)} %project_other.4), channel_id=1, source_target_pairs={{0,1},{1,0},{2,3},{3,2},{4,5},{5,4},{6,7},{7,6},{8,9},{9,8},{10,11... | collective-permute-start | bytes 1769480 | tf_op jit(solution)/shard_map/ppermute | solution.py:342
  46.1 12.6 %collective-permute-start.19 = (bf16[96,1536]{1,0:T(8,128)(2,1)S(1)}, bf16[96,1536]{1,0:T(8,128)(2,1)S(1)}, u32[]{:S(2)}, u32[]{:S(2)}) collective-permute-start(bf16[96,1536]{1,0:T(8,128)(2,1)S(1)} %project_own.3), channel_id=1, source_target_pairs={{0,2},{1,3},{2,0},{3,1},{4,6},{5,7},{6,4},{7,5},{8,10},{9,11},{10,... | collective-permute-start | bytes 884744 | tf_op jit(solution)/shard_map/ppermute | solution.py:339
  52.6 18.5 %collective-permute-start.23 = (bf16[96,1536]{1,0:T(8,128)(2,1)S(1)}, bf16[96,1536]{1,0:T(8,128)(2,1)S(1)}, u32[]{:S(2)}, u32[]{:S(2)}) collective-permute-start(bf16[96,1536]{1,0:T(8,128)(2,1)S(1)} %add_convert_fusion.refs_2_), channel_id=1, source_target_pairs={{0,1},{1,0},{2,3},{3,2},{4,5},{5,4},{6,7},{7,6},{8,9},{9,8},{10,11... | collective-permute-start | bytes 884744 | tf_op jit(solution)/shard_map/ppermute | solution.py:342
  54.6 10.5 %collective-permute-start.17 = (bf16[48,3072]{1,0:T(8,128)(2,1)S(1)}, bf16[48,3072]{1,0:T(8,128)(2,1)S(1)}, u32[]{:S(2)}, u32[]{:S(2)}) collective-permute-start(bf16[48,3072]{1,0:T(8,128)(2,1)S(1)} %get-tuple-element.20), channel_id=1, source_target_pairs={{0,2},{1,3},{2,0},{3,1},{4,6},{5,7},{6,4},{7,5},{8,10},{9,11},{10,... | collective-permute-start | bytes 884744 | tf_op jit(solution)/shard_map/ppermute | solution.py:339
  58.9 12.2 %collective-permute-start.20 = (bf16[96,1536]{1,0:T(8,128)(2,1)S(1)}, bf16[96,1536]{1,0:T(8,128)(2,1)S(1)}, u32[]{:S(2)}, u32[]{:S(2)}) collective-permute-start(bf16[96,1536]{1,0:T(8,128)(2,1)S(1)} %add_convert_fusion.1.refs_0_), channel_id=1, source_target_pairs={{0,1},{1,0},{2,3},{3,2},{4,5},{5,4},{6,7},{7,6},{8,9},{9,8},{10,11... | collective-permute-start | bytes 884744 | tf_op jit(solution)/shard_map/ppermute | solution.py:342
  59.0 12.0 %collective-permute-start.15 = (bf16[48,3072]{1,0:T(8,128)(2,1)S(1)}, bf16[48,3072]{1,0:T(8,128)(2,1)S(1)}, u32[]{:S(2)}, u32[]{:S(2)}) collective-permute-start(bf16[48,3072]{1,0:T(8,128)(2,1)S(1)} %get-tuple-element.19), channel_id=1, source_target_pairs={{0,2},{1,3},{2,0},{3,1},{4,6},{5,7},{6,4},{7,5},{8,10},{9,11},{10,... | collective-permute-start | bytes 884744 | tf_op jit(solution)/shard_map/ppermute | solution.py:339
  65.2 7.9 %collective-permute-start.18 = (bf16[48,3072]{1,0:T(8,128)(2,1)S(1)}, bf16[48,3072]{1,0:T(8,128)(2,1)S(1)}, u32[]{:S(2)}, u32[]{:S(2)}) collective-permute-start(bf16[48,3072]{1,0:T(8,128)(2,1)S(1)} %add_convert_fusion.2.refs_0_), channel_id=1, source_target_pairs={{0,1},{1,0},{2,3},{3,2},{4,5},{5,4},{6,7},{7,6},{8,9},{9,8},{10,11... | collective-permute-start | bytes 884744 | tf_op jit(solution)/shard_map/ppermute | solution.py:342
  71.0 3.4 %collective-permute-start.16 = (bf16[48,3072]{1,0:T(8,128)(2,1)S(1)}, bf16[48,3072]{1,0:T(8,128)(2,1)S(1)}, u32[]{:S(2)}, u32[]{:S(2)}) collective-permute-start(bf16[48,3072]{1,0:T(8,128)(2,1)S(1)} %add_convert_fusion.3.refs_0_), channel_id=1, source_target_pairs={{0,1},{1,0},{2,3},{3,2},{4,5},{5,4},{6,7},{7,6},{8,9},{9,8},{10,11... | collective-permute-start | bytes 884744 | tf_op jit(solution)/shard_map/ppermute | solution.py:342

commit v2 on v1

v2 whole, which is shorter than its diff:
```python
import functools
import math

import jax
import jax.numpy as jnp
from jax import lax
from jax.experimental import pallas as pl
from jax.experimental.pallas import tpu as pltpu
from jax.sharding import PartitionSpec as P


HEAD = 128
TAG_ROWS = 8
HIDE = -1e30
CUTS = (1, 1)
VMEM = pltpu.VMEM
F32 = jnp.float32
BF16 = jnp.bfloat16


def in_vmem():
    return pl.BlockSpec(memory_space=VMEM)


def in_place():
    return pl.BlockSpec(memory_space=pl.ANY)


def near(array):
    return pltpu.with_memory_space_constraint(array, VMEM)


def far(array):
    return pltpu.with_memory_space_constraint(array, pltpu.HBM)


def after(array, *others):
    return lax.optimization_barrier((array, *others))[0]


def cost(flops, moved):
    return pl.CostEstimate(flops=int(flops), bytes_accessed=int(moved), transcendentals=0)


def grant(mib):
    return pltpu.CompilerParams(vmem_limit_bytes=mib << 20)


def pack_body(run_rows, pos_ref, key_ref, value_ref, low_ref, high_ref, number_ref, sems):
    width = key_ref.shape[1]
    copies = [pltpu.make_async_copy(pos_ref, number_ref, sems.at[4])]
    for half, out in enumerate((low_ref, high_ref)):
        rows = pl.ds(half * run_rows, run_rows)
        for i, ref in enumerate((key_ref, value_ref)):
            target = out.at[pl.ds(0, run_rows), pl.ds(i * width, width)]
            copies.append(pltpu.make_async_copy(ref.at[rows, :], target, sems.at[2 * half + i]))
    for copy in copies:
        copy.start()
    copies[0].wait()
    run = (number_ref[0] // run_rows).astype(F32)
    for out in (low_ref, high_ref):
        out[run_rows:, :] = jnp.full((TAG_ROWS, 2 * width), run, F32).astype(BF16)
    for copy in copies[1:]:
        copy.wait()


def pack(positions, keys, values):
    run_rows = keys.shape[0] // 2
    shape = (run_rows + TAG_ROWS, 2 * keys.shape[1])
    return pl.pallas_call(
        functools.partial(pack_body, run_rows),
        out_shape=(VMEM(shape, BF16), VMEM(shape, BF16)),
        in_specs=[in_place()] * 3,
        out_specs=(in_vmem(), in_vmem()),
        scratch_shapes=[pltpu.SMEM(positions.shape, jnp.int32), pltpu.SemaphoreType.DMA((5,))],
        compiler_params=grant(4),
        cost_estimate=cost(4e10, 4 * keys.size * 2),
        name="pack",
    )(far(positions), far(keys), far(values))


def join_body(*refs):
    rows = refs[0].shape[0]
    for i, ref in enumerate(refs[:-1]):
        refs[-1][i * rows : (i + 1) * rows, :] = ref[...]


def join(pieces):
    rows, width = pieces[0].shape
    return pl.pallas_call(
        join_body,
        out_shape=VMEM((len(pieces) * rows, width), BF16),
        in_specs=[in_vmem()] * len(pieces),
        out_specs=in_vmem(),
        compiler_params=grant(4),
        cost_estimate=cost(2e8, 4 * len(pieces) * rows * width),
        name="join",
    )(*[near(piece) for piece in pieces])


def attend_body(run_rows, query_half, key_halves, begun, final, *refs):
    query_ref, own_ref = refs[:2]
    pieces = refs[2 : 2 + len(key_halves)]
    refs = refs[2 + len(key_halves) :]
    if begun:
        mixed_ref, top_ref, sum_ref = refs[:3]
        refs = refs[3:]
    if final:
        out_ref, kv_ref = refs
    else:
        mixed_out, top_out, sum_out, kv_ref = refs
    block_rows = run_rows + TAG_ROWS
    held = [
        (piece, row, half)
        for piece, half in zip(pieces, key_halves)
        for row in range(0, piece.shape[0], block_rows)
    ]
    kv_width = pieces[0].shape[1] // 2
    kv_heads = kv_width // HEAD
    group = query_ref.shape[1] // kv_width
    lanes = group * run_rows
    step = (1.0 / math.sqrt(HEAD)) * math.log2(math.e)
    query_rows = pl.ds(query_half * run_rows, run_rows)
    own_at = None if begun else next(i for i, (_, _, half) in enumerate(held) if half == query_half)

    own = own_ref[run_rows:block_rows, :HEAD].astype(F32)[:1, :]
    hidden = []
    for number, (piece, row, half) in enumerate(held):
        kv_ref[pl.ds(number * run_rows, run_rows), :] = piece[row : row + run_rows, :]
        if query_half == 1 and half == 0:
            hidden.append(None)
        elif number == own_at:
            key = lax.broadcasted_iota(jnp.int32, (run_rows, lanes), 0)
            query = lax.broadcasted_iota(jnp.int32, (run_rows, lanes), 1)
            query = query - sum((query >= h * run_rows).astype(jnp.int32) for h in range(1, group)) * run_rows
            hidden.append(jnp.where(key <= query, 0.0, HIDE))
        else:
            tag = piece[row + run_rows : row + block_rows, :HEAD].astype(F32)[:1, :]
            seen = tag < own if half == 0 else tag > own
            line = jnp.where(seen, 0.0, HIDE)
            hidden.append(jnp.concatenate([line] * -(-lanes // HEAD), axis=1)[:, :lanes])

    for kv_head in range(kv_heads):
        keys = kv_ref[:, kv_head * HEAD : (kv_head + 1) * HEAD]
        values = kv_ref[:, kv_width + kv_head * HEAD : kv_width + (kv_head + 1) * HEAD]
        heads = [kv_head * group + i for i in range(group)]
        query = jnp.concatenate([query_ref[query_rows, h * HEAD : (h + 1) * HEAD] for h in heads], axis=0)
        scores = lax.dot_general(keys, query, (((1,), (1,)), ((), ())), preferred_element_type=F32)
        parts = []
        for number in range(len(held)):
            part = scores[number * run_rows : (number + 1) * run_rows] * step
            parts.append(part if hidden[number] is None else part + hidden[number])
        top = functools.reduce(jnp.maximum, [jnp.max(part, axis=0, keepdims=True) for part in parts])
        if begun:
            top = jnp.maximum(top, top_ref[kv_head])
        parts = [jnp.exp2(part - top) for part in parts]
        amount = sum(jnp.sum(part, axis=0, keepdims=True) for part in parts)
        weights = jnp.concatenate([part.astype(BF16) for part in parts], axis=0)
        mixed = lax.dot_general(values, weights, (((0,), (0,)), ((), ())), preferred_element_type=F32)
        rows = slice(kv_head * HEAD, (kv_head + 1) * HEAD)
        if begun:
            factor = jnp.exp2(top_ref[kv_head] - top)
            mixed = mixed + mixed_ref[rows, :] * factor
            amount = amount + sum_ref[kv_head] * factor
        if final:
            mean = (mixed / amount).T.astype(BF16)
            for i, h in enumerate(heads):
                out_ref[:, h * HEAD : (h + 1) * HEAD] = mean[i * run_rows : (i + 1) * run_rows, :]
        else:
            mixed_out[rows, :] = mixed
            top_out[kv_head] = top
            sum_out[kv_head] = amount


def attend(queries, query_half, own, piece_sets, begun=None, final=True):
    run_rows = queries.shape[0] // 2
    key_halves = [half for half, pieces in enumerate(piece_sets) for piece in pieces]
    pieces = [piece for pieces in piece_sets for piece in pieces]
    total = sum(piece.shape[0] for piece in pieces) // (run_rows + TAG_ROWS) * run_rows
    kv_width = pieces[0].shape[1] // 2
    width = queries.shape[1]
    lanes = width // kv_width * run_rows
    line = VMEM((kv_width // HEAD, 1, lanes), F32)
    state = (VMEM((kv_width, lanes), F32), line, line)
    operands = [queries, own, *pieces, *(begun or [])]
    return pl.pallas_call(
        functools.partial(attend_body, run_rows, query_half, key_halves, begun is not None, final),
        out_shape=VMEM((run_rows, width), BF16) if final else state,
        in_specs=[in_vmem()] * len(operands),
        out_specs=in_vmem() if final else (in_vmem(),) * 3,
        scratch_shapes=[VMEM((total, 2 * kv_width), BF16)],
        compiler_params=grant(20),
        cost_estimate=cost(4 * run_rows * total * width, total * pieces[0].shape[1] * 2),
    )(*[near(operand) for operand in operands])


def project_body(cores, blocks, half, own, att_ref, weight_ref, *rest):
    outs = rest[2:] if own else rest
    width = outs[0].shape[1] // len(blocks)
    tp = lax.axis_index("tp")
    for i, yb in enumerate(blocks):
        block = yb * cores + ((tp % cores) ^ (0 if own else 1))
        start = pl.multiple_of(block * width, HEAD)
        total = jnp.dot(att_ref[...], weight_ref[:, pl.ds(start, width)], preferred_element_type=F32)
        columns = slice(i * width, (i + 1) * width)
        if own:
            arrived, residual = rest[0], rest[1]
            mine = jnp.where(tp // cores == yb, 1.0, 0.0).astype(F32)
            total = total.astype(BF16).astype(F32) + arrived[:, columns].astype(F32)
            rows = pl.ds(half * arrived.shape[0], arrived.shape[0])
            total = total + mine * residual[rows, :].astype(F32)
        total = total.astype(BF16)
        row = 0
        for out in outs:
            out[:, columns] = total[row : row + out.shape[0]]
            row += out.shape[0]


def project(cores, blocks, half, attended, weight, block_width, cuts=(1,), arrived=None, residual=None):
    rows, depth = attended.shape
    width = block_width * len(blocks)
    own = arrived is not None
    operands = [attended, weight] + ([arrived, residual] if own else [])
    result = pl.pallas_call(
        functools.partial(project_body, cores, blocks, half, own),
        out_shape=tuple(VMEM((rows * cut // sum(cuts), width), BF16) for cut in cuts),
        in_specs=[in_vmem()] * len(operands),
        out_specs=(in_vmem(),) * len(cuts),
        compiler_params=grant(8),
        cost_estimate=cost(2 * rows * depth * width, depth * width * 2),
        name="project_own" if own else "project_other",
    )(*[near(operand) for operand in operands])
    return result if own else result[0]


def finish_body(ny, cores, row, rows, places, count, last, *refs):
    blocks = ny * cores
    gains, refs = refs[:blocks], refs[blocks:]
    parts = refs[:count]
    line_ref = refs[count]
    quant_ref, line_out, stream_ref, quant_vmem, stream_vmem, line_vmem, sems = refs[-7:]
    width = parts[0].shape[1]
    tp = lax.axis_index("tp")
    y, core = tp // cores, tp % cores

    def part(yb, k):
        number, first = places[yb, k]
        return parts[number][first : first + rows, :].astype(F32)

    def gain(yb, k):
        chosen = gains[k][...]
        for distance in range(1, ny):
            chosen = jnp.where((y ^ yb) == distance, gains[distance * cores + k][...], chosen)
        return chosen

    stream = part(0, 0)
    for yb in range(1, ny):
        stream = jnp.where(y == yb, part(yb, 0), stream)
    stream_vmem[...] = stream.astype(BF16)
    copies = [pltpu.make_async_copy(stream_vmem, stream_ref.at[pl.ds(row, rows), :], sems.at[blocks])]
    copies[0].start()
    totals = {}
    for yb in range(ny):
        for k in range(cores):
            value = part(yb, k)
            totals[yb, k] = jnp.sum(value * value, axis=1, keepdims=True)
    square = jnp.zeros((rows, 1), F32)
    for yb in range(ny):
        for cb in range(cores):
            chosen = totals[yb, 0]
            for k in range(1, cores):
                chosen = jnp.where((core ^ k) == cb, totals[yb, k], chosen)
            square = square + chosen
    root = lax.rsqrt(square / (blocks * width) + 1e-05)
    peak = jnp.zeros((rows, 1), F32)
    for yb in range(ny):
        for k in range(cores):
            value = part(yb, k) * gain(yb, k)
            peak = jnp.maximum(peak, jnp.max(jnp.abs(value), axis=1, keepdims=True))
    peak = peak * root + 1e-06
    factor = root / peak
    lanes = line_ref.shape[-1]
    lane = lax.broadcasted_iota(jnp.int32, (rows, lanes), 1)
    here = lax.broadcasted_iota(jnp.int32, (rows, lanes), 0) + row == lane
    line = jnp.sum(jnp.where(here, peak, 0.0), axis=0, keepdims=True)
    if row:
        line = line + line_ref[...]
    if last:
        line_vmem[...] = line.reshape(line_vmem.shape)
        copies.append(pltpu.make_async_copy(line_vmem, line_out, sems.at[blocks + 1]))
        copies[-1].start()
    else:
        line_out[...] = line
    for yb in range(ny):
        for k in range(cores):
            value = part(yb, k) * gain(yb, k) * factor
            slot = yb * cores + k
            start = pl.multiple_of((yb * cores + (core ^ k)) * width, HEAD)
            quant_vmem[slot] = value.astype(BF16)
            target = quant_ref.at[pl.ds(row, rows), pl.ds(start, width)]
            copies.append(pltpu.make_async_copy(quant_vmem.at[slot], target, sems.at[slot]))
            copies[-1].start()
    for copy in copies:
        copy.wait()


def finish(ny, cores, row, rows, all_rows, gains, parts, places, earlier):
    width = parts[0].shape[1]
    blocks = ny * cores
    last = row + rows == all_rows
    operands = [near(operand) for operand in (*gains, *parts)]
    out_shape = (
        jax.ShapeDtypeStruct((all_rows, blocks * width), BF16),
        jax.ShapeDtypeStruct((all_rows,), F32) if last else VMEM((1, all_rows), F32),
        jax.ShapeDtypeStruct((all_rows, width), BF16),
    )
    aliases = {}
    if earlier is not None:
        aliases = {len(operands) + 1: 0, len(operands) + 2: 2}
        operands += [near(earlier[1]), earlier[0], earlier[2]]
    else:
        operands += [near(jnp.zeros((1, all_rows), F32))]
    n = 1 + blocks + len(parts)
    return pl.pallas_call(
        functools.partial(finish_body, ny, cores, row, rows, places, len(parts), last),
        out_shape=out_shape,
        in_specs=[in_vmem()] * n + [in_place()] * (len(operands) - n),
        out_specs=(in_place(), in_place() if last else in_vmem(), in_place()),
        scratch_shapes=[
            VMEM((blocks, rows, width), BF16),
            VMEM((rows, width), BF16),
            VMEM((all_rows,), F32),
            pltpu.SemaphoreType.DMA((blocks + 2,)),
        ],
        input_output_aliases=aliases,
        compiler_params=grant(8),
        cost_estimate=cost(2e9, 4 * rows * blocks * width),
    )(*operands)


def swap(size, count, stride, distance):
    def partner(index):
        digit = (index // stride) % size
        return index + ((digit ^ distance) - digit) * stride

    return [(index, partner(index)) for index in range(count)]


def tree_sum(terms):
    terms = [term.astype(F32) for term in terms]
    while len(terms) > 1:
        terms = [terms[i] + terms[i + 1] for i in range(0, len(terms), 2)]
    return terms[0].astype(BF16)


def on_device(sizes, queries, keys, values, positions, residual, norm_gain, out_weight):
    nz, nx, ny, cores = sizes
    n_seq, n_tp = nz * nx, ny * cores
    all_rows, block_width = residual.shape
    run_rows = all_rows // 2

    def move_z(array, k):
        return lax.ppermute(array, "seq", swap(nz, n_seq, nx, k))

    def move_x(array, k):
        return lax.ppermute(array, "seq", swap(nx, n_seq, 1, k))

    def move_y(array, k):
        return lax.ppermute(array, "tp", swap(ny, n_tp, cores, k))

    def move_core(array, k):
        return lax.ppermute(array, "tp", swap(cores, n_tp, 1, k))

    low, high = pack(positions, keys, values)
    low_pieces = [low] + [move_x(low, j) for j in range(1, nx)]

    distances = [nz - 1] + [k for k in (1, *range(nz - 2, 1, -1)) if k < nz - 1]
    column = {k: move_z(low, k) for k in distances}
    for k in distances:
        low_pieces += [column[k]] + [move_x(column[k], j) for j in range(1, nx)]

    high_line = [high] + [move_x(high, j) for j in range(1, nx)]
    high_line = join([after(high_line[0], column[distances[0]]), *high_line[1:]])
    step, high_pieces = nz // 2, [high_line]
    firsts = {k: move_z(high_line, k) for k in dict.fromkeys((step, 1)) if k}
    while step:
        for held in list(high_pieces):
            if held is high_line and step in firsts:
                high_pieces.append(firsts[step])
            else:
                high_pieces.append(move_z(held, step))
        step //= 2

    begun = attend(queries, 0, low, [low_pieces[:-nx]], None, False)
    early = attend(queries, 0, low, [low_pieces[-nx:]], begun)
    sent, parts = [], []
    for yb in range(ny):
        other = project(cores, [yb], 0, early, out_weight, block_width)
        sent.append(move_core(other, 1))
    for yb in range(ny):
        own = project(cores, [yb], 0, early, out_weight, block_width, (1,), sent[yb], residual)[0]
        total = tree_sum([own] + [move_y(own, k) for k in range(1, ny)])
        parts += [total, move_core(total, 1)]
    gains = [norm_gain] + [move_y(norm_gain, k) for k in range(1, ny)]
    gains = [gain if j == 0 else move_core(gain, j) for gain in gains for j in range(cores)]
    places = {(yb, k): (yb * cores + k, 0) for yb in range(ny) for k in range(cores)}
    result = finish(ny, cores, 0, run_rows, all_rows, gains, parts, places, None)

    begun = attend(queries, 1, low, [low_pieces, high_pieces[:-1]], None, False)
    late = attend(queries, 1, low, [[], high_pieces[-1:]], begun)
    sent, parts = [], []
    for yb in range(ny):
        other = project(cores, [yb], 1, late, out_weight, block_width)
        sent.append(move_core(other, 1))
    for yb in range(ny):
        cuts = CUTS if yb == ny - 1 else (1,)
        owns = project(cores, [yb], 1, late, out_weight, block_width, cuts, sent[yb], residual)
        for own in owns:
            total = tree_sum([own] + [move_y(own, k) for k in range(1, ny)])
            parts += [total, move_core(total, 1)]
    row, blocks = 0, (ny - 1) * cores
    for i, share in enumerate(CUTS):
        rows = run_rows * share // sum(CUTS)
        places = {(yb, k): (yb * cores + k, row) for yb in range(ny - 1) for k in range(cores)}
        places.update({(ny - 1, k): (blocks + k, 0) for k in range(cores)})
        chosen = parts[:blocks] + parts[blocks + i * cores : blocks + (i + 1) * cores]
        result = finish(ny, cores, run_rows + row, rows, all_rows, gains, chosen, places, result)
        row += rows
    quantized, scale, stream = result
    return (quantized, scale, stream)


def sizes_of(mesh):
    along_seq, along_tp = list(mesh.devices[:, 0]), list(mesh.devices[0, :])
    nx = len({device.coords[0] for device in along_seq})
    ny = len({device.coords[1] for device in along_tp})
    return (len(along_seq) // nx, nx, ny, len(along_tp) // ny)


def solution(mesh):
    return jax.shard_map(
        functools.partial(on_device, sizes_of(mesh)),
        mesh=mesh,
        in_specs=(
            P("seq", "tp"),
            P("seq", "tp"),
            P("seq", "tp"),
            P("seq"),
            P("seq", "tp"),
            P(None, "tp"),
            P("tp", None),
        ),
        out_specs=(P("seq", None), P("seq"), P("seq", "tp")),
        check_vma=False,
    )
```

time: 76.6 us -> 83.2 us (1.086)
  starting transfers between devices: 21.9 us -> 26.3 us
  waiting for transfers between devices: 33.9 us -> 35.4 us
    ppermute x5 -> x6, waiting for transfers between devices: 17.6 us -> 21 us  [move_y(): return lax.ppermute(array, 'tp', swap(ny, n_tp, cores, k))]
    ppermute x5, starting transfers between devices: 3.54 us -> 6.71 us  [move_x(): return lax.ppermute(array, 'seq', swap(nx, n_seq, 1, k))]
    ppermute x5, waiting for transfers between devices: 3.48 us -> 1.95 us  [move_x(): return lax.ppermute(array, 'seq', swap(nx, n_seq, 1, k))]
    ppermute x8 -> x11, starting transfers between devices: 1.04 us -> 2.34 us  [move_core(): return lax.ppermute(array, 'tp', swap(cores, n_tp, 1, k))]
    ppermute x6, starting transfers between devices: 10.4 us -> 9.17 us  [move_z(): return lax.ppermute(array, 'seq', swap(nz, n_seq, nx, k))]
    ppermute x5 -> x6, starting transfers between devices: 6.91 us -> 8.13 us  [move_y(): return lax.ppermute(array, 'tp', swap(ny, n_tp, cores, k))]
    pallas_call x5 -> x7, Pallas kernels: 10.9 us -> 11.3 us  [the longest x4 6.68 us: attend(): pl.pallas_call(functools.partial(attend_body, run_rows, query_half, key_h...]
    pallas_call x6 -> x8, Pallas kernels: 7.26 us -> 7.51 us  [project(): pl.pallas_call(functools.partial(project_body, cores, blocks, half, own),...]
  transfers between devices with their start and end apart: 24 -> 28, of which waited for: 9 -> 11; matrix products, arithmetic and copies ran while one was open for 0% -> 0% of each run, Pallas kernels for 21% -> 21%
where the time goes in v2:
time: 83.2 us; the launch traced here: 83.1 us
  waiting for transfers between devices  35.4 us (43%)
  starting transfers between devices  26.3 us (32%)
  Pallas kernels  19.9 us (24%)
  between operations  1.06 us (1%)
    ppermute x6, waiting for transfers between devices, move_y(): return lax.ppermute(array, 'tp', swap(ny, n_tp, cores, k))  21 us
    ppermute x6, waiting for transfers between devices, move_z(): return lax.ppermute(array, 'seq', swap(nz, n_seq, nx, k))  12.4 us
    ppermute x6, starting transfers between devices, move_z(): return lax.ppermute(array, 'seq', swap(nz, n_seq, nx, k))  9.17 us
    ppermute x6, starting transfers between devices, move_y(): return lax.ppermute(array, 'tp', swap(ny, n_tp, cores, k))  8.13 us
    pallas_call x8, Pallas kernels, project(): pl.pallas_call(functools.partial(project_body, cores, blocks, half, own),...  7.51 us
    ppermute x5, starting transfers between devices, move_x(): return lax.ppermute(array, 'seq', swap(nx, n_seq, 1, k))  6.71 us
    pallas_call x4, Pallas kernels, attend(): pl.pallas_call(functools.partial(attend_body, run_rows, query_half, key_h...  6.68 us
    pallas_call x3, Pallas kernels, finish(): pl.pallas_call(functools.partial(finish_body, ny, cores, row, rows, place...  4.64 us
  transfers between devices with their start and end apart: 28, of which 11 were waited for; matrix products, arithmetic and copies ran while one was open for 0% of the time, Pallas kernels for 21%

profile of v2, /device:TPU:0, one launch (start us, length us, event | category | flops | bytes accessed | tf_op | source)
XLA Modules:
  0.0 83.1 jit_solution(15460317002871001837)
XLA Ops:
  0.7 1.1 %pack.1 = (bf16[104,512]{1,0:T(8,128)(2,1)S(1)}, bf16[104,512]{1,0:T(8,128)(2,1)S(1)}) custom-call(s32[192]{0:T(256)} %pos_ref.1, bf16[192,256]{1,0:T(8,128)(2,1)} %key_ref.1, bf16[192,256]{1,0:T(8,128)(2,1)} %value_ref.1), custom_call_target="tpu_custom_call" | custom-call | flops 40000000000 | bytes 393216 | tf_op jit(solution)/shard_map/pack/pallas_call | solution.py:70
  1.7 5.1 %collective-permute-start.3 = (bf16[104,512]{1,0:T(8,128)(2,1)S(1)}, bf16[104,512]{1,0:T(8,128)(2,1)S(1)}, u32[]{:S(2)}, u32[]{:S(2)}) collective-permute-start(bf16[104,512]{1,0:T(8,128)(2,1)S(1)} %get-tuple-element.20.refs_1_.refs_2_), channel_id=1, source_target_pairs={{0,24},{4,28},{8,16},{12,20},{16,8},{20,12},{24,0},{28,4},{1,25},{... | collective-permute-start | bytes 319496 | tf_op jit(solution)/shard_map/ppermute | solution.py:363
  6.9 0.6 collective-permute-start.11
  7.5 1.6 %collective-permute-start.7 = (bf16[104,512]{1,0:T(8,128)(2,1)S(1)}, bf16[104,512]{1,0:T(8,128)(2,1)S(1)}, u32[]{:S(2)}, u32[]{:S(2)}) collective-permute-start(bf16[104,512]{1,0:T(8,128)(2,1)S(1)} %get-tuple-element.20.refs_1_.refs_2_), channel_id=1, source_target_pairs={{0,4},{4,0},{8,12},{12,8},{16,20},{20,16},{24,28},{28,24},{1,5},{5... | collective-permute-start | bytes 319496 | tf_op jit(solution)/shard_map/ppermute | solution.py:366
  9.1 1.6 %collective-permute-done.3.refs_4_ = bf16[104,512]{1,0:T(8,128)(2,1)S(1)} collective-permute-done((bf16[104,512]{1,0:T(8,128)(2,1)S(1)}, bf16[104,512]{1,0:T(8,128)(2,1)S(1)}, u32[]{:S(2)}, u32[]{:S(2)}) %collective-permute-start.3) | collective-permute-done | bytes 106528 | tf_op jit(solution)/shard_map/ppermute | solution.py:363
  10.7 1.7 %collective-permute-start.8 = (bf16[104,512]{1,0:T(8,128)(2,1)S(1)}, bf16[104,512]{1,0:T(8,128)(2,1)S(1)}, u32[]{:S(2)}, u32[]{:S(2)}) collective-permute-start(bf16[104,512]{1,0:T(8,128)(2,1)S(1)} %collective-permute-done.3.refs_4_), channel_id=1, source_target_pairs={{0,4},{4,0},{8,12},{12,8},{16,20},{20,16},{24,28},{28,24},{1,5},{5... | collective-permute-start | bytes 319496 | tf_op jit(solution)/shard_map/ppermute | solution.py:366
  12.4 0.8 collective-permute-done.9.refs_6_
  13.2 1.4 %collective-permute-start.10 = (bf16[104,512]{1,0:T(8,128)(2,1)S(1)}, bf16[104,512]{1,0:T(8,128)(2,1)S(1)}, u32[]{:S(2)}, u32[]{:S(2)}) collective-permute-start(bf16[104,512]{1,0:T(8,128)(2,1)S(1)} %collective-permute-done.9.refs_6_), channel_id=1, source_target_pairs={{0,4},{4,0},{8,12},{12,8},{16,20},{20,16},{24,28},{28,24},{1,5},{5... | collective-permute-start | bytes 319496 | tf_op jit(solution)/shard_map/ppermute | solution.py:366
  14.6 1.2 %collective-permute-done.11.refs_8_.refs_2_ = bf16[104,512]{1,0:T(8,128)(2,1)S(1)} collective-permute-done((bf16[104,512]{1,0:T(8,128)(2,1)S(1)}, bf16[104,512]{1,0:T(8,128)(2,1)S(1)}, u32[]{:S(2)}, u32[]{:S(2)}) %collective-permute-start.11) | collective-permute-done | bytes 106528 | tf_op jit(solution)/shard_map/ppermute | solution.py:363
  15.8 1.5 %collective-permute-start.12 = (bf16[104,512]{1,0:T(8,128)(2,1)S(1)}, bf16[104,512]{1,0:T(8,128)(2,1)S(1)}, u32[]{:S(2)}, u32[]{:S(2)}) collective-permute-start(bf16[104,512]{1,0:T(8,128)(2,1)S(1)} %collective-permute-done.11.refs_8_.refs_2_), channel_id=1, source_target_pairs={{0,4},{4,0},{8,12},{12,8},{16,20},{20,16},{24,28},{28,24},{1,5},{5... | collective-permute-start | bytes 319496 | tf_op jit(solution)/shard_map/ppermute | solution.py:366
  17.3 0.5 collective-permute-start.4
  17.9 0.4 collective-permute-done.10.refs_7_
  18.2 1.5 %shard_map.96 = (f32[256,576]{1,0:T(8,128)S(1)}, f32[2,1,576]{2,1,0:T(1,128)S(1)}, f32[2,1,576]{2,1,0:T(1,128)S(1)}) custom-call(bf16[192,1536]{1,0:T(8,128)(2,1)S(1)} %copy-done.2, bf16[104,512]{1,0:T(8,128)(2,1)S(1)} %get-tuple-element.20.refs_1_.refs_2_, bf16[104,512]{1,0:T(8,128)(2,1)S(1)} %get-tuple-element.20.refs_1_.refs_2_, ...), custom_call_target="tpu_custom_call" | custom-call | flops 339738624 | bytes 589824 | tf_op jit(solution)/shard_map/pallas_call | solution.py:186
  19.8 1.6 %collective-permute-done.12.refs_9_.refs_3_ = bf16[104,512]{1,0:T(8,128)(2,1)S(1)} collective-permute-done((bf16[104,512]{1,0:T(8,128)(2,1)S(1)}, bf16[104,512]{1,0:T(8,128)(2,1)S(1)}, u32[]{:S(2)}, u32[]{:S(2)}) %collective-permute-start.12) | collective-permute-done | bytes 106528 | tf_op jit(solution)/shard_map/ppermute | solution.py:366
  21.3 0.9 %shard_map.97.att_ref = bf16[96,1536]{1,0:T(8,128)(2,1)S(1)} custom-call(bf16[192,1536]{1,0:T(8,128)(2,1)S(1)} %copy-done.2, bf16[104,512]{1,0:T(8,128)(2,1)S(1)} %get-tuple-element.20.refs_1_.refs_2_, bf16[104,512]{1,0:T(8,128)(2,1)S(1)} %collective-permute-done.11.refs_8_.refs_2_, bf16[104,512]{1,0:T(8,128)(2,1)S(1)} %collective-permute-done.12.refs_9_.refs_3_, ...), custom_call_target="tpu_custom_call" | custom-call | flops 113246208 | bytes 196608 | tf_op jit(solution)/shard_map/pallas_call | solution.py:186
  22.3 0.9 %project_other.7 = bf16[96,1536]{1,0:T(8,128)(2,1)S(1)} custom-call(bf16[96,1536]{1,0:T(8,128)(2,1)S(1)} %shard_map.97.att_ref, bf16[1536,6144]{1,0:T(8,128)(2,1)S(1)} %copy-done), custom_call_target="tpu_custom_call" | custom-call | flops 452984832 | bytes 4718592 | tf_op jit(solution)/shard_map/project_other/pallas_call | solution.py:224
  23.3 1.0 %collective-permute-start.5 = (bf16[208,512]{1,0:T(8,128)(2,1)S(1)}, bf16[208,512]{1,0:T(8,128)(2,1)S(1)}, u32[]{:S(2)}, u32[]{:S(2)}) collective-permute-start(bf16[208,512]{1,0:T(8,128)(2,1)S(1)} %join.1.refs_10_), channel_id=1, source_target_pairs={{0,16},{4,20},{8,24},{12,28},{16,0},{20,4},{24,8},{28,12},{1,17},{... | collective-permute-start | bytes 638984 | tf_op jit(solution)/shard_map/ppermute | solution.py:363
  24.3 0.9 %project_other.6 = bf16[96,1536]{1,0:T(8,128)(2,1)S(1)} custom-call(bf16[96,1536]{1,0:T(8,128)(2,1)S(1)} %shard_map.97.att_ref, bf16[1536,6144]{1,0:T(8,128)(2,1)S(1)} %copy-done), custom_call_target="tpu_custom_call" | custom-call | flops 452984832 | bytes 4718592 | tf_op jit(solution)/shard_map/project_other/pallas_call | solution.py:224
  25.2 0.3 collective-permute-start.22
  25.4 2.4 %collective-permute-start.13 = (bf16[208,512]{1,0:T(8,128)(2,1)S(1)}, bf16[208,512]{1,0:T(8,128)(2,1)S(1)}, u32[]{:S(2)}, u32[]{:S(2)}) collective-permute-start(bf16[208,512]{1,0:T(8,128)(2,1)S(1)} %join.1.refs_10_), channel_id=1, source_target_pairs={{0,8},{4,12},{8,0},{12,4},{16,24},{20,28},{24,16},{28,20},{1,9},{5... | collective-permute-start | bytes 638984 | tf_op jit(solution)/shard_map/ppermute | solution.py:363
  27.9 8.7 %collective-permute-done.5.refs_11_ = bf16[208,512]{1,0:T(8,128)(2,1)S(1)} collective-permute-done((bf16[208,512]{1,0:T(8,128)(2,1)S(1)}, bf16[208,512]{1,0:T(8,128)(2,1)S(1)}, u32[]{:S(2)}, u32[]{:S(2)}) %collective-permute-start.5) | collective-permute-done | bytes 213024 | tf_op jit(solution)/shard_map/ppermute | solution.py:363
  36.6 0.9 %project_own.7 = bf16[96,1536]{1,0:T(8,128)(2,1)S(1)} custom-call(bf16[96,1536]{1,0:T(8,128)(2,1)S(1)} %shard_map.97.att_ref, bf16[1536,6144]{1,0:T(8,128)(2,1)S(1)} %copy-done, bf16[96,1536]{1,0:T(8,128)(2,1)S(1)} %collective-permute-done.25.rest_0_, bf16[192,1536]{1,0:T(8,128)(2,1)S(1)} %copy-done.1), custom_call_target="tpu_custom_call" | custom-call | flops 452984832 | bytes 4718592 | tf_op jit(solution)/shard_map/project_own/pallas_call | solution.py:224
  37.6 1.6 %collective-permute-start.26 = (bf16[96,1536]{1,0:T(8,128)(2,1)S(1)}, bf16[96,1536]{1,0:T(8,128)(2,1)S(1)}, u32[]{:S(2)}, u32[]{:S(2)}) collective-permute-start(bf16[96,1536]{1,0:T(8,128)(2,1)S(1)} %project_own.7), channel_id=1, source_target_pairs={{0,2},{1,3},{2,0},{3,1},{4,6},{5,7},{6,4},{7,5},{8,10},{9,11},{10,... | collective-permute-start | bytes 884744 | tf_op jit(solution)/shard_map/ppermute | solution.py:369
  39.1 0.5 collective-permute-start.1
  39.7 6.6 %collective-permute-done.1.refs_2_ = f32[1,1536]{1,0:T(1,128)S(1)} collective-permute-done((f32[1,1536]{1,0:T(1,128)S(1)}, f32[1,1536]{1,0:T(1,128)S(1)}, u32[]{:S(2)}, u32[]{:S(2)}) %collective-permute-start.1) | collective-permute-done | bytes 6176 | tf_op jit(solution)/shard_map/ppermute | solution.py:369
  46.3 0.5 collective-permute-start.2
  46.8 3.3 %shard_map.94 = (f32[256,576]{1,0:T(8,128)S(1)}, f32[2,1,576]{2,1,0:T(1,128)S(1)}, f32[2,1,576]{2,1,0:T(1,128)S(1)}) custom-call(bf16[192,1536]{1,0:T(8,128)(2,1)S(1)} %copy-done.2, bf16[104,512]{1,0:T(8,128)(2,1)S(1)} %get-tuple-element.20.refs_1_.refs_2_, bf16[104,512]{1,0:T(8,128)(2,1)S(1)} %get-tuple-element.20.refs_1_.refs_2_, ...), custom_call_target="tpu_custom_call" | custom-call | flops 792723456 | bytes 1376256 | tf_op jit(solution)/shard_map/pallas_call | solution.py:186
  50.1 0.9 %project_own.6 = bf16[96,1536]{1,0:T(8,128)(2,1)S(1)} custom-call(bf16[96,1536]{1,0:T(8,128)(2,1)S(1)} %shard_map.97.att_ref, bf16[1536,6144]{1,0:T(8,128)(2,1)S(1)} %copy-done, bf16[96,1536]{1,0:T(8,128)(2,1)S(1)} %collective-permute-done.22.rest_0_, bf16[192,1536]{1,0:T(8,128)(2,1)S(1)} %copy-done.1), custom_call_target="tpu_custom_call" | custom-call | flops 452984832 | bytes 4718592 | tf_op jit(solution)/shard_map/project_own/pallas_call | solution.py:224
  51.0 1.6 %collective-permute-start.23 = (bf16[96,1536]{1,0:T(8,128)(2,1)S(1)}, bf16[96,1536]{1,0:T(8,128)(2,1)S(1)}, u32[]{:S(2)}, u32[]{:S(2)}) collective-permute-start(bf16[96,1536]{1,0:T(8,128)(2,1)S(1)} %project_own.6), channel_id=1, source_target_pairs={{0,2},{1,3},{2,0},{3,1},{4,6},{5,7},{6,4},{7,5},{8,10},{9,11},{10,... | collective-permute-start | bytes 884744 | tf_op jit(solution)/shard_map/ppermute | solution.py:369
  52.6 0.9 %shard_map.95.att_ref = bf16[96,1536]{1,0:T(8,128)(2,1)S(1)} custom-call(bf16[192,1536]{1,0:T(8,128)(2,1)S(1)} %copy-done.2, bf16[104,512]{1,0:T(8,128)(2,1)S(1)} %get-tuple-element.20.refs_1_.refs_2_, bf16[208,512]{1,0:T(8,128)(2,1)S(1)} %collective-permute-done.6.refs_2_, f32[256,576]{1,0:T(8,128)S(1)} %get-tuple-element.23.refs_3_, ...), custom_call_target="tpu_custom_call" | custom-call | flops 113246208 | bytes 196608 | tf_op jit(solution)/shard_map/pallas_call | solution.py:186
  53.5 0.9 %project_other.5 = bf16[96,1536]{1,0:T(8,128)(2,1)S(1)} custom-call(bf16[96,1536]{1,0:T(8,128)(2,1)S(1)} %shard_map.95.att_ref, bf16[1536,6144]{1,0:T(8,128)(2,1)S(1)} %copy-done), custom_call_target="tpu_custom_call" | custom-call | flops 452984832 | bytes 4718592 | tf_op jit(solution)/shard_map/project_other/pallas_call | solution.py:224
  54.5 0.9 %project_other.4 = bf16[96,1536]{1,0:T(8,128)(2,1)S(1)} custom-call(bf16[96,1536]{1,0:T(8,128)(2,1)S(1)} %shard_map.95.att_ref, bf16[1536,6144]{1,0:T(8,128)(2,1)S(1)} %copy-done), custom_call_target="tpu_custom_call" | custom-call | flops 452984832 | bytes 4718592 | tf_op jit(solution)/shard_map/project_other/pallas_call | solution.py:224
  55.4 0.5 collective-permute-start.14
  56.1 0.1 collective-permute-start.27
  56.2 1.1 %project_own.5 = (bf16[48,1536]{1,0:T(8,128)(2,1)S(1)}, bf16[48,1536]{1,0:T(8,128)(2,1)S(1)}) custom-call(bf16[96,1536]{1,0:T(8,128)(2,1)S(1)} %shard_map.95.att_ref, bf16[1536,6144]{1,0:T(8,128)(2,1)S(1)} %copy-done, bf16[96,1536]{1,0:T(8,128)(2,1)S(1)} %collective-permute-done.17.rest_0_, bf16[192,1536]{1,0:T(8,128)(2,1)S(1)} %copy-done.1), custom_call_target="tpu_custom_call" | custom-call | flops 452984832 | bytes 4718592 | tf_op jit(solution)/shard_map/project_own/pallas_call | solution.py:224
  57.3 2.7 %collective-permute-done.23 = bf16[96,1536]{1,0:T(8,128)(2,1)S(1)} collective-permute-done((bf16[96,1536]{1,0:T(8,128)(2,1)S(1)}, bf16[96,1536]{1,0:T(8,128)(2,1)S(1)}, u32[]{:S(2)}, u32[]{:S(2)}) %collective-permute-start.23) | collective-permute-done | bytes 294944 | tf_op jit(solution)/shard_map/ppermute | solution.py:369
  60.0 1.5 %collective-permute-start.20 = (bf16[48,1536]{1,0:T(8,128)(2,1)S(1)}, bf16[48,1536]{1,0:T(8,128)(2,1)S(1)}, u32[]{:S(2)}, u32[]{:S(2)}) collective-permute-start(bf16[48,1536]{1,0:T(8,128)(2,1)S(1)} %get-tuple-element.27), channel_id=1, source_target_pairs={{0,2},{1,3},{2,0},{3,1},{4,6},{5,7},{6,4},{7,5},{8,10},{9,11},{10,... | collective-permute-start | bytes 442376 | tf_op jit(solution)/shard_map/ppermute | solution.py:369
  61.7 0.9 %project_own.4 = bf16[96,1536]{1,0:T(8,128)(2,1)S(1)} custom-call(bf16[96,1536]{1,0:T(8,128)(2,1)S(1)} %shard_map.95.att_ref, bf16[1536,6144]{1,0:T(8,128)(2,1)S(1)} %copy-done, bf16[96,1536]{1,0:T(8,128)(2,1)S(1)} %collective-permute-done.14.rest_0_, bf16[192,1536]{1,0:T(8,128)(2,1)S(1)} %copy-done.1), custom_call_target="tpu_custom_call" | custom-call | flops 452984832 | bytes 4718592 | tf_op jit(solution)/shard_map/project_own/pallas_call | solution.py:224
  62.6 2.5 %collective-permute-done.20 = bf16[48,1536]{1,0:T(8,128)(2,1)S(1)} collective-permute-done((bf16[48,1536]{1,0:T(8,128)(2,1)S(1)}, bf16[48,1536]{1,0:T(8,128)(2,1)S(1)}, u32[]{:S(2)}, u32[]{:S(2)}) %collective-permute-start.20) | collective-permute-done | bytes 147488 | tf_op jit(solution)/shard_map/ppermute | solution.py:369
  65.2 1.5 %collective-permute-start.15 = (bf16[96,1536]{1,0:T(8,128)(2,1)S(1)}, bf16[96,1536]{1,0:T(8,128)(2,1)S(1)}, u32[]{:S(2)}, u32[]{:S(2)}) collective-permute-start(bf16[96,1536]{1,0:T(8,128)(2,1)S(1)} %project_own.4), channel_id=1, source_target_pairs={{0,2},{1,3},{2,0},{3,1},{4,6},{5,7},{6,4},{7,5},{8,10},{9,11},{10,... | collective-permute-start | bytes 884744 | tf_op jit(solution)/shard_map/ppermute | solution.py:369
  66.7 5.6 %collective-permute-done.15 = bf16[96,1536]{1,0:T(8,128)(2,1)S(1)} collective-permute-done((bf16[96,1536]{1,0:T(8,128)(2,1)S(1)}, bf16[96,1536]{1,0:T(8,128)(2,1)S(1)}, u32[]{:S(2)}, u32[]{:S(2)}) %collective-permute-start.15) | collective-permute-done | bytes 294944 | tf_op jit(solution)/shard_map/ppermute | solution.py:369
  72.3 1.5 %collective-permute-start.18 = (bf16[48,1536]{1,0:T(8,128)(2,1)S(1)}, bf16[48,1536]{1,0:T(8,128)(2,1)S(1)}, u32[]{:S(2)}, u32[]{:S(2)}) collective-permute-start(bf16[48,1536]{1,0:T(8,128)(2,1)S(1)} %get-tuple-element.26), channel_id=1, source_target_pairs={{0,2},{1,3},{2,0},{3,1},{4,6},{5,7},{6,4},{7,5},{8,10},{9,11},{10,... | collective-permute-start | bytes 442376 | tf_op jit(solution)/shard_map/ppermute | solution.py:369
  73.9 3.6 %collective-permute-done.18 = bf16[48,1536]{1,0:T(8,128)(2,1)S(1)} collective-permute-done((bf16[48,1536]{1,0:T(8,128)(2,1)S(1)}, bf16[48,1536]{1,0:T(8,128)(2,1)S(1)}, u32[]{:S(2)}, u32[]{:S(2)}) %collective-permute-start.18) | collective-permute-done | bytes 147488 | tf_op jit(solution)/shard_map/ppermute | solution.py:369
  77.5 0.6 collective-permute-start.21
  78.1 0.1 collective-permute-start.19
  78.2 2.0 %shard_map.98 = (bf16[192,6144]{1,0:T(8,128)(2,1)}, f32[1,192]{1,0:T(1,128)S(1)}, bf16[192,1536]{1,0:T(8,128)(2,1)}) custom-call(f32[1,1536]{1,0:T(1,128)S(1)} %copy-done.3, f32[1,1536]{1,0:T(1,128)S(1)} %collective-permute-done.refs_1_, f32[1,1536]{1,0:T(1,128)S(1)} %collective-permute-done.1.refs_2_, f32[1,1536]{1,0:T(1,128)S(1)} %collective-permute-done.2.refs_3_, ...), custom_call_target="tpu_custom_call" | custom-call | flops 2000000000 | bytes 2359296 | tf_op jit(solution)/shard_map/pallas_call | solution.py:324
  80.2 1.3 %shard_map.99 = (bf16[192,6144]{1,0:T(8,128)(2,1)}, f32[1,192]{1,0:T(1,128)S(1)}, bf16[192,1536]{1,0:T(8,128)(2,1)}) custom-call(f32[1,1536]{1,0:T(1,128)S(1)} %copy-done.3, f32[1,1536]{1,0:T(1,128)S(1)} %collective-permute-done.refs_1_, f32[1,1536]{1,0:T(1,128)S(1)} %collective-permute-done.1.refs_2_, ...), custom_call_target="tpu_custom_call", output_to_operand_aliasing={{0}: (9, {}), {2}: (10, {})} | custom-call | flops 2000000000 | bytes 1179648 | tf_op jit(solution)/shard_map/pallas_call | solution.py:324
  81.6 1.3 %shard_map.100 = (bf16[192,6144]{1,0:T(8,128)(2,1)}, f32[192]{0:T(256)}, bf16[192,1536]{1,0:T(8,128)(2,1)}) custom-call(f32[1,1536]{1,0:T(1,128)S(1)} %copy-done.3, f32[1,1536]{1,0:T(1,128)S(1)} %collective-permute-done.refs_1_, f32[1,1536]{1,0:T(1,128)S(1)} %collective-permute-done.1.refs_2_, ...), custom_call_target="tpu_custom_call", output_to_operand_aliasing={{0}: (9, {}), {2}: (10, {})} | custom-call | flops 2000000000 | bytes 1179648 | tf_op jit(solution)/shard_map/pallas_call | solution.py:324
  (39 shorter events, 0.6 us)
Async XLA Ops:
  0.6 17.6 %copy-start.2 = (bf16[192,1536]{1,0:T(8,128)(2,1)S(1)}, bf16[192,1536]{1,0:T(8,128)(2,1)}, u32[]{:S(2)}) copy-start(bf16[192,1536]{1,0:T(8,128)(2,1)} %refs_0_.10) | copy-start | bytes 1769476
  0.6 21.6 %copy-start = (bf16[1536,6144]{1,0:T(8,128)(2,1)S(1)}, bf16[1536,6144]{1,0:T(8,128)(2,1)}, u32[]{:S(2)}) copy-start(bf16[1536,6144]{1,0:T(8,128)(2,1)} %weight_ref.15) | copy-start | bytes 56623108
  1.7 9.0 %collective-permute-start.3 = (bf16[104,512]{1,0:T(8,128)(2,1)S(1)}, bf16[104,512]{1,0:T(8,128)(2,1)S(1)}, u32[]{:S(2)}, u32[]{:S(2)}) collective-permute-start(bf16[104,512]{1,0:T(8,128)(2,1)S(1)} %get-tuple-element.20.refs_1_.refs_2_), channel_id=1, source_target_pairs={{0,24},{4,28},{8,16},{12,20},{16,8},{20,12},{24,0},{28,4},{1,25},{... | collective-permute-start | bytes 319496 | tf_op jit(solution)/shard_map/ppermute | solution.py:363
  6.9 6.3 %collective-permute-start.9 = (bf16[104,512]{1,0:T(8,128)(2,1)S(1)}, bf16[104,512]{1,0:T(8,128)(2,1)S(1)}, u32[]{:S(2)}, u32[]{:S(2)}) collective-permute-start(bf16[104,512]{1,0:T(8,128)(2,1)S(1)} %get-tuple-element.20.refs_1_.refs_2_), channel_id=1, source_target_pairs={{0,8},{4,12},{8,0},{12,4},{16,24},{20,28},{24,16},{28,20},{1,9},{5... | collective-permute-start | bytes 319496 | tf_op jit(solution)/shard_map/ppermute | solution.py:363
  6.9 9.0 %collective-permute-start.11 = (bf16[104,512]{1,0:T(8,128)(2,1)S(1)}, bf16[104,512]{1,0:T(8,128)(2,1)S(1)}, u32[]{:S(2)}, u32[]{:S(2)}) collective-permute-start(bf16[104,512]{1,0:T(8,128)(2,1)S(1)} %get-tuple-element.20.refs_1_.refs_2_), channel_id=1, source_target_pairs={{0,16},{4,20},{8,24},{12,28},{16,0},{20,4},{24,8},{28,12},{1,17},{... | collective-permute-start | bytes 319496 | tf_op jit(solution)/shard_map/ppermute | solution.py:363
  7.5 10.4 %collective-permute-start.7 = (bf16[104,512]{1,0:T(8,128)(2,1)S(1)}, bf16[104,512]{1,0:T(8,128)(2,1)S(1)}, u32[]{:S(2)}, u32[]{:S(2)}) collective-permute-start(bf16[104,512]{1,0:T(8,128)(2,1)S(1)} %get-tuple-element.20.refs_1_.refs_2_), channel_id=1, source_target_pairs={{0,4},{4,0},{8,12},{12,8},{16,20},{20,16},{24,28},{28,24},{1,5},{5... | collective-permute-start | bytes 319496 | tf_op jit(solution)/shard_map/ppermute | solution.py:366
  10.7 7.1 %collective-permute-start.8 = (bf16[104,512]{1,0:T(8,128)(2,1)S(1)}, bf16[104,512]{1,0:T(8,128)(2,1)S(1)}, u32[]{:S(2)}, u32[]{:S(2)}) collective-permute-start(bf16[104,512]{1,0:T(8,128)(2,1)S(1)} %collective-permute-done.3.refs_4_), channel_id=1, source_target_pairs={{0,4},{4,0},{8,12},{12,8},{16,20},{20,16},{24,28},{28,24},{1,5},{5... | collective-permute-start | bytes 319496 | tf_op jit(solution)/shard_map/ppermute | solution.py:366
  13.2 5.0 %collective-permute-start.10 = (bf16[104,512]{1,0:T(8,128)(2,1)S(1)}, bf16[104,512]{1,0:T(8,128)(2,1)S(1)}, u32[]{:S(2)}, u32[]{:S(2)}) collective-permute-start(bf16[104,512]{1,0:T(8,128)(2,1)S(1)} %collective-permute-done.9.refs_6_), channel_id=1, source_target_pairs={{0,4},{4,0},{8,12},{12,8},{16,20},{20,16},{24,28},{28,24},{1,5},{5... | collective-permute-start | bytes 319496 | tf_op jit(solution)/shard_map/ppermute | solution.py:366
  15.8 5.5 %collective-permute-start.12 = (bf16[104,512]{1,0:T(8,128)(2,1)S(1)}, bf16[104,512]{1,0:T(8,128)(2,1)S(1)}, u32[]{:S(2)}, u32[]{:S(2)}) collective-permute-start(bf16[104,512]{1,0:T(8,128)(2,1)S(1)} %collective-permute-done.11.refs_8_.refs_2_), channel_id=1, source_target_pairs={{0,4},{4,0},{8,12},{12,8},{16,20},{20,16},{24,28},{28,24},{1,5},{5... | collective-permute-start | bytes 319496 | tf_op jit(solution)/shard_map/ppermute | solution.py:366
  17.3 6.0 %collective-permute-start.4 = (bf16[104,512]{1,0:T(8,128)(2,1)S(1)}, bf16[104,512]{1,0:T(8,128)(2,1)S(1)}, u32[]{:S(2)}, u32[]{:S(2)}) collective-permute-start(bf16[104,512]{1,0:T(8,128)(2,1)S(1)} %get-tuple-element.22.refs_0_), channel_id=1, source_target_pairs={{0,4},{4,0},{8,12},{12,8},{16,20},{20,16},{24,28},{28,24},{1,5},{5... | collective-permute-start | bytes 319496 | tf_op jit(solution)/shard_map/ppermute | solution.py:366
  23.2 13.4 %collective-permute-start.25 = (bf16[96,1536]{1,0:T(8,128)(2,1)S(1)}, bf16[96,1536]{1,0:T(8,128)(2,1)S(1)}, u32[]{:S(2)}, u32[]{:S(2)}) collective-permute-start(bf16[96,1536]{1,0:T(8,128)(2,1)S(1)} %project_other.7), channel_id=1, source_target_pairs={{0,1},{1,0},{2,3},{3,2},{4,5},{5,4},{6,7},{7,6},{8,9},{9,8},{10,11... | collective-permute-start | bytes 884744 | tf_op jit(solution)/shard_map/ppermute | solution.py:372
  23.3 13.3 %copy-start.1 = (bf16[192,1536]{1,0:T(8,128)(2,1)S(1)}, bf16[192,1536]{1,0:T(8,128)(2,1)}, u32[]{:S(2)}) copy-start(bf16[192,1536]{1,0:T(8,128)(2,1)} %rest_1_.7) | copy-start | bytes 1769476
  23.3 13.3 %collective-permute-start.5 = (bf16[208,512]{1,0:T(8,128)(2,1)S(1)}, bf16[208,512]{1,0:T(8,128)(2,1)S(1)}, u32[]{:S(2)}, u32[]{:S(2)}) collective-permute-start(bf16[208,512]{1,0:T(8,128)(2,1)S(1)} %join.1.refs_10_), channel_id=1, source_target_pairs={{0,16},{4,20},{8,24},{12,28},{16,0},{20,4},{24,8},{28,12},{1,17},{... | collective-permute-start | bytes 638984 | tf_op jit(solution)/shard_map/ppermute | solution.py:363
  25.2 14.0 %copy-start.3 = (f32[1,1536]{1,0:T(1,128)S(1)}, f32[1,1536]{1,0:T(1,128)}, u32[]{:S(2)}) copy-start(f32[1,1536]{1,0:T(1,128)} %refs_0_.13) | copy-start | bytes 18436
  25.2 24.9 %collective-permute-start.22 = (bf16[96,1536]{1,0:T(8,128)(2,1)S(1)}, bf16[96,1536]{1,0:T(8,128)(2,1)S(1)}, u32[]{:S(2)}, u32[]{:S(2)}) collective-permute-start(bf16[96,1536]{1,0:T(8,128)(2,1)S(1)} %project_other.6), channel_id=1, source_target_pairs={{0,1},{1,0},{2,3},{3,2},{4,5},{5,4},{6,7},{7,6},{8,9},{9,8},{10,11... | collective-permute-start | bytes 884744 | tf_op jit(solution)/shard_map/ppermute | solution.py:372
  25.4 20.8 %collective-permute-start.13 = (bf16[208,512]{1,0:T(8,128)(2,1)S(1)}, bf16[208,512]{1,0:T(8,128)(2,1)S(1)}, u32[]{:S(2)}, u32[]{:S(2)}) collective-permute-start(bf16[208,512]{1,0:T(8,128)(2,1)S(1)} %join.1.refs_10_), channel_id=1, source_target_pairs={{0,8},{4,12},{8,0},{12,4},{16,24},{20,28},{24,16},{28,20},{1,9},{5... | collective-permute-start | bytes 638984 | tf_op jit(solution)/shard_map/ppermute | solution.py:363
  36.6 16.0 %collective-permute-start.6 = (bf16[208,512]{1,0:T(8,128)(2,1)S(1)}, bf16[208,512]{1,0:T(8,128)(2,1)S(1)}, u32[]{:S(2)}, u32[]{:S(2)}) collective-permute-start(bf16[208,512]{1,0:T(8,128)(2,1)S(1)} %collective-permute-done.5.refs_11_), channel_id=1, source_target_pairs={{0,8},{4,12},{8,0},{12,4},{16,24},{20,28},{24,16},{28,20},{1,9},{5... | collective-permute-start | bytes 638984 | tf_op jit(solution)/shard_map/ppermute | solution.py:363
  37.6 17.8 %collective-permute-start.26 = (bf16[96,1536]{1,0:T(8,128)(2,1)S(1)}, bf16[96,1536]{1,0:T(8,128)(2,1)S(1)}, u32[]{:S(2)}, u32[]{:S(2)}) collective-permute-start(bf16[96,1536]{1,0:T(8,128)(2,1)S(1)} %project_own.7), channel_id=1, source_target_pairs={{0,2},{1,3},{2,0},{3,1},{4,6},{5,7},{6,4},{7,5},{8,10},{9,11},{10,... | collective-permute-start | bytes 884744 | tf_op jit(solution)/shard_map/ppermute | solution.py:369
  39.1 7.1 %collective-permute-start.1 = (f32[1,1536]{1,0:T(1,128)S(1)}, f32[1,1536]{1,0:T(1,128)S(1)}, u32[]{:S(2)}, u32[]{:S(2)}) collective-permute-start(f32[1,1536]{1,0:T(1,128)S(1)} %copy-done.3), channel_id=1, source_target_pairs={{0,2},{1,3},{2,0},{3,1},{4,6},{5,7},{6,4},{7,5},{8,10},{9,11},{10,... | collective-permute-start | bytes 18440 | tf_op jit(solution)/shard_map/ppermute | solution.py:369
  46.2 31.3 %collective-permute-start = (f32[1,1536]{1,0:T(1,128)S(1)}, f32[1,1536]{1,0:T(1,128)S(1)}, u32[]{:S(2)}, u32[]{:S(2)}) collective-permute-start(f32[1,1536]{1,0:T(1,128)S(1)} %copy-done.3), channel_id=1, source_target_pairs={{0,1},{1,0},{2,3},{3,2},{4,5},{5,4},{6,7},{7,6},{8,9},{9,8},{10,11... | collective-permute-start | bytes 18440 | tf_op jit(solution)/shard_map/ppermute | solution.py:372
  46.3 31.9 %collective-permute-start.2 = (f32[1,1536]{1,0:T(1,128)S(1)}, f32[1,1536]{1,0:T(1,128)S(1)}, u32[]{:S(2)}, u32[]{:S(2)}) collective-permute-start(f32[1,1536]{1,0:T(1,128)S(1)} %collective-permute-done.1.refs_2_), channel_id=1, source_target_pairs={{0,1},{1,0},{2,3},{3,2},{4,5},{5,4},{6,7},{7,6},{8,9},{9,8},{10,11... | collective-permute-start | bytes 18440 | tf_op jit(solution)/shard_map/ppermute | solution.py:372
  51.0 9.0 %collective-permute-start.23 = (bf16[96,1536]{1,0:T(8,128)(2,1)S(1)}, bf16[96,1536]{1,0:T(8,128)(2,1)S(1)}, u32[]{:S(2)}, u32[]{:S(2)}) collective-permute-start(bf16[96,1536]{1,0:T(8,128)(2,1)S(1)} %project_own.6), channel_id=1, source_target_pairs={{0,2},{1,3},{2,0},{3,1},{4,6},{5,7},{6,4},{7,5},{8,10},{9,11},{10,... | collective-permute-start | bytes 884744 | tf_op jit(solution)/shard_map/ppermute | solution.py:369
  54.4 1.6 %collective-permute-start.17 = (bf16[96,1536]{1,0:T(8,128)(2,1)S(1)}, bf16[96,1536]{1,0:T(8,128)(2,1)S(1)}, u32[]{:S(2)}, u32[]{:S(2)}) collective-permute-start(bf16[96,1536]{1,0:T(8,128)(2,1)S(1)} %project_other.5), channel_id=1, source_target_pairs={{0,1},{1,0},{2,3},{3,2},{4,5},{5,4},{6,7},{7,6},{8,9},{9,8},{10,11... | collective-permute-start | bytes 884744 | tf_op jit(solution)/shard_map/ppermute | solution.py:372
  55.4 6.2 %collective-permute-start.14 = (bf16[96,1536]{1,0:T(8,128)(2,1)S(1)}, bf16[96,1536]{1,0:T(8,128)(2,1)S(1)}, u32[]{:S(2)}, u32[]{:S(2)}) collective-permute-start(bf16[96,1536]{1,0:T(8,128)(2,1)S(1)} %project_other.4), channel_id=1, source_target_pairs={{0,1},{1,0},{2,3},{3,2},{4,5},{5,4},{6,7},{7,6},{8,9},{9,8},{10,11... | collective-permute-start | bytes 884744 | tf_op jit(solution)/shard_map/ppermute | solution.py:372
  56.1 22.1 %collective-permute-start.27 = (bf16[96,1536]{1,0:T(8,128)(2,1)S(1)}, bf16[96,1536]{1,0:T(8,128)(2,1)S(1)}, u32[]{:S(2)}, u32[]{:S(2)}) collective-permute-start(bf16[96,1536]{1,0:T(8,128)(2,1)S(1)} %add_convert_fusion.refs_6_), channel_id=1, source_target_pairs={{0,1},{1,0},{2,3},{3,2},{4,5},{5,4},{6,7},{7,6},{8,9},{9,8},{10,11... | collective-permute-start | bytes 884744 | tf_op jit(solution)/shard_map/ppermute | solution.py:372
  60.0 5.1 %collective-permute-start.20 = (bf16[48,1536]{1,0:T(8,128)(2,1)S(1)}, bf16[48,1536]{1,0:T(8,128)(2,1)S(1)}, u32[]{:S(2)}, u32[]{:S(2)}) collective-permute-start(bf16[48,1536]{1,0:T(8,128)(2,1)S(1)} %get-tuple-element.27), channel_id=1, source_target_pairs={{0,2},{1,3},{2,0},{3,1},{4,6},{5,7},{6,4},{7,5},{8,10},{9,11},{10,... | collective-permute-start | bytes 442376 | tf_op jit(solution)/shard_map/ppermute | solution.py:369
  61.6 16.6 %collective-permute-start.24 = (bf16[96,1536]{1,0:T(8,128)(2,1)S(1)}, bf16[96,1536]{1,0:T(8,128)(2,1)S(1)}, u32[]{:S(2)}, u32[]{:S(2)}) collective-permute-start(bf16[96,1536]{1,0:T(8,128)(2,1)S(1)} %add_convert_fusion.1.refs_4_), channel_id=1, source_target_pairs={{0,1},{1,0},{2,3},{3,2},{4,5},{5,4},{6,7},{7,6},{8,9},{9,8},{10,11... | collective-permute-start | bytes 884744 | tf_op jit(solution)/shard_map/ppermute | solution.py:372
  65.2 7.2 %collective-permute-start.15 = (bf16[96,1536]{1,0:T(8,128)(2,1)S(1)}, bf16[96,1536]{1,0:T(8,128)(2,1)S(1)}, u32[]{:S(2)}, u32[]{:S(2)}) collective-permute-start(bf16[96,1536]{1,0:T(8,128)(2,1)S(1)} %project_own.4), channel_id=1, source_target_pairs={{0,2},{1,3},{2,0},{3,1},{4,6},{5,7},{6,4},{7,5},{8,10},{9,11},{10,... | collective-permute-start | bytes 884744 | tf_op jit(solution)/shard_map/ppermute | solution.py:369
  72.3 5.1 %collective-permute-start.18 = (bf16[48,1536]{1,0:T(8,128)(2,1)S(1)}, bf16[48,1536]{1,0:T(8,128)(2,1)S(1)}, u32[]{:S(2)}, u32[]{:S(2)}) collective-permute-start(bf16[48,1536]{1,0:T(8,128)(2,1)S(1)} %get-tuple-element.26), channel_id=1, source_target_pairs={{0,2},{1,3},{2,0},{3,1},{4,6},{5,7},{6,4},{7,5},{8,10},{9,11},{10,... | collective-permute-start | bytes 442376 | tf_op jit(solution)/shard_map/ppermute | solution.py:369
  77.5 2.8 %collective-permute-start.16 = (bf16[96,1536]{1,0:T(8,128)(2,1)S(1)}, bf16[96,1536]{1,0:T(8,128)(2,1)S(1)}, u32[]{:S(2)}, u32[]{:S(2)}) collective-permute-start(bf16[96,1536]{1,0:T(8,128)(2,1)S(1)} %add_convert_fusion.2.refs_4_), channel_id=1, source_target_pairs={{0,1},{1,0},{2,3},{3,2},{4,5},{5,4},{6,7},{7,6},{8,9},{9,8},{10,11... | collective-permute-start | bytes 884744 | tf_op jit(solution)/shard_map/ppermute | solution.py:372
  77.5 2.7 %collective-permute-start.21 = (bf16[48,1536]{1,0:T(8,128)(2,1)S(1)}, bf16[48,1536]{1,0:T(8,128)(2,1)S(1)}, u32[]{:S(2)}, u32[]{:S(2)}) collective-permute-start(bf16[48,1536]{1,0:T(8,128)(2,1)S(1)} %add_convert_fusion.3.refs_6_), channel_id=1, source_target_pairs={{0,1},{1,0},{2,3},{3,2},{4,5},{5,4},{6,7},{7,6},{8,9},{9,8},{10,11... | collective-permute-start | bytes 442376 | tf_op jit(solution)/shard_map/ppermute | solution.py:372
  78.1 3.5 %collective-permute-start.19 = (bf16[48,1536]{1,0:T(8,128)(2,1)S(1)}, bf16[48,1536]{1,0:T(8,128)(2,1)S(1)}, u32[]{:S(2)}, u32[]{:S(2)}) collective-permute-start(bf16[48,1536]{1,0:T(8,128)(2,1)S(1)} %add_convert_fusion.4.refs_6_), channel_id=1, source_target_pairs={{0,1},{1,0},{2,3},{3,2},{4,5},{5,4},{6,7},{7,6},{8,9},{9,8},{10,11... | collective-permute-start | bytes 442376 | tf_op jit(solution)/shard_map/ppermute | solution.py:372

commit v3 on v2

--- a/solution.py
+++ b/solution.py
@@ -194,12 +194,12 @@
     )(*[near(operand) for operand in operands])
 
 
-def project_body(cores, blocks, half, own, att_ref, weight_ref, *rest):
+def project_body(cores, blocks, half, distance, own, att_ref, weight_ref, *rest):
     outs = rest[2:] if own else rest
     width = outs[0].shape[1] // len(blocks)
     tp = lax.axis_index("tp")
     for i, yb in enumerate(blocks):
-        block = yb * cores + ((tp % cores) ^ (0 if own else 1))
+        block = yb * cores + ((tp % cores) ^ distance)
         start = pl.multiple_of(block * width, HEAD)
         total = jnp.dot(att_ref[...], weight_ref[:, pl.ds(start, width)], preferred_element_type=F32)
         columns = slice(i * width, (i + 1) * width)
@@ -216,13 +216,13 @@
             row += out.shape[0]
 
 
-def project(cores, blocks, half, attended, weight, block_width, cuts=(1,), arrived=None, residual=None):
+def project(cores, blocks, half, distance, attended, weight, block_width, cuts=(1,), arrived=None, residual=None):
     rows, depth = attended.shape
     width = block_width * len(blocks)
     own = arrived is not None
     operands = [attended, weight] + ([arrived, residual] if own else [])
     result = pl.pallas_call(
-        functools.partial(project_body, cores, blocks, half, own),
+        functools.partial(project_body, cores, blocks, half, distance, own),
         out_shape=tuple(VMEM((rows * cut // sum(cuts), width), BF16) for cut in cuts),
         in_specs=[in_vmem()] * len(operands),
         out_specs=(in_vmem(),) * len(cuts),
@@ -231,6 +231,26 @@
         name="project_own" if own else "project_other",
     )(*[near(operand) for operand in operands])
     return result if own else result[0]
+
+
+def combine_body(cores, yb, half, own_ref, arrived_ref, residual_ref, out_ref):
+    rows = own_ref.shape[0]
+    mine = jnp.where(lax.axis_index("tp") // cores == yb, 1.0, 0.0).astype(F32)
+    total = own_ref[...].astype(F32) + arrived_ref[...].astype(F32)
+    total = total + mine * residual_ref[half * rows : (half + 1) * rows, :].astype(F32)
+    out_ref[...] = total.astype(BF16)
+
+
+def combine(cores, yb, half, own, arrived, residual):
+    return pl.pallas_call(
+        functools.partial(combine_body, cores, yb, half),
+        out_shape=VMEM(own.shape, BF16),
+        in_specs=[in_vmem()] * 3,
+        out_specs=in_vmem(),
+        compiler_params=grant(8),
+        cost_estimate=cost(2e8, 8 * own.size),
+        name="combine",
+    )(near(own), near(arrived), near(residual))
 
 
 def finish_body(ny, cores, row, rows, places, count, last, *refs):
@@ -393,12 +413,16 @@
 
     begun = attend(queries, 0, low, [low_pieces[:-nx]], None, False)
     early = attend(queries, 0, low, [low_pieces[-nx:]], begun)
-    sent, parts = [], []
-    for yb in range(ny):
-        other = project(cores, [yb], 0, early, out_weight, block_width)
-        sent.append(move_core(other, 1))
-    for yb in range(ny):
-        own = project(cores, [yb], 0, early, out_weight, block_width, (1,), sent[yb], residual)[0]
+    parts = []
+    for yb in range(ny):
+        other = project(cores, [yb], 0, 1, early, out_weight, block_width)
+        arrived = move_core(other, 1)
+        if yb == 0:
+            own = project(cores, [yb], 0, 0, early, out_weight, block_width)
+        else:
+            own = project(cores, [yb], 0, 0, early, out_weight, block_width, (1,), arrived, residual)[0]
+        if yb == 0:
+            own = combine(cores, yb, 0, own, arrived, residual)
         total = tree_sum([own] + [move_y(own, k) for k in range(1, ny)])
         parts += [total, move_core(total, 1)]
     gains = [norm_gain] + [move_y(norm_gain, k) for k in range(1, ny)]
@@ -408,13 +432,17 @@
 
     begun = attend(queries, 1, low, [low_pieces, high_pieces[:-1]], None, False)
     late = attend(queries, 1, low, [[], high_pieces[-1:]], begun)
-    sent, parts = [], []
-    for yb in range(ny):
-        other = project(cores, [yb], 1, late, out_weight, block_width)
-        sent.append(move_core(other, 1))
+    parts = []
     for yb in range(ny):
         cuts = CUTS if yb == ny - 1 else (1,)
-        owns = project(cores, [yb], 1, late, out_weight, block_width, cuts, sent[yb], residual)
+        other = project(cores, [yb], 1, 1, late, out_weight, block_width)
+        arrived = move_core(other, 1)
+        if yb == 0 and yb < ny - 1:
+            own = project(cores, [yb], 1, 0, late, out_weight, block_width)
+        else:
+            owns = project(cores, [yb], 1, 0, late, out_weight, block_width, cuts, arrived, residual)
+        if yb == 0 and yb < ny - 1:
+            owns = [combine(cores, yb, 1, own, arrived, residual)]
         for own in owns:
             total = tree_sum([own] + [move_y(own, k) for k in range(1, ny)])
             parts += [total, move_core(total, 1)]

time: 83.2 us -> 82.4 us (level)
  waiting for transfers between devices: 35.4 us -> 34.4 us
    ppermute x6, waiting for transfers between devices: 21 us -> 20 us  [move_y(): return lax.ppermute(array, 'tp', swap(ny, n_tp, cores, k))]
    pallas_call x8 -> x10, Pallas kernels: 7.51 us -> 7.64 us  [the longest x8 7.38 us: project(): pl.pallas_call(functools.partial(project_body, cores, blocks, half, dista...]
  transfers between devices with their start and end apart: 28 -> 28, of which waited for: 11 -> 11; matrix products, arithmetic and copies ran while one was open for 0% -> 0% of each run, Pallas kernels for 21% -> 22%
where the time goes in v3:
time: 82.4 us; the launch traced here: 82.2 us
  waiting for transfers between devices  34.4 us (42%)
  starting transfers between devices  26.4 us (32%)
  Pallas kernels  20.1 us (24%)
  between operations  1.1 us (1%)
    ppermute x6, waiting for transfers between devices, move_y(): return lax.ppermute(array, 'tp', swap(ny, n_tp, cores, k))  20 us
    ppermute x6, waiting for transfers between devices, move_z(): return lax.ppermute(array, 'seq', swap(nz, n_seq, nx, k))  12.4 us
    ppermute x6, starting transfers between devices, move_z(): return lax.ppermute(array, 'seq', swap(nz, n_seq, nx, k))  9.18 us
    ppermute x6, starting transfers between devices, move_y(): return lax.ppermute(array, 'tp', swap(ny, n_tp, cores, k))  8.22 us
    pallas_call x8, Pallas kernels, project(): pl.pallas_call(functools.partial(project_body, cores, blocks, half, dista...  7.38 us
    ppermute x5, starting transfers between devices, move_x(): return lax.ppermute(array, 'seq', swap(nx, n_seq, 1, k))  6.71 us
    pallas_call x4, Pallas kernels, attend(): pl.pallas_call(functools.partial(attend_body, run_rows, query_half, key_h...  6.68 us
    pallas_call x3, Pallas kernels, finish(): pl.pallas_call(functools.partial(finish_body, ny, cores, row, rows, place...  4.66 us
  transfers between devices with their start and end apart: 28, of which 11 were waited for; matrix products, arithmetic and copies ran while one was open for 0% of the time, Pallas kernels for 22%

profile of v3, /device:TPU:0, one launch (start us, length us, event | category | flops | bytes accessed | tf_op | source)
XLA Modules:
  0.0 82.2 jit_solution(15465135521394549826)
XLA Ops:
  0.7 1.1 %pack.1 = (bf16[104,512]{1,0:T(8,128)(2,1)S(1)}, bf16[104,512]{1,0:T(8,128)(2,1)S(1)}) custom-call(s32[192]{0:T(256)} %pos_ref.1, bf16[192,256]{1,0:T(8,128)(2,1)} %key_ref.1, bf16[192,256]{1,0:T(8,128)(2,1)} %value_ref.1), custom_call_target="tpu_custom_call" | custom-call | flops 40000000000 | bytes 393216 | tf_op jit(solution)/shard_map/pack/pallas_call | solution.py:70
  1.7 5.1 %collective-permute-start.3 = (bf16[104,512]{1,0:T(8,128)(2,1)S(1)}, bf16[104,512]{1,0:T(8,128)(2,1)S(1)}, u32[]{:S(2)}, u32[]{:S(2)}) collective-permute-start(bf16[104,512]{1,0:T(8,128)(2,1)S(1)} %get-tuple-element.20.refs_1_.refs_2_), channel_id=1, source_target_pairs={{0,24},{4,28},{8,16},{12,20},{16,8},{20,12},{24,0},{28,4},{1,25},{... | collective-permute-start | bytes 319496 | tf_op jit(solution)/shard_map/ppermute | solution.py:383
  6.9 0.6 collective-permute-start.11
  7.5 1.6 %collective-permute-start.7 = (bf16[104,512]{1,0:T(8,128)(2,1)S(1)}, bf16[104,512]{1,0:T(8,128)(2,1)S(1)}, u32[]{:S(2)}, u32[]{:S(2)}) collective-permute-start(bf16[104,512]{1,0:T(8,128)(2,1)S(1)} %get-tuple-element.20.refs_1_.refs_2_), channel_id=1, source_target_pairs={{0,4},{4,0},{8,12},{12,8},{16,20},{20,16},{24,28},{28,24},{1,5},{5... | collective-permute-start | bytes 319496 | tf_op jit(solution)/shard_map/ppermute | solution.py:386
  9.1 1.6 %collective-permute-done.3.refs_4_ = bf16[104,512]{1,0:T(8,128)(2,1)S(1)} collective-permute-done((bf16[104,512]{1,0:T(8,128)(2,1)S(1)}, bf16[104,512]{1,0:T(8,128)(2,1)S(1)}, u32[]{:S(2)}, u32[]{:S(2)}) %collective-permute-start.3) | collective-permute-done | bytes 106528 | tf_op jit(solution)/shard_map/ppermute | solution.py:383
  10.7 1.7 %collective-permute-start.8 = (bf16[104,512]{1,0:T(8,128)(2,1)S(1)}, bf16[104,512]{1,0:T(8,128)(2,1)S(1)}, u32[]{:S(2)}, u32[]{:S(2)}) collective-permute-start(bf16[104,512]{1,0:T(8,128)(2,1)S(1)} %collective-permute-done.3.refs_4_), channel_id=1, source_target_pairs={{0,4},{4,0},{8,12},{12,8},{16,20},{20,16},{24,28},{28,24},{1,5},{5... | collective-permute-start | bytes 319496 | tf_op jit(solution)/shard_map/ppermute | solution.py:386
  12.4 0.8 collective-permute-done.9.refs_6_
  13.2 1.4 %collective-permute-start.10 = (bf16[104,512]{1,0:T(8,128)(2,1)S(1)}, bf16[104,512]{1,0:T(8,128)(2,1)S(1)}, u32[]{:S(2)}, u32[]{:S(2)}) collective-permute-start(bf16[104,512]{1,0:T(8,128)(2,1)S(1)} %collective-permute-done.9.refs_6_), channel_id=1, source_target_pairs={{0,4},{4,0},{8,12},{12,8},{16,20},{20,16},{24,28},{28,24},{1,5},{5... | collective-permute-start | bytes 319496 | tf_op jit(solution)/shard_map/ppermute | solution.py:386
  14.6 1.2 %collective-permute-done.11.refs_8_.refs_2_ = bf16[104,512]{1,0:T(8,128)(2,1)S(1)} collective-permute-done((bf16[104,512]{1,0:T(8,128)(2,1)S(1)}, bf16[104,512]{1,0:T(8,128)(2,1)S(1)}, u32[]{:S(2)}, u32[]{:S(2)}) %collective-permute-start.11) | collective-permute-done | bytes 106528 | tf_op jit(solution)/shard_map/ppermute | solution.py:383
  15.8 1.5 %collective-permute-start.12 = (bf16[104,512]{1,0:T(8,128)(2,1)S(1)}, bf16[104,512]{1,0:T(8,128)(2,1)S(1)}, u32[]{:S(2)}, u32[]{:S(2)}) collective-permute-start(bf16[104,512]{1,0:T(8,128)(2,1)S(1)} %collective-permute-done.11.refs_8_.refs_2_), channel_id=1, source_target_pairs={{0,4},{4,0},{8,12},{12,8},{16,20},{20,16},{24,28},{28,24},{1,5},{5... | collective-permute-start | bytes 319496 | tf_op jit(solution)/shard_map/ppermute | solution.py:386
  17.3 0.5 collective-permute-start.4
  17.9 0.4 collective-permute-done.10.refs_7_
  18.2 1.5 %shard_map.96 = (f32[256,576]{1,0:T(8,128)S(1)}, f32[2,1,576]{2,1,0:T(1,128)S(1)}, f32[2,1,576]{2,1,0:T(1,128)S(1)}) custom-call(bf16[192,1536]{1,0:T(8,128)(2,1)S(1)} %copy-done.2, bf16[104,512]{1,0:T(8,128)(2,1)S(1)} %get-tuple-element.20.refs_1_.refs_2_, bf16[104,512]{1,0:T(8,128)(2,1)S(1)} %get-tuple-element.20.refs_1_.refs_2_, ...), custom_call_target="tpu_custom_call" | custom-call | flops 339738624 | bytes 589824 | tf_op jit(solution)/shard_map/pallas_call | solution.py:186
  19.8 1.6 %collective-permute-done.12.refs_9_.refs_3_ = bf16[104,512]{1,0:T(8,128)(2,1)S(1)} collective-permute-done((bf16[104,512]{1,0:T(8,128)(2,1)S(1)}, bf16[104,512]{1,0:T(8,128)(2,1)S(1)}, u32[]{:S(2)}, u32[]{:S(2)}) %collective-permute-start.12) | collective-permute-done | bytes 106528 | tf_op jit(solution)/shard_map/ppermute | solution.py:386
  21.3 0.9 %shard_map.97.att_ref = bf16[96,1536]{1,0:T(8,128)(2,1)S(1)} custom-call(bf16[192,1536]{1,0:T(8,128)(2,1)S(1)} %copy-done.2, bf16[104,512]{1,0:T(8,128)(2,1)S(1)} %get-tuple-element.20.refs_1_.refs_2_, bf16[104,512]{1,0:T(8,128)(2,1)S(1)} %collective-permute-done.11.refs_8_.refs_2_, bf16[104,512]{1,0:T(8,128)(2,1)S(1)} %collective-permute-done.12.refs_9_.refs_3_, ...), custom_call_target="tpu_custom_call" | custom-call | flops 113246208 | bytes 196608 | tf_op jit(solution)/shard_map/pallas_call | solution.py:186
  22.3 0.9 %project_other.11 = bf16[96,1536]{1,0:T(8,128)(2,1)S(1)} custom-call(bf16[96,1536]{1,0:T(8,128)(2,1)S(1)} %shard_map.97.att_ref, bf16[1536,6144]{1,0:T(8,128)(2,1)S(1)} %copy-done), custom_call_target="tpu_custom_call" | custom-call | flops 452984832 | bytes 4718592 | tf_op jit(solution)/shard_map/project_other/pallas_call | solution.py:224
  23.3 1.0 %collective-permute-start.5 = (bf16[208,512]{1,0:T(8,128)(2,1)S(1)}, bf16[208,512]{1,0:T(8,128)(2,1)S(1)}, u32[]{:S(2)}, u32[]{:S(2)}) collective-permute-start(bf16[208,512]{1,0:T(8,128)(2,1)S(1)} %join.1.refs_10_), channel_id=1, source_target_pairs={{0,16},{4,20},{8,24},{12,28},{16,0},{20,4},{24,8},{28,12},{1,17},{... | collective-permute-start | bytes 638984 | tf_op jit(solution)/shard_map/ppermute | solution.py:383
  24.3 0.9 %project_other.10 = bf16[96,1536]{1,0:T(8,128)(2,1)S(1)} custom-call(bf16[96,1536]{1,0:T(8,128)(2,1)S(1)} %shard_map.97.att_ref, bf16[1536,6144]{1,0:T(8,128)(2,1)S(1)} %copy-done), custom_call_target="tpu_custom_call" | custom-call | flops 452984832 | bytes 4718592 | tf_op jit(solution)/shard_map/project_other/pallas_call | solution.py:224
  25.2 0.3 collective-permute-start.22
  25.4 2.4 %collective-permute-start.13 = (bf16[208,512]{1,0:T(8,128)(2,1)S(1)}, bf16[208,512]{1,0:T(8,128)(2,1)S(1)}, u32[]{:S(2)}, u32[]{:S(2)}) collective-permute-start(bf16[208,512]{1,0:T(8,128)(2,1)S(1)} %join.1.refs_10_), channel_id=1, source_target_pairs={{0,8},{4,12},{8,0},{12,4},{16,24},{20,28},{24,16},{28,20},{1,9},{5... | collective-permute-start | bytes 638984 | tf_op jit(solution)/shard_map/ppermute | solution.py:383
  27.9 8.7 %collective-permute-done.5.refs_11_ = bf16[208,512]{1,0:T(8,128)(2,1)S(1)} collective-permute-done((bf16[208,512]{1,0:T(8,128)(2,1)S(1)}, bf16[208,512]{1,0:T(8,128)(2,1)S(1)}, u32[]{:S(2)}, u32[]{:S(2)}) %collective-permute-start.5) | collective-permute-done | bytes 213024 | tf_op jit(solution)/shard_map/ppermute | solution.py:383
  36.6 1.0 %project_own.3 = bf16[96,1536]{1,0:T(8,128)(2,1)S(1)} custom-call(bf16[96,1536]{1,0:T(8,128)(2,1)S(1)} %shard_map.97.att_ref, bf16[1536,6144]{1,0:T(8,128)(2,1)S(1)} %copy-done, bf16[96,1536]{1,0:T(8,128)(2,1)S(1)} %collective-permute-done.25.rest_0_, bf16[192,1536]{1,0:T(8,128)(2,1)S(1)} %copy-done.1), custom_call_target="tpu_custom_call" | custom-call | flops 452984832 | bytes 4718592 | tf_op jit(solution)/shard_map/project_own/pallas_call | solution.py:224
  37.6 1.6 %collective-permute-start.26 = (bf16[96,1536]{1,0:T(8,128)(2,1)S(1)}, bf16[96,1536]{1,0:T(8,128)(2,1)S(1)}, u32[]{:S(2)}, u32[]{:S(2)}) collective-permute-start(bf16[96,1536]{1,0:T(8,128)(2,1)S(1)} %project_own.3), channel_id=1, source_target_pairs={{0,2},{1,3},{2,0},{3,1},{4,6},{5,7},{6,4},{7,5},{8,10},{9,11},{10,... | collective-permute-start | bytes 884744 | tf_op jit(solution)/shard_map/ppermute | solution.py:389
  39.1 0.5 collective-permute-start.1
  39.6 0.9 %project_other.9.own_ref = bf16[96,1536]{1,0:T(8,128)(2,1)S(1)} custom-call(bf16[96,1536]{1,0:T(8,128)(2,1)S(1)} %shard_map.97.att_ref, bf16[1536,6144]{1,0:T(8,128)(2,1)S(1)} %copy-done), custom_call_target="tpu_custom_call" | custom-call | flops 452984832 | bytes 4718592 | tf_op jit(solution)/shard_map/project_other/pallas_call | solution.py:224
  40.5 5.7 %collective-permute-done.1.refs_2_ = f32[1,1536]{1,0:T(1,128)S(1)} collective-permute-done((f32[1,1536]{1,0:T(1,128)S(1)}, f32[1,1536]{1,0:T(1,128)S(1)}, u32[]{:S(2)}, u32[]{:S(2)}) %collective-permute-start.1) | collective-permute-done | bytes 6176 | tf_op jit(solution)/shard_map/ppermute | solution.py:389
  46.2 0.5 collective-permute-start.2
  46.8 3.3 %shard_map.94 = (f32[256,576]{1,0:T(8,128)S(1)}, f32[2,1,576]{2,1,0:T(1,128)S(1)}, f32[2,1,576]{2,1,0:T(1,128)S(1)}) custom-call(bf16[192,1536]{1,0:T(8,128)(2,1)S(1)} %copy-done.2, bf16[104,512]{1,0:T(8,128)(2,1)S(1)} %get-tuple-element.20.refs_1_.refs_2_, bf16[104,512]{1,0:T(8,128)(2,1)S(1)} %get-tuple-element.20.refs_1_.refs_2_, ...), custom_call_target="tpu_custom_call" | custom-call | flops 792723456 | bytes 1376256 | tf_op jit(solution)/shard_map/pallas_call | solution.py:186
  50.1 0.1 combine.3
  50.2 1.6 %collective-permute-start.23 = (bf16[96,1536]{1,0:T(8,128)(2,1)S(1)}, bf16[96,1536]{1,0:T(8,128)(2,1)S(1)}, u32[]{:S(2)}, u32[]{:S(2)}) collective-permute-start(bf16[96,1536]{1,0:T(8,128)(2,1)S(1)} %combine.3), channel_id=1, source_target_pairs={{0,2},{1,3},{2,0},{3,1},{4,6},{5,7},{6,4},{7,5},{8,10},{9,11},{10,... | collective-permute-start | bytes 884744 | tf_op jit(solution)/shard_map/ppermute | solution.py:389
  51.8 0.9 %shard_map.95.att_ref = bf16[96,1536]{1,0:T(8,128)(2,1)S(1)} custom-call(bf16[192,1536]{1,0:T(8,128)(2,1)S(1)} %copy-done.2, bf16[104,512]{1,0:T(8,128)(2,1)S(1)} %get-tuple-element.20.refs_1_.refs_2_, bf16[208,512]{1,0:T(8,128)(2,1)S(1)} %collective-permute-done.6.refs_2_, f32[256,576]{1,0:T(8,128)S(1)} %get-tuple-element.23.refs_3_, ...), custom_call_target="tpu_custom_call" | custom-call | flops 113246208 | bytes 196608 | tf_op jit(solution)/shard_map/pallas_call | solution.py:186
  52.7 0.9 %project_other.8 = bf16[96,1536]{1,0:T(8,128)(2,1)S(1)} custom-call(bf16[96,1536]{1,0:T(8,128)(2,1)S(1)} %shard_map.95.att_ref, bf16[1536,6144]{1,0:T(8,128)(2,1)S(1)} %copy-done), custom_call_target="tpu_custom_call" | custom-call | flops 452984832 | bytes 4718592 | tf_op jit(solution)/shard_map/project_other/pallas_call | solution.py:224
  53.7 0.9 %project_other.7 = bf16[96,1536]{1,0:T(8,128)(2,1)S(1)} custom-call(bf16[96,1536]{1,0:T(8,128)(2,1)S(1)} %shard_map.95.att_ref, bf16[1536,6144]{1,0:T(8,128)(2,1)S(1)} %copy-done), custom_call_target="tpu_custom_call" | custom-call | flops 452984832 | bytes 4718592 | tf_op jit(solution)/shard_map/project_other/pallas_call | solution.py:224
  54.6 1.1 %project_other.6.own_ref = bf16[96,1536]{1,0:T(8,128)(2,1)S(1)} custom-call(bf16[96,1536]{1,0:T(8,128)(2,1)S(1)} %shard_map.95.att_ref, bf16[1536,6144]{1,0:T(8,128)(2,1)S(1)} %copy-done), custom_call_target="tpu_custom_call" | custom-call | flops 452984832 | bytes 4718592 | tf_op jit(solution)/shard_map/project_other/pallas_call | solution.py:224
  55.7 0.5 collective-permute-start.14
  56.4 0.9 %project_own.2 = (bf16[48,1536]{1,0:T(8,128)(2,1)S(1)}, bf16[48,1536]{1,0:T(8,128)(2,1)S(1)}) custom-call(bf16[96,1536]{1,0:T(8,128)(2,1)S(1)} %shard_map.95.att_ref, bf16[1536,6144]{1,0:T(8,128)(2,1)S(1)} %copy-done, bf16[96,1536]{1,0:T(8,128)(2,1)S(1)} %collective-permute-done.17.rest_0_, bf16[192,1536]{1,0:T(8,128)(2,1)S(1)} %copy-done.1), custom_call_target="tpu_custom_call" | custom-call | flops 452984832 | bytes 4718592 | tf_op jit(solution)/shard_map/project_own/pallas_call | solution.py:224
  57.3 1.8 %collective-permute-done.23 = bf16[96,1536]{1,0:T(8,128)(2,1)S(1)} collective-permute-done((bf16[96,1536]{1,0:T(8,128)(2,1)S(1)}, bf16[96,1536]{1,0:T(8,128)(2,1)S(1)}, u32[]{:S(2)}, u32[]{:S(2)}) %collective-permute-start.23) | collective-permute-done | bytes 294944 | tf_op jit(solution)/shard_map/ppermute | solution.py:389
  59.2 1.5 %collective-permute-start.20 = (bf16[48,1536]{1,0:T(8,128)(2,1)S(1)}, bf16[48,1536]{1,0:T(8,128)(2,1)S(1)}, u32[]{:S(2)}, u32[]{:S(2)}) collective-permute-start(bf16[48,1536]{1,0:T(8,128)(2,1)S(1)} %get-tuple-element.27), channel_id=1, source_target_pairs={{0,2},{1,3},{2,0},{3,1},{4,6},{5,7},{6,4},{7,5},{8,10},{9,11},{10,... | collective-permute-start | bytes 442376 | tf_op jit(solution)/shard_map/ppermute | solution.py:389
  60.8 0.1 combine.2
  61.0 3.3 %collective-permute-done.20 = bf16[48,1536]{1,0:T(8,128)(2,1)S(1)} collective-permute-done((bf16[48,1536]{1,0:T(8,128)(2,1)S(1)}, bf16[48,1536]{1,0:T(8,128)(2,1)S(1)}, u32[]{:S(2)}, u32[]{:S(2)}) %collective-permute-start.20) | collective-permute-done | bytes 147488 | tf_op jit(solution)/shard_map/ppermute | solution.py:389
  64.3 1.5 %collective-permute-start.15 = (bf16[96,1536]{1,0:T(8,128)(2,1)S(1)}, bf16[96,1536]{1,0:T(8,128)(2,1)S(1)}, u32[]{:S(2)}, u32[]{:S(2)}) collective-permute-start(bf16[96,1536]{1,0:T(8,128)(2,1)S(1)} %combine.2), channel_id=1, source_target_pairs={{0,2},{1,3},{2,0},{3,1},{4,6},{5,7},{6,4},{7,5},{8,10},{9,11},{10,... | collective-permute-start | bytes 884744 | tf_op jit(solution)/shard_map/ppermute | solution.py:389
  65.9 5.6 %collective-permute-done.15 = bf16[96,1536]{1,0:T(8,128)(2,1)S(1)} collective-permute-done((bf16[96,1536]{1,0:T(8,128)(2,1)S(1)}, bf16[96,1536]{1,0:T(8,128)(2,1)S(1)}, u32[]{:S(2)}, u32[]{:S(2)}) %collective-permute-start.15) | collective-permute-done | bytes 294944 | tf_op jit(solution)/shard_map/ppermute | solution.py:389
  71.5 1.5 %collective-permute-start.18 = (bf16[48,1536]{1,0:T(8,128)(2,1)S(1)}, bf16[48,1536]{1,0:T(8,128)(2,1)S(1)}, u32[]{:S(2)}, u32[]{:S(2)}) collective-permute-start(bf16[48,1536]{1,0:T(8,128)(2,1)S(1)} %get-tuple-element.26), channel_id=1, source_target_pairs={{0,2},{1,3},{2,0},{3,1},{4,6},{5,7},{6,4},{7,5},{8,10},{9,11},{10,... | collective-permute-start | bytes 442376 | tf_op jit(solution)/shard_map/ppermute | solution.py:389
  73.1 3.6 %collective-permute-done.18 = bf16[48,1536]{1,0:T(8,128)(2,1)S(1)} collective-permute-done((bf16[48,1536]{1,0:T(8,128)(2,1)S(1)}, bf16[48,1536]{1,0:T(8,128)(2,1)S(1)}, u32[]{:S(2)}, u32[]{:S(2)}) %collective-permute-start.18) | collective-permute-done | bytes 147488 | tf_op jit(solution)/shard_map/ppermute | solution.py:389
  76.7 0.6 collective-permute-start.21
  77.4 2.0 %shard_map.98 = (bf16[192,6144]{1,0:T(8,128)(2,1)}, f32[1,192]{1,0:T(1,128)S(1)}, bf16[192,1536]{1,0:T(8,128)(2,1)}) custom-call(f32[1,1536]{1,0:T(1,128)S(1)} %copy-done.3, f32[1,1536]{1,0:T(1,128)S(1)} %collective-permute-done.refs_1_, f32[1,1536]{1,0:T(1,128)S(1)} %collective-permute-done.1.refs_2_, f32[1,1536]{1,0:T(1,128)S(1)} %collective-permute-done.2.refs_3_, ...), custom_call_target="tpu_custom_call" | custom-call | flops 2000000000 | bytes 2359296 | tf_op jit(solution)/shard_map/pallas_call | solution.py:344
  79.4 1.3 %shard_map.99 = (bf16[192,6144]{1,0:T(8,128)(2,1)}, f32[1,192]{1,0:T(1,128)S(1)}, bf16[192,1536]{1,0:T(8,128)(2,1)}) custom-call(f32[1,1536]{1,0:T(1,128)S(1)} %copy-done.3, f32[1,1536]{1,0:T(1,128)S(1)} %collective-permute-done.refs_1_, f32[1,1536]{1,0:T(1,128)S(1)} %collective-permute-done.1.refs_2_, ...), custom_call_target="tpu_custom_call", output_to_operand_aliasing={{0}: (9, {}), {2}: (10, {})} | custom-call | flops 2000000000 | bytes 1179648 | tf_op jit(solution)/shard_map/pallas_call | solution.py:344
  80.7 1.3 %shard_map.100 = (bf16[192,6144]{1,0:T(8,128)(2,1)}, f32[192]{0:T(256)}, bf16[192,1536]{1,0:T(8,128)(2,1)}) custom-call(f32[1,1536]{1,0:T(1,128)S(1)} %copy-done.3, f32[1,1536]{1,0:T(1,128)S(1)} %collective-permute-done.refs_1_, f32[1,1536]{1,0:T(1,128)S(1)} %collective-permute-done.1.refs_2_, ...), custom_call_target="tpu_custom_call", output_to_operand_aliasing={{0}: (9, {}), {2}: (10, {})} | custom-call | flops 2000000000 | bytes 1179648 | tf_op jit(solution)/shard_map/pallas_call | solution.py:344
  (41 shorter events, 0.8 us)
Async XLA Ops:
  0.6 17.6 %copy-start.2 = (bf16[192,1536]{1,0:T(8,128)(2,1)S(1)}, bf16[192,1536]{1,0:T(8,128)(2,1)}, u32[]{:S(2)}) copy-start(bf16[192,1536]{1,0:T(8,128)(2,1)} %refs_0_.10) | copy-start | bytes 1769476
  0.6 21.6 %copy-start = (bf16[1536,6144]{1,0:T(8,128)(2,1)S(1)}, bf16[1536,6144]{1,0:T(8,128)(2,1)}, u32[]{:S(2)}) copy-start(bf16[1536,6144]{1,0:T(8,128)(2,1)} %weight_ref.15) | copy-start | bytes 56623108
  1.7 9.0 %collective-permute-start.3 = (bf16[104,512]{1,0:T(8,128)(2,1)S(1)}, bf16[104,512]{1,0:T(8,128)(2,1)S(1)}, u32[]{:S(2)}, u32[]{:S(2)}) collective-permute-start(bf16[104,512]{1,0:T(8,128)(2,1)S(1)} %get-tuple-element.20.refs_1_.refs_2_), channel_id=1, source_target_pairs={{0,24},{4,28},{8,16},{12,20},{16,8},{20,12},{24,0},{28,4},{1,25},{... | collective-permute-start | bytes 319496 | tf_op jit(solution)/shard_map/ppermute | solution.py:383
  6.9 6.3 %collective-permute-start.9 = (bf16[104,512]{1,0:T(8,128)(2,1)S(1)}, bf16[104,512]{1,0:T(8,128)(2,1)S(1)}, u32[]{:S(2)}, u32[]{:S(2)}) collective-permute-start(bf16[104,512]{1,0:T(8,128)(2,1)S(1)} %get-tuple-element.20.refs_1_.refs_2_), channel_id=1, source_target_pairs={{0,8},{4,12},{8,0},{12,4},{16,24},{20,28},{24,16},{28,20},{1,9},{5... | collective-permute-start | bytes 319496 | tf_op jit(solution)/shard_map/ppermute | solution.py:383
  6.9 9.0 %collective-permute-start.11 = (bf16[104,512]{1,0:T(8,128)(2,1)S(1)}, bf16[104,512]{1,0:T(8,128)(2,1)S(1)}, u32[]{:S(2)}, u32[]{:S(2)}) collective-permute-start(bf16[104,512]{1,0:T(8,128)(2,1)S(1)} %get-tuple-element.20.refs_1_.refs_2_), channel_id=1, source_target_pairs={{0,16},{4,20},{8,24},{12,28},{16,0},{20,4},{24,8},{28,12},{1,17},{... | collective-permute-start | bytes 319496 | tf_op jit(solution)/shard_map/ppermute | solution.py:383
  7.5 10.4 %collective-permute-start.7 = (bf16[104,512]{1,0:T(8,128)(2,1)S(1)}, bf16[104,512]{1,0:T(8,128)(2,1)S(1)}, u32[]{:S(2)}, u32[]{:S(2)}) collective-permute-start(bf16[104,512]{1,0:T(8,128)(2,1)S(1)} %get-tuple-element.20.refs_1_.refs_2_), channel_id=1, source_target_pairs={{0,4},{4,0},{8,12},{12,8},{16,20},{20,16},{24,28},{28,24},{1,5},{5... | collective-permute-start | bytes 319496 | tf_op jit(solution)/shard_map/ppermute | solution.py:386
  10.7 7.1 %collective-permute-start.8 = (bf16[104,512]{1,0:T(8,128)(2,1)S(1)}, bf16[104,512]{1,0:T(8,128)(2,1)S(1)}, u32[]{:S(2)}, u32[]{:S(2)}) collective-permute-start(bf16[104,512]{1,0:T(8,128)(2,1)S(1)} %collective-permute-done.3.refs_4_), channel_id=1, source_target_pairs={{0,4},{4,0},{8,12},{12,8},{16,20},{20,16},{24,28},{28,24},{1,5},{5... | collective-permute-start | bytes 319496 | tf_op jit(solution)/shard_map/ppermute | solution.py:386
  13.2 5.0 %collective-permute-start.10 = (bf16[104,512]{1,0:T(8,128)(2,1)S(1)}, bf16[104,512]{1,0:T(8,128)(2,1)S(1)}, u32[]{:S(2)}, u32[]{:S(2)}) collective-permute-start(bf16[104,512]{1,0:T(8,128)(2,1)S(1)} %collective-permute-done.9.refs_6_), channel_id=1, source_target_pairs={{0,4},{4,0},{8,12},{12,8},{16,20},{20,16},{24,28},{28,24},{1,5},{5... | collective-permute-start | bytes 319496 | tf_op jit(solution)/shard_map/ppermute | solution.py:386
  15.8 5.5 %collective-permute-start.12 = (bf16[104,512]{1,0:T(8,128)(2,1)S(1)}, bf16[104,512]{1,0:T(8,128)(2,1)S(1)}, u32[]{:S(2)}, u32[]{:S(2)}) collective-permute-start(bf16[104,512]{1,0:T(8,128)(2,1)S(1)} %collective-permute-done.11.refs_8_.refs_2_), channel_id=1, source_target_pairs={{0,4},{4,0},{8,12},{12,8},{16,20},{20,16},{24,28},{28,24},{1,5},{5... | collective-permute-start | bytes 319496 | tf_op jit(solution)/shard_map/ppermute | solution.py:386
  17.3 5.9 %collective-permute-start.4 = (bf16[104,512]{1,0:T(8,128)(2,1)S(1)}, bf16[104,512]{1,0:T(8,128)(2,1)S(1)}, u32[]{:S(2)}, u32[]{:S(2)}) collective-permute-start(bf16[104,512]{1,0:T(8,128)(2,1)S(1)} %get-tuple-element.22.refs_0_), channel_id=1, source_target_pairs={{0,4},{4,0},{8,12},{12,8},{16,20},{20,16},{24,28},{28,24},{1,5},{5... | collective-permute-start | bytes 319496 | tf_op jit(solution)/shard_map/ppermute | solution.py:386
  23.2 13.4 %collective-permute-start.25 = (bf16[96,1536]{1,0:T(8,128)(2,1)S(1)}, bf16[96,1536]{1,0:T(8,128)(2,1)S(1)}, u32[]{:S(2)}, u32[]{:S(2)}) collective-permute-start(bf16[96,1536]{1,0:T(8,128)(2,1)S(1)} %project_other.11), channel_id=1, source_target_pairs={{0,1},{1,0},{2,3},{3,2},{4,5},{5,4},{6,7},{7,6},{8,9},{9,8},{10,11... | collective-permute-start | bytes 884744 | tf_op jit(solution)/shard_map/ppermute | solution.py:392
  23.3 13.3 %copy-start.1 = (bf16[192,1536]{1,0:T(8,128)(2,1)S(1)}, bf16[192,1536]{1,0:T(8,128)(2,1)}, u32[]{:S(2)}) copy-start(bf16[192,1536]{1,0:T(8,128)(2,1)} %rest_1_.3) | copy-start | bytes 1769476
  23.3 13.3 %collective-permute-start.5 = (bf16[208,512]{1,0:T(8,128)(2,1)S(1)}, bf16[208,512]{1,0:T(8,128)(2,1)S(1)}, u32[]{:S(2)}, u32[]{:S(2)}) collective-permute-start(bf16[208,512]{1,0:T(8,128)(2,1)S(1)} %join.1.refs_10_), channel_id=1, source_target_pairs={{0,16},{4,20},{8,24},{12,28},{16,0},{20,4},{24,8},{28,12},{1,17},{... | collective-permute-start | bytes 638984 | tf_op jit(solution)/shard_map/ppermute | solution.py:383
  25.2 14.0 %copy-start.3 = (f32[1,1536]{1,0:T(1,128)S(1)}, f32[1,1536]{1,0:T(1,128)}, u32[]{:S(2)}) copy-start(f32[1,1536]{1,0:T(1,128)} %refs_0_.13) | copy-start | bytes 18436
  25.2 24.9 %collective-permute-start.22 = (bf16[96,1536]{1,0:T(8,128)(2,1)S(1)}, bf16[96,1536]{1,0:T(8,128)(2,1)S(1)}, u32[]{:S(2)}, u32[]{:S(2)}) collective-permute-start(bf16[96,1536]{1,0:T(8,128)(2,1)S(1)} %project_other.10), channel_id=1, source_target_pairs={{0,1},{1,0},{2,3},{3,2},{4,5},{5,4},{6,7},{7,6},{8,9},{9,8},{10,11... | collective-permute-start | bytes 884744 | tf_op jit(solution)/shard_map/ppermute | solution.py:392
  25.4 20.8 %collective-permute-start.13 = (bf16[208,512]{1,0:T(8,128)(2,1)S(1)}, bf16[208,512]{1,0:T(8,128)(2,1)S(1)}, u32[]{:S(2)}, u32[]{:S(2)}) collective-permute-start(bf16[208,512]{1,0:T(8,128)(2,1)S(1)} %join.1.refs_10_), channel_id=1, source_target_pairs={{0,8},{4,12},{8,0},{12,4},{16,24},{20,28},{24,16},{28,20},{1,9},{5... | collective-permute-start | bytes 638984 | tf_op jit(solution)/shard_map/ppermute | solution.py:383
  36.6 15.2 %collective-permute-start.6 = (bf16[208,512]{1,0:T(8,128)(2,1)S(1)}, bf16[208,512]{1,0:T(8,128)(2,1)S(1)}, u32[]{:S(2)}, u32[]{:S(2)}) collective-permute-start(bf16[208,512]{1,0:T(8,128)(2,1)S(1)} %collective-permute-done.5.refs_11_), channel_id=1, source_target_pairs={{0,8},{4,12},{8,0},{12,4},{16,24},{20,28},{24,16},{28,20},{1,9},{5... | collective-permute-start | bytes 638984 | tf_op jit(solution)/shard_map/ppermute | solution.py:383
  37.6 18.1 %collective-permute-start.26 = (bf16[96,1536]{1,0:T(8,128)(2,1)S(1)}, bf16[96,1536]{1,0:T(8,128)(2,1)S(1)}, u32[]{:S(2)}, u32[]{:S(2)}) collective-permute-start(bf16[96,1536]{1,0:T(8,128)(2,1)S(1)} %project_own.3), channel_id=1, source_target_pairs={{0,2},{1,3},{2,0},{3,1},{4,6},{5,7},{6,4},{7,5},{8,10},{9,11},{10,... | collective-permute-start | bytes 884744 | tf_op jit(solution)/shard_map/ppermute | solution.py:389
  39.1 7.1 %collective-permute-start.1 = (f32[1,1536]{1,0:T(1,128)S(1)}, f32[1,1536]{1,0:T(1,128)S(1)}, u32[]{:S(2)}, u32[]{:S(2)}) collective-permute-start(f32[1,1536]{1,0:T(1,128)S(1)} %copy-done.3), channel_id=1, source_target_pairs={{0,2},{1,3},{2,0},{3,1},{4,6},{5,7},{6,4},{7,5},{8,10},{9,11},{10,... | collective-permute-start | bytes 18440 | tf_op jit(solution)/shard_map/ppermute | solution.py:389
  46.2 30.4 %collective-permute-start = (f32[1,1536]{1,0:T(1,128)S(1)}, f32[1,1536]{1,0:T(1,128)S(1)}, u32[]{:S(2)}, u32[]{:S(2)}) collective-permute-start(f32[1,1536]{1,0:T(1,128)S(1)} %copy-done.3), channel_id=1, source_target_pairs={{0,1},{1,0},{2,3},{3,2},{4,5},{5,4},{6,7},{7,6},{8,9},{9,8},{10,11... | collective-permute-start | bytes 18440 | tf_op jit(solution)/shard_map/ppermute | solution.py:392
  46.2 31.0 %collective-permute-start.2 = (f32[1,1536]{1,0:T(1,128)S(1)}, f32[1,1536]{1,0:T(1,128)S(1)}, u32[]{:S(2)}, u32[]{:S(2)}) collective-permute-start(f32[1,1536]{1,0:T(1,128)S(1)} %collective-permute-done.1.refs_2_), channel_id=1, source_target_pairs={{0,1},{1,0},{2,3},{3,2},{4,5},{5,4},{6,7},{7,6},{8,9},{9,8},{10,11... | collective-permute-start | bytes 18440 | tf_op jit(solution)/shard_map/ppermute | solution.py:392
  50.2 9.0 %collective-permute-start.23 = (bf16[96,1536]{1,0:T(8,128)(2,1)S(1)}, bf16[96,1536]{1,0:T(8,128)(2,1)S(1)}, u32[]{:S(2)}, u32[]{:S(2)}) collective-permute-start(bf16[96,1536]{1,0:T(8,128)(2,1)S(1)} %combine.3), channel_id=1, source_target_pairs={{0,2},{1,3},{2,0},{3,1},{4,6},{5,7},{6,4},{7,5},{8,10},{9,11},{10,... | collective-permute-start | bytes 884744 | tf_op jit(solution)/shard_map/ppermute | solution.py:389
  53.6 2.7 %collective-permute-start.17 = (bf16[96,1536]{1,0:T(8,128)(2,1)S(1)}, bf16[96,1536]{1,0:T(8,128)(2,1)S(1)}, u32[]{:S(2)}, u32[]{:S(2)}) collective-permute-start(bf16[96,1536]{1,0:T(8,128)(2,1)S(1)} %project_other.8), channel_id=1, source_target_pairs={{0,1},{1,0},{2,3},{3,2},{4,5},{5,4},{6,7},{7,6},{8,9},{9,8},{10,11... | collective-permute-start | bytes 884744 | tf_op jit(solution)/shard_map/ppermute | solution.py:392
  55.7 5.1 %collective-permute-start.14 = (bf16[96,1536]{1,0:T(8,128)(2,1)S(1)}, bf16[96,1536]{1,0:T(8,128)(2,1)S(1)}, u32[]{:S(2)}, u32[]{:S(2)}) collective-permute-start(bf16[96,1536]{1,0:T(8,128)(2,1)S(1)} %project_other.7), channel_id=1, source_target_pairs={{0,1},{1,0},{2,3},{3,2},{4,5},{5,4},{6,7},{7,6},{8,9},{9,8},{10,11... | collective-permute-start | bytes 884744 | tf_op jit(solution)/shard_map/ppermute | solution.py:392
  56.3 21.1 %collective-permute-start.27 = (bf16[96,1536]{1,0:T(8,128)(2,1)S(1)}, bf16[96,1536]{1,0:T(8,128)(2,1)S(1)}, u32[]{:S(2)}, u32[]{:S(2)}) collective-permute-start(bf16[96,1536]{1,0:T(8,128)(2,1)S(1)} %add_convert_fusion.refs_6_), channel_id=1, source_target_pairs={{0,1},{1,0},{2,3},{3,2},{4,5},{5,4},{6,7},{7,6},{8,9},{9,8},{10,11... | collective-permute-start | bytes 884744 | tf_op jit(solution)/shard_map/ppermute | solution.py:392
  59.2 5.1 %collective-permute-start.20 = (bf16[48,1536]{1,0:T(8,128)(2,1)S(1)}, bf16[48,1536]{1,0:T(8,128)(2,1)S(1)}, u32[]{:S(2)}, u32[]{:S(2)}) collective-permute-start(bf16[48,1536]{1,0:T(8,128)(2,1)S(1)} %get-tuple-element.27), channel_id=1, source_target_pairs={{0,2},{1,3},{2,0},{3,1},{4,6},{5,7},{6,4},{7,5},{8,10},{9,11},{10,... | collective-permute-start | bytes 442376 | tf_op jit(solution)/shard_map/ppermute | solution.py:389
  60.8 16.6 %collective-permute-start.24 = (bf16[96,1536]{1,0:T(8,128)(2,1)S(1)}, bf16[96,1536]{1,0:T(8,128)(2,1)S(1)}, u32[]{:S(2)}, u32[]{:S(2)}) collective-permute-start(bf16[96,1536]{1,0:T(8,128)(2,1)S(1)} %add_convert_fusion.1.refs_4_), channel_id=1, source_target_pairs={{0,1},{1,0},{2,3},{3,2},{4,5},{5,4},{6,7},{7,6},{8,9},{9,8},{10,11... | collective-permute-start | bytes 884744 | tf_op jit(solution)/shard_map/ppermute | solution.py:392
  64.3 7.2 %collective-permute-start.15 = (bf16[96,1536]{1,0:T(8,128)(2,1)S(1)}, bf16[96,1536]{1,0:T(8,128)(2,1)S(1)}, u32[]{:S(2)}, u32[]{:S(2)}) collective-permute-start(bf16[96,1536]{1,0:T(8,128)(2,1)S(1)} %combine.2), channel_id=1, source_target_pairs={{0,2},{1,3},{2,0},{3,1},{4,6},{5,7},{6,4},{7,5},{8,10},{9,11},{10,... | collective-permute-start | bytes 884744 | tf_op jit(solution)/shard_map/ppermute | solution.py:389
  71.5 5.1 %collective-permute-start.18 = (bf16[48,1536]{1,0:T(8,128)(2,1)S(1)}, bf16[48,1536]{1,0:T(8,128)(2,1)S(1)}, u32[]{:S(2)}, u32[]{:S(2)}) collective-permute-start(bf16[48,1536]{1,0:T(8,128)(2,1)S(1)} %get-tuple-element.26), channel_id=1, source_target_pairs={{0,2},{1,3},{2,0},{3,1},{4,6},{5,7},{6,4},{7,5},{8,10},{9,11},{10,... | collective-permute-start | bytes 442376 | tf_op jit(solution)/shard_map/ppermute | solution.py:389
  76.6 2.8 %collective-permute-start.16 = (bf16[96,1536]{1,0:T(8,128)(2,1)S(1)}, bf16[96,1536]{1,0:T(8,128)(2,1)S(1)}, u32[]{:S(2)}, u32[]{:S(2)}) collective-permute-start(bf16[96,1536]{1,0:T(8,128)(2,1)S(1)} %add_convert_fusion.2.refs_4_), channel_id=1, source_target_pairs={{0,1},{1,0},{2,3},{3,2},{4,5},{5,4},{6,7},{7,6},{8,9},{9,8},{10,11... | collective-permute-start | bytes 884744 | tf_op jit(solution)/shard_map/ppermute | solution.py:392
  76.7 2.7 %collective-permute-start.21 = (bf16[48,1536]{1,0:T(8,128)(2,1)S(1)}, bf16[48,1536]{1,0:T(8,128)(2,1)S(1)}, u32[]{:S(2)}, u32[]{:S(2)}) collective-permute-start(bf16[48,1536]{1,0:T(8,128)(2,1)S(1)} %add_convert_fusion.3.refs_6_), channel_id=1, source_target_pairs={{0,1},{1,0},{2,3},{3,2},{4,5},{5,4},{6,7},{7,6},{8,9},{9,8},{10,11... | collective-permute-start | bytes 442376 | tf_op jit(solution)/shard_map/ppermute | solution.py:392
  77.3 3.5 %collective-permute-start.19 = (bf16[48,1536]{1,0:T(8,128)(2,1)S(1)}, bf16[48,1536]{1,0:T(8,128)(2,1)S(1)}, u32[]{:S(2)}, u32[]{:S(2)}) collective-permute-start(bf16[48,1536]{1,0:T(8,128)(2,1)S(1)} %add_convert_fusion.4.refs_6_), channel_id=1, source_target_pairs={{0,1},{1,0},{2,3},{3,2},{4,5},{5,4},{6,7},{7,6},{8,9},{9,8},{10,11... | collective-permute-start | bytes 442376 | tf_op jit(solution)/shard_map/ppermute | solution.py:392

commit v4 on v3

--- a/solution.py
+++ b/solution.py
@@ -191,6 +191,7 @@
         scratch_shapes=[VMEM((total, 2 * kv_width), BF16)],
         compiler_params=grant(20),
         cost_estimate=cost(4 * run_rows * total * width, total * pieces[0].shape[1] * 2),
+        name="attend",
     )(*[near(operand) for operand in operands])
 
 
@@ -228,7 +229,7 @@
         out_specs=(in_vmem(),) * len(cuts),
         compiler_params=grant(8),
         cost_estimate=cost(2 * rows * depth * width, depth * width * 2),
-        name="project_own" if own else "project_other",
+        name="project",
     )(*[near(operand) for operand in operands])
     return result if own else result[0]
 
@@ -355,6 +356,7 @@
         input_output_aliases=aliases,
         compiler_params=grant(8),
         cost_estimate=cost(2e9, 4 * rows * blocks * width),
+        name="finish",
     )(*operands)
 
 
@@ -411,8 +413,8 @@
                 high_pieces.append(move_z(held, step))
         step //= 2
 
-    begun = attend(queries, 0, low, [low_pieces[:-nx]], None, False)
-    early = attend(queries, 0, low, [low_pieces[-nx:]], begun)
+    begun = attend(queries, 0, low, [low_pieces[: nx + 1]], None, False)
+    early = attend(queries, 0, low, [low_pieces[nx + 1 :]], begun)
     parts = []
     for yb in range(ny):
         other = project(cores, [yb], 0, 1, early, out_weight, block_width)

time: 82.4 us -> 82.9 us (level)
  transfers between devices with their start and end apart: 28 -> 28, of which waited for: 11 -> 10; matrix products, arithmetic and copies ran while one was open for 0% -> 0% of each run, Pallas kernels for 22% -> 21%
where the time goes in v4:
time: 82.9 us; the launch traced here: 82.7 us
  waiting for transfers between devices  34.9 us (42%)
  starting transfers between devices  26.3 us (32%)
  Pallas kernels  20.1 us (24%)
  between operations  1.11 us (1%)
    ppermute x6, waiting for transfers between devices, move_y(): return lax.ppermute(array, 'tp', swap(ny, n_tp, cores, k))  20.1 us
    ppermute x6, waiting for transfers between devices, move_z(): return lax.ppermute(array, 'seq', swap(nz, n_seq, nx, k))  12.4 us
    ppermute x6, starting transfers between devices, move_z(): return lax.ppermute(array, 'seq', swap(nz, n_seq, nx, k))  9.17 us
    ppermute x6, starting transfers between devices, move_y(): return lax.ppermute(array, 'tp', swap(ny, n_tp, cores, k))  8.16 us
    pallas_call x8, Pallas kernels, project(): pl.pallas_call(functools.partial(project_body, cores, blocks, half, dista...  7.4 us
    ppermute x5, starting transfers between devices, move_x(): return lax.ppermute(array, 'seq', swap(nx, n_seq, 1, k))  6.71 us
    pallas_call x4, Pallas kernels, attend(): pl.pallas_call(functools.partial(attend_body, run_rows, query_half, key_h...  6.68 us
    pallas_call x3, Pallas kernels, finish(): pl.pallas_call(functools.partial(finish_body, ny, cores, row, rows, place...  4.65 us
  transfers between devices with their start and end apart: 28, of which 10 were waited for; matrix products, arithmetic and copies ran while one was open for 0% of the time, Pallas kernels for 21%

profile of v4, /device:TPU:0, one launch (start us, length us, event | category | flops | bytes accessed | tf_op | source)
XLA Modules:
  0.0 82.7 jit_solution(4098526855798655151)
XLA Ops:
  0.7 1.1 %pack.1 = (bf16[104,512]{1,0:T(8,128)(2,1)S(1)}, bf16[104,512]{1,0:T(8,128)(2,1)S(1)}) custom-call(s32[192]{0:T(256)} %pos_ref.1, bf16[192,256]{1,0:T(8,128)(2,1)} %key_ref.1, bf16[192,256]{1,0:T(8,128)(2,1)} %value_ref.1), custom_call_target="tpu_custom_call" | custom-call | flops 40000000000 | bytes 393216 | tf_op jit(solution)/shard_map/pack/pallas_call | solution.py:70
  1.7 5.1 %collective-permute-start.3 = (bf16[104,512]{1,0:T(8,128)(2,1)S(1)}, bf16[104,512]{1,0:T(8,128)(2,1)S(1)}, u32[]{:S(2)}, u32[]{:S(2)}) collective-permute-start(bf16[104,512]{1,0:T(8,128)(2,1)S(1)} %get-tuple-element.20.refs_1_.refs_2_), channel_id=1, source_target_pairs={{0,24},{4,28},{8,16},{12,20},{16,8},{20,12},{24,0},{28,4},{1,25},{... | collective-permute-start | bytes 319496 | tf_op jit(solution)/shard_map/ppermute | solution.py:385
  6.9 0.6 collective-permute-start.11
  7.5 1.6 %collective-permute-start.7 = (bf16[104,512]{1,0:T(8,128)(2,1)S(1)}, bf16[104,512]{1,0:T(8,128)(2,1)S(1)}, u32[]{:S(2)}, u32[]{:S(2)}) collective-permute-start(bf16[104,512]{1,0:T(8,128)(2,1)S(1)} %get-tuple-element.20.refs_1_.refs_2_), channel_id=1, source_target_pairs={{0,4},{4,0},{8,12},{12,8},{16,20},{20,16},{24,28},{28,24},{1,5},{5... | collective-permute-start | bytes 319496 | tf_op jit(solution)/shard_map/ppermute | solution.py:388
  9.1 1.6 %collective-permute-done.3.refs_4_ = bf16[104,512]{1,0:T(8,128)(2,1)S(1)} collective-permute-done((bf16[104,512]{1,0:T(8,128)(2,1)S(1)}, bf16[104,512]{1,0:T(8,128)(2,1)S(1)}, u32[]{:S(2)}, u32[]{:S(2)}) %collective-permute-start.3) | collective-permute-done | bytes 106528 | tf_op jit(solution)/shard_map/ppermute | solution.py:385
  10.7 1.7 %collective-permute-start.8 = (bf16[104,512]{1,0:T(8,128)(2,1)S(1)}, bf16[104,512]{1,0:T(8,128)(2,1)S(1)}, u32[]{:S(2)}, u32[]{:S(2)}) collective-permute-start(bf16[104,512]{1,0:T(8,128)(2,1)S(1)} %collective-permute-done.3.refs_4_), channel_id=1, source_target_pairs={{0,4},{4,0},{8,12},{12,8},{16,20},{20,16},{24,28},{28,24},{1,5},{5... | collective-permute-start | bytes 319496 | tf_op jit(solution)/shard_map/ppermute | solution.py:388
  12.4 0.8 collective-permute-done.9.refs_6_.refs_3_
  13.2 1.4 %collective-permute-start.10 = (bf16[104,512]{1,0:T(8,128)(2,1)S(1)}, bf16[104,512]{1,0:T(8,128)(2,1)S(1)}, u32[]{:S(2)}, u32[]{:S(2)}) collective-permute-start(bf16[104,512]{1,0:T(8,128)(2,1)S(1)} %collective-permute-done.9.refs_6_.refs_3_), channel_id=1, source_target_pairs={{0,4},{4,0},{8,12},{12,8},{16,20},{20,16},{24,28},{28,24},{1,5},{5... | collective-permute-start | bytes 319496 | tf_op jit(solution)/shard_map/ppermute | solution.py:388
  14.6 1.2 %collective-permute-done.11.refs_8_.refs_5_ = bf16[104,512]{1,0:T(8,128)(2,1)S(1)} collective-permute-done((bf16[104,512]{1,0:T(8,128)(2,1)S(1)}, bf16[104,512]{1,0:T(8,128)(2,1)S(1)}, u32[]{:S(2)}, u32[]{:S(2)}) %collective-permute-start.11) | collective-permute-done | bytes 106528 | tf_op jit(solution)/shard_map/ppermute | solution.py:385
  15.8 1.5 %collective-permute-start.12 = (bf16[104,512]{1,0:T(8,128)(2,1)S(1)}, bf16[104,512]{1,0:T(8,128)(2,1)S(1)}, u32[]{:S(2)}, u32[]{:S(2)}) collective-permute-start(bf16[104,512]{1,0:T(8,128)(2,1)S(1)} %collective-permute-done.11.refs_8_.refs_5_), channel_id=1, source_target_pairs={{0,4},{4,0},{8,12},{12,8},{16,20},{20,16},{24,28},{28,24},{1,5},{5... | collective-permute-start | bytes 319496 | tf_op jit(solution)/shard_map/ppermute | solution.py:388
  17.3 0.5 collective-permute-start.4
  17.9 1.1 %attend.6 = (f32[256,576]{1,0:T(8,128)S(1)}, f32[2,1,576]{2,1,0:T(1,128)S(1)}, f32[2,1,576]{2,1,0:T(1,128)S(1)}) custom-call(bf16[192,1536]{1,0:T(8,128)(2,1)S(1)} %copy-done.2, bf16[104,512]{1,0:T(8,128)(2,1)S(1)} %get-tuple-element.20.refs_1_.refs_2_, bf16[104,512]{1,0:T(8,128)(2,1)S(1)} %get-tuple-element.20.refs_1_.refs_2_, ...), custom_call_target="tpu_custom_call" | custom-call | flops 169869312 | bytes 294912 | tf_op jit(solution)/shard_map/attend/pallas_call | solution.py:186
  19.0 2.4 %collective-permute-done.12.refs_9_.refs_6_ = bf16[104,512]{1,0:T(8,128)(2,1)S(1)} collective-permute-done((bf16[104,512]{1,0:T(8,128)(2,1)S(1)}, bf16[104,512]{1,0:T(8,128)(2,1)S(1)}, u32[]{:S(2)}, u32[]{:S(2)}) %collective-permute-start.12) | collective-permute-done | bytes 106528 | tf_op jit(solution)/shard_map/ppermute | solution.py:388
  21.3 1.4 %attend.7.att_ref = bf16[96,1536]{1,0:T(8,128)(2,1)S(1)} custom-call(bf16[192,1536]{1,0:T(8,128)(2,1)S(1)} %copy-done.2, bf16[104,512]{1,0:T(8,128)(2,1)S(1)} %get-tuple-element.20.refs_1_.refs_2_, bf16[104,512]{1,0:T(8,128)(2,1)S(1)} %collective-permute-done.8.refs_5_.refs_2_, bf16[104,512]{1,0:T(8,128)(2,1)S(1)} %collective-permute-done.9.refs_6_.refs_3_, ...), custom_call_target="tpu_custom_call" | custom-call | flops 283115520 | bytes 491520 | tf_op jit(solution)/shard_map/attend/pallas_call | solution.py:186
  22.8 0.9 %project.14 = bf16[96,1536]{1,0:T(8,128)(2,1)S(1)} custom-call(bf16[96,1536]{1,0:T(8,128)(2,1)S(1)} %attend.7.att_ref, bf16[1536,6144]{1,0:T(8,128)(2,1)S(1)} %copy-done), custom_call_target="tpu_custom_call" | custom-call | flops 452984832 | bytes 4718592 | tf_op jit(solution)/shard_map/project/pallas_call | solution.py:225
  23.8 1.0 %collective-permute-start.5 = (bf16[208,512]{1,0:T(8,128)(2,1)S(1)}, bf16[208,512]{1,0:T(8,128)(2,1)S(1)}, u32[]{:S(2)}, u32[]{:S(2)}) collective-permute-start(bf16[208,512]{1,0:T(8,128)(2,1)S(1)} %join.1.refs_10_), channel_id=1, source_target_pairs={{0,16},{4,20},{8,24},{12,28},{16,0},{20,4},{24,8},{28,12},{1,17},{... | collective-permute-start | bytes 638984 | tf_op jit(solution)/shard_map/ppermute | solution.py:385
  24.8 0.9 %project.13 = bf16[96,1536]{1,0:T(8,128)(2,1)S(1)} custom-call(bf16[96,1536]{1,0:T(8,128)(2,1)S(1)} %attend.7.att_ref, bf16[1536,6144]{1,0:T(8,128)(2,1)S(1)} %copy-done), custom_call_target="tpu_custom_call" | custom-call | flops 452984832 | bytes 4718592 | tf_op jit(solution)/shard_map/project/pallas_call | solution.py:225
  25.7 0.3 collective-permute-start.22
  25.9 2.4 %collective-permute-start.13 = (bf16[208,512]{1,0:T(8,128)(2,1)S(1)}, bf16[208,512]{1,0:T(8,128)(2,1)S(1)}, u32[]{:S(2)}, u32[]{:S(2)}) collective-permute-start(bf16[208,512]{1,0:T(8,128)(2,1)S(1)} %join.1.refs_10_), channel_id=1, source_target_pairs={{0,8},{4,12},{8,0},{12,4},{16,24},{20,28},{24,16},{28,20},{1,9},{5... | collective-permute-start | bytes 638984 | tf_op jit(solution)/shard_map/ppermute | solution.py:385
  28.4 8.7 %collective-permute-done.5.refs_11_ = bf16[208,512]{1,0:T(8,128)(2,1)S(1)} collective-permute-done((bf16[208,512]{1,0:T(8,128)(2,1)S(1)}, bf16[208,512]{1,0:T(8,128)(2,1)S(1)}, u32[]{:S(2)}, u32[]{:S(2)}) %collective-permute-start.5) | collective-permute-done | bytes 213024 | tf_op jit(solution)/shard_map/ppermute | solution.py:385
  37.1 0.9 %project.15 = bf16[96,1536]{1,0:T(8,128)(2,1)S(1)} custom-call(bf16[96,1536]{1,0:T(8,128)(2,1)S(1)} %attend.7.att_ref, bf16[1536,6144]{1,0:T(8,128)(2,1)S(1)} %copy-done, bf16[96,1536]{1,0:T(8,128)(2,1)S(1)} %collective-permute-done.25.rest_0_, bf16[192,1536]{1,0:T(8,128)(2,1)S(1)} %copy-done.1), custom_call_target="tpu_custom_call" | custom-call | flops 452984832 | bytes 4718592 | tf_op jit(solution)/shard_map/project/pallas_call | solution.py:225
  38.0 1.6 %collective-permute-start.26 = (bf16[96,1536]{1,0:T(8,128)(2,1)S(1)}, bf16[96,1536]{1,0:T(8,128)(2,1)S(1)}, u32[]{:S(2)}, u32[]{:S(2)}) collective-permute-start(bf16[96,1536]{1,0:T(8,128)(2,1)S(1)} %project.15), channel_id=1, source_target_pairs={{0,2},{1,3},{2,0},{3,1},{4,6},{5,7},{6,4},{7,5},{8,10},{9,11},{10,... | collective-permute-start | bytes 884744 | tf_op jit(solution)/shard_map/ppermute | solution.py:391
  39.6 0.5 collective-permute-start.1
  40.1 0.9 %project.12.own_ref = bf16[96,1536]{1,0:T(8,128)(2,1)S(1)} custom-call(bf16[96,1536]{1,0:T(8,128)(2,1)S(1)} %attend.7.att_ref, bf16[1536,6144]{1,0:T(8,128)(2,1)S(1)} %copy-done), custom_call_target="tpu_custom_call" | custom-call | flops 452984832 | bytes 4718592 | tf_op jit(solution)/shard_map/project/pallas_call | solution.py:225
  41.0 5.7 %collective-permute-done.1.refs_2_ = f32[1,1536]{1,0:T(1,128)S(1)} collective-permute-done((f32[1,1536]{1,0:T(1,128)S(1)}, f32[1,1536]{1,0:T(1,128)S(1)}, u32[]{:S(2)}, u32[]{:S(2)}) %collective-permute-start.1) | collective-permute-done | bytes 6176 | tf_op jit(solution)/shard_map/ppermute | solution.py:391
  46.7 0.5 collective-permute-start.2
  47.2 3.3 %attend.4 = (f32[256,576]{1,0:T(8,128)S(1)}, f32[2,1,576]{2,1,0:T(1,128)S(1)}, f32[2,1,576]{2,1,0:T(1,128)S(1)}) custom-call(bf16[192,1536]{1,0:T(8,128)(2,1)S(1)} %copy-done.2, bf16[104,512]{1,0:T(8,128)(2,1)S(1)} %get-tuple-element.20.refs_1_.refs_2_, bf16[104,512]{1,0:T(8,128)(2,1)S(1)} %get-tuple-element.20.refs_1_.refs_2_, ...), custom_call_target="tpu_custom_call" | custom-call | flops 792723456 | bytes 1376256 | tf_op jit(solution)/shard_map/attend/pallas_call | solution.py:186
  50.5 0.1 combine.3
  50.7 1.6 %collective-permute-start.23 = (bf16[96,1536]{1,0:T(8,128)(2,1)S(1)}, bf16[96,1536]{1,0:T(8,128)(2,1)S(1)}, u32[]{:S(2)}, u32[]{:S(2)}) collective-permute-start(bf16[96,1536]{1,0:T(8,128)(2,1)S(1)} %combine.3), channel_id=1, source_target_pairs={{0,2},{1,3},{2,0},{3,1},{4,6},{5,7},{6,4},{7,5},{8,10},{9,11},{10,... | collective-permute-start | bytes 884744 | tf_op jit(solution)/shard_map/ppermute | solution.py:391
  52.2 0.9 %attend.5.att_ref = bf16[96,1536]{1,0:T(8,128)(2,1)S(1)} custom-call(bf16[192,1536]{1,0:T(8,128)(2,1)S(1)} %copy-done.2, bf16[104,512]{1,0:T(8,128)(2,1)S(1)} %get-tuple-element.20.refs_1_.refs_2_, bf16[208,512]{1,0:T(8,128)(2,1)S(1)} %collective-permute-done.6.refs_2_, f32[256,576]{1,0:T(8,128)S(1)} %get-tuple-element.23.refs_3_, ...), custom_call_target="tpu_custom_call" | custom-call | flops 113246208 | bytes 196608 | tf_op jit(solution)/shard_map/attend/pallas_call | solution.py:186
  53.2 0.9 %project.10 = bf16[96,1536]{1,0:T(8,128)(2,1)S(1)} custom-call(bf16[96,1536]{1,0:T(8,128)(2,1)S(1)} %attend.5.att_ref, bf16[1536,6144]{1,0:T(8,128)(2,1)S(1)} %copy-done), custom_call_target="tpu_custom_call" | custom-call | flops 452984832 | bytes 4718592 | tf_op jit(solution)/shard_map/project/pallas_call | solution.py:225
  54.2 0.9 %project.9 = bf16[96,1536]{1,0:T(8,128)(2,1)S(1)} custom-call(bf16[96,1536]{1,0:T(8,128)(2,1)S(1)} %attend.5.att_ref, bf16[1536,6144]{1,0:T(8,128)(2,1)S(1)} %copy-done), custom_call_target="tpu_custom_call" | custom-call | flops 452984832 | bytes 4718592 | tf_op jit(solution)/shard_map/project/pallas_call | solution.py:225
  55.1 1.1 %project.8.own_ref = bf16[96,1536]{1,0:T(8,128)(2,1)S(1)} custom-call(bf16[96,1536]{1,0:T(8,128)(2,1)S(1)} %attend.5.att_ref, bf16[1536,6144]{1,0:T(8,128)(2,1)S(1)} %copy-done), custom_call_target="tpu_custom_call" | custom-call | flops 452984832 | bytes 4718592 | tf_op jit(solution)/shard_map/project/pallas_call | solution.py:225
  56.1 0.5 collective-permute-start.14
  56.8 0.1 collective-permute-start.27
  56.9 0.9 %project.11 = (bf16[48,1536]{1,0:T(8,128)(2,1)S(1)}, bf16[48,1536]{1,0:T(8,128)(2,1)S(1)}) custom-call(bf16[96,1536]{1,0:T(8,128)(2,1)S(1)} %attend.5.att_ref, bf16[1536,6144]{1,0:T(8,128)(2,1)S(1)} %copy-done, bf16[96,1536]{1,0:T(8,128)(2,1)S(1)} %collective-permute-done.17.rest_0_, bf16[192,1536]{1,0:T(8,128)(2,1)S(1)} %copy-done.1), custom_call_target="tpu_custom_call" | custom-call | flops 452984832 | bytes 4718592 | tf_op jit(solution)/shard_map/project/pallas_call | solution.py:225
  57.8 1.8 %collective-permute-done.23 = bf16[96,1536]{1,0:T(8,128)(2,1)S(1)} collective-permute-done((bf16[96,1536]{1,0:T(8,128)(2,1)S(1)}, bf16[96,1536]{1,0:T(8,128)(2,1)S(1)}, u32[]{:S(2)}, u32[]{:S(2)}) %collective-permute-start.23) | collective-permute-done | bytes 294944 | tf_op jit(solution)/shard_map/ppermute | solution.py:391
  59.7 1.5 %collective-permute-start.20 = (bf16[48,1536]{1,0:T(8,128)(2,1)S(1)}, bf16[48,1536]{1,0:T(8,128)(2,1)S(1)}, u32[]{:S(2)}, u32[]{:S(2)}) collective-permute-start(bf16[48,1536]{1,0:T(8,128)(2,1)S(1)} %get-tuple-element.27), channel_id=1, source_target_pairs={{0,2},{1,3},{2,0},{3,1},{4,6},{5,7},{6,4},{7,5},{8,10},{9,11},{10,... | collective-permute-start | bytes 442376 | tf_op jit(solution)/shard_map/ppermute | solution.py:391
  61.3 0.1 combine.2
  61.5 3.3 %collective-permute-done.20 = bf16[48,1536]{1,0:T(8,128)(2,1)S(1)} collective-permute-done((bf16[48,1536]{1,0:T(8,128)(2,1)S(1)}, bf16[48,1536]{1,0:T(8,128)(2,1)S(1)}, u32[]{:S(2)}, u32[]{:S(2)}) %collective-permute-start.20) | collective-permute-done | bytes 147488 | tf_op jit(solution)/shard_map/ppermute | solution.py:391
  64.8 1.5 %collective-permute-start.15 = (bf16[96,1536]{1,0:T(8,128)(2,1)S(1)}, bf16[96,1536]{1,0:T(8,128)(2,1)S(1)}, u32[]{:S(2)}, u32[]{:S(2)}) collective-permute-start(bf16[96,1536]{1,0:T(8,128)(2,1)S(1)} %combine.2), channel_id=1, source_target_pairs={{0,2},{1,3},{2,0},{3,1},{4,6},{5,7},{6,4},{7,5},{8,10},{9,11},{10,... | collective-permute-start | bytes 884744 | tf_op jit(solution)/shard_map/ppermute | solution.py:391
  66.3 5.6 %collective-permute-done.15 = bf16[96,1536]{1,0:T(8,128)(2,1)S(1)} collective-permute-done((bf16[96,1536]{1,0:T(8,128)(2,1)S(1)}, bf16[96,1536]{1,0:T(8,128)(2,1)S(1)}, u32[]{:S(2)}, u32[]{:S(2)}) %collective-permute-start.15) | collective-permute-done | bytes 294944 | tf_op jit(solution)/shard_map/ppermute | solution.py:391
  72.0 1.5 %collective-permute-start.18 = (bf16[48,1536]{1,0:T(8,128)(2,1)S(1)}, bf16[48,1536]{1,0:T(8,128)(2,1)S(1)}, u32[]{:S(2)}, u32[]{:S(2)}) collective-permute-start(bf16[48,1536]{1,0:T(8,128)(2,1)S(1)} %get-tuple-element.26), channel_id=1, source_target_pairs={{0,2},{1,3},{2,0},{3,1},{4,6},{5,7},{6,4},{7,5},{8,10},{9,11},{10,... | collective-permute-start | bytes 442376 | tf_op jit(solution)/shard_map/ppermute | solution.py:391
  73.6 3.6 %collective-permute-done.18 = bf16[48,1536]{1,0:T(8,128)(2,1)S(1)} collective-permute-done((bf16[48,1536]{1,0:T(8,128)(2,1)S(1)}, bf16[48,1536]{1,0:T(8,128)(2,1)S(1)}, u32[]{:S(2)}, u32[]{:S(2)}) %collective-permute-start.18) | collective-permute-done | bytes 147488 | tf_op jit(solution)/shard_map/ppermute | solution.py:391
  77.2 0.6 collective-permute-start.21
  77.9 2.0 %finish.3 = (bf16[192,6144]{1,0:T(8,128)(2,1)}, f32[1,192]{1,0:T(1,128)S(1)}, bf16[192,1536]{1,0:T(8,128)(2,1)}) custom-call(f32[1,1536]{1,0:T(1,128)S(1)} %copy-done.3, f32[1,1536]{1,0:T(1,128)S(1)} %collective-permute-done.refs_1_, f32[1,1536]{1,0:T(1,128)S(1)} %collective-permute-done.1.refs_2_, f32[1,1536]{1,0:T(1,128)S(1)} %collective-permute-done.2.refs_3_, ...), custom_call_target="tpu_custom_call" | custom-call | flops 2000000000 | bytes 2359296 | tf_op jit(solution)/shard_map/finish/pallas_call | solution.py:345
  79.9 1.3 %finish.4 = (bf16[192,6144]{1,0:T(8,128)(2,1)}, f32[1,192]{1,0:T(1,128)S(1)}, bf16[192,1536]{1,0:T(8,128)(2,1)}) custom-call(f32[1,1536]{1,0:T(1,128)S(1)} %copy-done.3, f32[1,1536]{1,0:T(1,128)S(1)} %collective-permute-done.refs_1_, f32[1,1536]{1,0:T(1,128)S(1)} %collective-permute-done.1.refs_2_, ...), custom_call_target="tpu_custom_call", output_to_operand_aliasing={{0}: (9, {}), {2}: (10, {})} | custom-call | flops 2000000000 | bytes 1179648 | tf_op jit(solution)/shard_map/finish/pallas_call | solution.py:345
  81.2 1.3 %finish.5 = (bf16[192,6144]{1,0:T(8,128)(2,1)}, f32[192]{0:T(256)}, bf16[192,1536]{1,0:T(8,128)(2,1)}) custom-call(f32[1,1536]{1,0:T(1,128)S(1)} %copy-done.3, f32[1,1536]{1,0:T(1,128)S(1)} %collective-permute-done.refs_1_, f32[1,1536]{1,0:T(1,128)S(1)} %collective-permute-done.1.refs_2_, ...), custom_call_target="tpu_custom_call", output_to_operand_aliasing={{0}: (9, {}), {2}: (10, {})} | custom-call | flops 2000000000 | bytes 1179648 | tf_op jit(solution)/shard_map/finish/pallas_call | solution.py:345
  (41 shorter events, 0.7 us)
Async XLA Ops:
  0.6 17.2 %copy-start.2 = (bf16[192,1536]{1,0:T(8,128)(2,1)S(1)}, bf16[192,1536]{1,0:T(8,128)(2,1)}, u32[]{:S(2)}) copy-start(bf16[192,1536]{1,0:T(8,128)(2,1)} %refs_0_.10) | copy-start | bytes 1769476
  0.6 22.1 %copy-start = (bf16[1536,6144]{1,0:T(8,128)(2,1)S(1)}, bf16[1536,6144]{1,0:T(8,128)(2,1)}, u32[]{:S(2)}) copy-start(bf16[1536,6144]{1,0:T(8,128)(2,1)} %weight_ref.15) | copy-start | bytes 56623108
  1.7 9.0 %collective-permute-start.3 = (bf16[104,512]{1,0:T(8,128)(2,1)S(1)}, bf16[104,512]{1,0:T(8,128)(2,1)S(1)}, u32[]{:S(2)}, u32[]{:S(2)}) collective-permute-start(bf16[104,512]{1,0:T(8,128)(2,1)S(1)} %get-tuple-element.20.refs_1_.refs_2_), channel_id=1, source_target_pairs={{0,24},{4,28},{8,16},{12,20},{16,8},{20,12},{24,0},{28,4},{1,25},{... | collective-permute-start | bytes 319496 | tf_op jit(solution)/shard_map/ppermute | solution.py:385
  6.9 6.3 %collective-permute-start.9 = (bf16[104,512]{1,0:T(8,128)(2,1)S(1)}, bf16[104,512]{1,0:T(8,128)(2,1)S(1)}, u32[]{:S(2)}, u32[]{:S(2)}) collective-permute-start(bf16[104,512]{1,0:T(8,128)(2,1)S(1)} %get-tuple-element.20.refs_1_.refs_2_), channel_id=1, source_target_pairs={{0,8},{4,12},{8,0},{12,4},{16,24},{20,28},{24,16},{28,20},{1,9},{5... | collective-permute-start | bytes 319496 | tf_op jit(solution)/shard_map/ppermute | solution.py:385
  6.9 9.0 %collective-permute-start.11 = (bf16[104,512]{1,0:T(8,128)(2,1)S(1)}, bf16[104,512]{1,0:T(8,128)(2,1)S(1)}, u32[]{:S(2)}, u32[]{:S(2)}) collective-permute-start(bf16[104,512]{1,0:T(8,128)(2,1)S(1)} %get-tuple-element.20.refs_1_.refs_2_), channel_id=1, source_target_pairs={{0,16},{4,20},{8,24},{12,28},{16,0},{20,4},{24,8},{28,12},{1,17},{... | collective-permute-start | bytes 319496 | tf_op jit(solution)/shard_map/ppermute | solution.py:385
  7.5 10.4 %collective-permute-start.7 = (bf16[104,512]{1,0:T(8,128)(2,1)S(1)}, bf16[104,512]{1,0:T(8,128)(2,1)S(1)}, u32[]{:S(2)}, u32[]{:S(2)}) collective-permute-start(bf16[104,512]{1,0:T(8,128)(2,1)S(1)} %get-tuple-element.20.refs_1_.refs_2_), channel_id=1, source_target_pairs={{0,4},{4,0},{8,12},{12,8},{16,20},{20,16},{24,28},{28,24},{1,5},{5... | collective-permute-start | bytes 319496 | tf_op jit(solution)/shard_map/ppermute | solution.py:388
  10.7 8.2 %collective-permute-start.8 = (bf16[104,512]{1,0:T(8,128)(2,1)S(1)}, bf16[104,512]{1,0:T(8,128)(2,1)S(1)}, u32[]{:S(2)}, u32[]{:S(2)}) collective-permute-start(bf16[104,512]{1,0:T(8,128)(2,1)S(1)} %collective-permute-done.3.refs_4_), channel_id=1, source_target_pairs={{0,4},{4,0},{8,12},{12,8},{16,20},{20,16},{24,28},{28,24},{1,5},{5... | collective-permute-start | bytes 319496 | tf_op jit(solution)/shard_map/ppermute | solution.py:388
  13.2 5.7 %collective-permute-start.10 = (bf16[104,512]{1,0:T(8,128)(2,1)S(1)}, bf16[104,512]{1,0:T(8,128)(2,1)S(1)}, u32[]{:S(2)}, u32[]{:S(2)}) collective-permute-start(bf16[104,512]{1,0:T(8,128)(2,1)S(1)} %collective-permute-done.9.refs_6_.refs_3_), channel_id=1, source_target_pairs={{0,4},{4,0},{8,12},{12,8},{16,20},{20,16},{24,28},{28,24},{1,5},{5... | collective-permute-start | bytes 319496 | tf_op jit(solution)/shard_map/ppermute | solution.py:388
  15.8 5.5 %collective-permute-start.12 = (bf16[104,512]{1,0:T(8,128)(2,1)S(1)}, bf16[104,512]{1,0:T(8,128)(2,1)S(1)}, u32[]{:S(2)}, u32[]{:S(2)}) collective-permute-start(bf16[104,512]{1,0:T(8,128)(2,1)S(1)} %collective-permute-done.11.refs_8_.refs_5_), channel_id=1, source_target_pairs={{0,4},{4,0},{8,12},{12,8},{16,20},{20,16},{24,28},{28,24},{1,5},{5... | collective-permute-start | bytes 319496 | tf_op jit(solution)/shard_map/ppermute | solution.py:388
  17.3 6.4 %collective-permute-start.4 = (bf16[104,512]{1,0:T(8,128)(2,1)S(1)}, bf16[104,512]{1,0:T(8,128)(2,1)S(1)}, u32[]{:S(2)}, u32[]{:S(2)}) collective-permute-start(bf16[104,512]{1,0:T(8,128)(2,1)S(1)} %get-tuple-element.22.refs_0_), channel_id=1, source_target_pairs={{0,4},{4,0},{8,12},{12,8},{16,20},{20,16},{24,28},{28,24},{1,5},{5... | collective-permute-start | bytes 319496 | tf_op jit(solution)/shard_map/ppermute | solution.py:388
  23.7 13.4 %collective-permute-start.25 = (bf16[96,1536]{1,0:T(8,128)(2,1)S(1)}, bf16[96,1536]{1,0:T(8,128)(2,1)S(1)}, u32[]{:S(2)}, u32[]{:S(2)}) collective-permute-start(bf16[96,1536]{1,0:T(8,128)(2,1)S(1)} %project.14), channel_id=1, source_target_pairs={{0,1},{1,0},{2,3},{3,2},{4,5},{5,4},{6,7},{7,6},{8,9},{9,8},{10,11... | collective-permute-start | bytes 884744 | tf_op jit(solution)/shard_map/ppermute | solution.py:394
  23.8 13.3 %copy-start.1 = (bf16[192,1536]{1,0:T(8,128)(2,1)S(1)}, bf16[192,1536]{1,0:T(8,128)(2,1)}, u32[]{:S(2)}) copy-start(bf16[192,1536]{1,0:T(8,128)(2,1)} %rest_1_.3) | copy-start | bytes 1769476
  23.8 13.3 %collective-permute-start.5 = (bf16[208,512]{1,0:T(8,128)(2,1)S(1)}, bf16[208,512]{1,0:T(8,128)(2,1)S(1)}, u32[]{:S(2)}, u32[]{:S(2)}) collective-permute-start(bf16[208,512]{1,0:T(8,128)(2,1)S(1)} %join.1.refs_10_), channel_id=1, source_target_pairs={{0,16},{4,20},{8,24},{12,28},{16,0},{20,4},{24,8},{28,12},{1,17},{... | collective-permute-start | bytes 638984 | tf_op jit(solution)/shard_map/ppermute | solution.py:385
  25.7 14.0 %copy-start.3 = (f32[1,1536]{1,0:T(1,128)S(1)}, f32[1,1536]{1,0:T(1,128)}, u32[]{:S(2)}) copy-start(f32[1,1536]{1,0:T(1,128)} %refs_0_.13) | copy-start | bytes 18436
  25.7 24.9 %collective-permute-start.22 = (bf16[96,1536]{1,0:T(8,128)(2,1)S(1)}, bf16[96,1536]{1,0:T(8,128)(2,1)S(1)}, u32[]{:S(2)}, u32[]{:S(2)}) collective-permute-start(bf16[96,1536]{1,0:T(8,128)(2,1)S(1)} %project.13), channel_id=1, source_target_pairs={{0,1},{1,0},{2,3},{3,2},{4,5},{5,4},{6,7},{7,6},{8,9},{9,8},{10,11... | collective-permute-start | bytes 884744 | tf_op jit(solution)/shard_map/ppermute | solution.py:394
  25.9 20.8 %collective-permute-start.13 = (bf16[208,512]{1,0:T(8,128)(2,1)S(1)}, bf16[208,512]{1,0:T(8,128)(2,1)S(1)}, u32[]{:S(2)}, u32[]{:S(2)}) collective-permute-start(bf16[208,512]{1,0:T(8,128)(2,1)S(1)} %join.1.refs_10_), channel_id=1, source_target_pairs={{0,8},{4,12},{8,0},{12,4},{16,24},{20,28},{24,16},{28,20},{1,9},{5... | collective-permute-start | bytes 638984 | tf_op jit(solution)/shard_map/ppermute | solution.py:385
  37.1 15.2 %collective-permute-start.6 = (bf16[208,512]{1,0:T(8,128)(2,1)S(1)}, bf16[208,512]{1,0:T(8,128)(2,1)S(1)}, u32[]{:S(2)}, u32[]{:S(2)}) collective-permute-start(bf16[208,512]{1,0:T(8,128)(2,1)S(1)} %collective-permute-done.5.refs_11_), channel_id=1, source_target_pairs={{0,8},{4,12},{8,0},{12,4},{16,24},{20,28},{24,16},{28,20},{1,9},{5... | collective-permute-start | bytes 638984 | tf_op jit(solution)/shard_map/ppermute | solution.py:385
  38.0 18.1 %collective-permute-start.26 = (bf16[96,1536]{1,0:T(8,128)(2,1)S(1)}, bf16[96,1536]{1,0:T(8,128)(2,1)S(1)}, u32[]{:S(2)}, u32[]{:S(2)}) collective-permute-start(bf16[96,1536]{1,0:T(8,128)(2,1)S(1)} %project.15), channel_id=1, source_target_pairs={{0,2},{1,3},{2,0},{3,1},{4,6},{5,7},{6,4},{7,5},{8,10},{9,11},{10,... | collective-permute-start | bytes 884744 | tf_op jit(solution)/shard_map/ppermute | solution.py:391
  39.6 7.1 %collective-permute-start.1 = (f32[1,1536]{1,0:T(1,128)S(1)}, f32[1,1536]{1,0:T(1,128)S(1)}, u32[]{:S(2)}, u32[]{:S(2)}) collective-permute-start(f32[1,1536]{1,0:T(1,128)S(1)} %copy-done.3), channel_id=1, source_target_pairs={{0,2},{1,3},{2,0},{3,1},{4,6},{5,7},{6,4},{7,5},{8,10},{9,11},{10,... | collective-permute-start | bytes 18440 | tf_op jit(solution)/shard_map/ppermute | solution.py:391
  46.7 30.4 %collective-permute-start = (f32[1,1536]{1,0:T(1,128)S(1)}, f32[1,1536]{1,0:T(1,128)S(1)}, u32[]{:S(2)}, u32[]{:S(2)}) collective-permute-start(f32[1,1536]{1,0:T(1,128)S(1)} %copy-done.3), channel_id=1, source_target_pairs={{0,1},{1,0},{2,3},{3,2},{4,5},{5,4},{6,7},{7,6},{8,9},{9,8},{10,11... | collective-permute-start | bytes 18440 | tf_op jit(solution)/shard_map/ppermute | solution.py:394
  46.7 31.0 %collective-permute-start.2 = (f32[1,1536]{1,0:T(1,128)S(1)}, f32[1,1536]{1,0:T(1,128)S(1)}, u32[]{:S(2)}, u32[]{:S(2)}) collective-permute-start(f32[1,1536]{1,0:T(1,128)S(1)} %collective-permute-done.1.refs_2_), channel_id=1, source_target_pairs={{0,1},{1,0},{2,3},{3,2},{4,5},{5,4},{6,7},{7,6},{8,9},{9,8},{10,11... | collective-permute-start | bytes 18440 | tf_op jit(solution)/shard_map/ppermute | solution.py:394
  50.7 9.0 %collective-permute-start.23 = (bf16[96,1536]{1,0:T(8,128)(2,1)S(1)}, bf16[96,1536]{1,0:T(8,128)(2,1)S(1)}, u32[]{:S(2)}, u32[]{:S(2)}) collective-permute-start(bf16[96,1536]{1,0:T(8,128)(2,1)S(1)} %combine.3), channel_id=1, source_target_pairs={{0,2},{1,3},{2,0},{3,1},{4,6},{5,7},{6,4},{7,5},{8,10},{9,11},{10,... | collective-permute-start | bytes 884744 | tf_op jit(solution)/shard_map/ppermute | solution.py:391
  54.1 2.7 %collective-permute-start.17 = (bf16[96,1536]{1,0:T(8,128)(2,1)S(1)}, bf16[96,1536]{1,0:T(8,128)(2,1)S(1)}, u32[]{:S(2)}, u32[]{:S(2)}) collective-permute-start(bf16[96,1536]{1,0:T(8,128)(2,1)S(1)} %project.10), channel_id=1, source_target_pairs={{0,1},{1,0},{2,3},{3,2},{4,5},{5,4},{6,7},{7,6},{8,9},{9,8},{10,11... | collective-permute-start | bytes 884744 | tf_op jit(solution)/shard_map/ppermute | solution.py:394
  56.1 5.1 %collective-permute-start.14 = (bf16[96,1536]{1,0:T(8,128)(2,1)S(1)}, bf16[96,1536]{1,0:T(8,128)(2,1)S(1)}, u32[]{:S(2)}, u32[]{:S(2)}) collective-permute-start(bf16[96,1536]{1,0:T(8,128)(2,1)S(1)} %project.9), channel_id=1, source_target_pairs={{0,1},{1,0},{2,3},{3,2},{4,5},{5,4},{6,7},{7,6},{8,9},{9,8},{10,11... | collective-permute-start | bytes 884744 | tf_op jit(solution)/shard_map/ppermute | solution.py:394
  56.8 21.1 %collective-permute-start.27 = (bf16[96,1536]{1,0:T(8,128)(2,1)S(1)}, bf16[96,1536]{1,0:T(8,128)(2,1)S(1)}, u32[]{:S(2)}, u32[]{:S(2)}) collective-permute-start(bf16[96,1536]{1,0:T(8,128)(2,1)S(1)} %add_convert_fusion.refs_6_), channel_id=1, source_target_pairs={{0,1},{1,0},{2,3},{3,2},{4,5},{5,4},{6,7},{7,6},{8,9},{9,8},{10,11... | collective-permute-start | bytes 884744 | tf_op jit(solution)/shard_map/ppermute | solution.py:394
  59.7 5.1 %collective-permute-start.20 = (bf16[48,1536]{1,0:T(8,128)(2,1)S(1)}, bf16[48,1536]{1,0:T(8,128)(2,1)S(1)}, u32[]{:S(2)}, u32[]{:S(2)}) collective-permute-start(bf16[48,1536]{1,0:T(8,128)(2,1)S(1)} %get-tuple-element.27), channel_id=1, source_target_pairs={{0,2},{1,3},{2,0},{3,1},{4,6},{5,7},{6,4},{7,5},{8,10},{9,11},{10,... | collective-permute-start | bytes 442376 | tf_op jit(solution)/shard_map/ppermute | solution.py:391
  61.2 16.6 %collective-permute-start.24 = (bf16[96,1536]{1,0:T(8,128)(2,1)S(1)}, bf16[96,1536]{1,0:T(8,128)(2,1)S(1)}, u32[]{:S(2)}, u32[]{:S(2)}) collective-permute-start(bf16[96,1536]{1,0:T(8,128)(2,1)S(1)} %add_convert_fusion.1.refs_4_), channel_id=1, source_target_pairs={{0,1},{1,0},{2,3},{3,2},{4,5},{5,4},{6,7},{7,6},{8,9},{9,8},{10,11... | collective-permute-start | bytes 884744 | tf_op jit(solution)/shard_map/ppermute | solution.py:394
  64.8 7.2 %collective-permute-start.15 = (bf16[96,1536]{1,0:T(8,128)(2,1)S(1)}, bf16[96,1536]{1,0:T(8,128)(2,1)S(1)}, u32[]{:S(2)}, u32[]{:S(2)}) collective-permute-start(bf16[96,1536]{1,0:T(8,128)(2,1)S(1)} %combine.2), channel_id=1, source_target_pairs={{0,2},{1,3},{2,0},{3,1},{4,6},{5,7},{6,4},{7,5},{8,10},{9,11},{10,... | collective-permute-start | bytes 884744 | tf_op jit(solution)/shard_map/ppermute | solution.py:391
  72.0 5.1 %collective-permute-start.18 = (bf16[48,1536]{1,0:T(8,128)(2,1)S(1)}, bf16[48,1536]{1,0:T(8,128)(2,1)S(1)}, u32[]{:S(2)}, u32[]{:S(2)}) collective-permute-start(bf16[48,1536]{1,0:T(8,128)(2,1)S(1)} %get-tuple-element.26), channel_id=1, source_target_pairs={{0,2},{1,3},{2,0},{3,1},{4,6},{5,7},{6,4},{7,5},{8,10},{9,11},{10,... | collective-permute-start | bytes 442376 | tf_op jit(solution)/shard_map/ppermute | solution.py:391
  77.1 2.8 %collective-permute-start.16 = (bf16[96,1536]{1,0:T(8,128)(2,1)S(1)}, bf16[96,1536]{1,0:T(8,128)(2,1)S(1)}, u32[]{:S(2)}, u32[]{:S(2)}) collective-permute-start(bf16[96,1536]{1,0:T(8,128)(2,1)S(1)} %add_convert_fusion.2.refs_4_), channel_id=1, source_target_pairs={{0,1},{1,0},{2,3},{3,2},{4,5},{5,4},{6,7},{7,6},{8,9},{9,8},{10,11... | collective-permute-start | bytes 884744 | tf_op jit(solution)/shard_map/ppermute | solution.py:394
  77.2 2.7 %collective-permute-start.21 = (bf16[48,1536]{1,0:T(8,128)(2,1)S(1)}, bf16[48,1536]{1,0:T(8,128)(2,1)S(1)}, u32[]{:S(2)}, u32[]{:S(2)}) collective-permute-start(bf16[48,1536]{1,0:T(8,128)(2,1)S(1)} %add_convert_fusion.3.refs_6_), channel_id=1, source_target_pairs={{0,1},{1,0},{2,3},{3,2},{4,5},{5,4},{6,7},{7,6},{8,9},{9,8},{10,11... | collective-permute-start | bytes 442376 | tf_op jit(solution)/shard_map/ppermute | solution.py:394
  77.8 3.5 %collective-permute-start.19 = (bf16[48,1536]{1,0:T(8,128)(2,1)S(1)}, bf16[48,1536]{1,0:T(8,128)(2,1)S(1)}, u32[]{:S(2)}, u32[]{:S(2)}) collective-permute-start(bf16[48,1536]{1,0:T(8,128)(2,1)S(1)} %add_convert_fusion.4.refs_6_), channel_id=1, source_target_pairs={{0,1},{1,0},{2,3},{3,2},{4,5},{5,4},{6,7},{7,6},{8,9},{9,8},{10,11... | collective-permute-start | bytes 442376 | tf_op jit(solution)/shard_map/ppermute | solution.py:394
